TPU v7x, 32 devices: a whole 2x2x4 slice. The times are simulated.
32 devices in a mesh: head: 2 (over core), seq: 8 (over z, y), mp: 2 (over x).
Axes of the slice: x: 2, y: 2, z: 4, core: 2. Of those that a mesh axis runs over, the one named last changes fastest.
Arguments:
- trunk: bfloat16 [128, 8192], P('seq', 'mp'), may hold values from -6 to 6
- branch: bfloat16 [2, 128, 8192], P('head', 'seq', 'mp'), may hold values from -6 to 6
- unembed: bfloat16 [18432, 8192], P('seq', 'mp'), may hold values from -0.09375 to 0.09375
- targets: int32 [2, 128], P('head'), may hold values from 0 to 18431
- loss_grad: float32 [2, 128], P('head'), may hold values from 0.25 to 4
Outputs:
- d_branch: bfloat16 [2, 128, 8192], P('head', 'seq', 'mp')
- d_trunk: bfloat16 [128, 8192], P('seq', 'mp')
- d_unembed: float32 [18432, 8192], P('seq', 'mp')
All inputs are finite; a program needn't handle non-finite values.
Results may differ from a plain program's by a relative error of at most 0.0051.
Values may be sent and summed in bfloat16 or wider, within the bound.
No kernel may reach another device: no remote copies, remote signals or barrier semaphores. Data moves between devices by JAX's collectives and lax.ppermute only.
A program may use at most 192 MiB of HBM per device.

v0:
```python
import jax
import jax.numpy as jnp
from jax import lax
from jax.sharding import PartitionSpec as P

soft_cap = 30.0


def shards(trunk, branch, unembed, targets, loss_grad):
    block_rows = unembed.shape[0]
    hidden = (trunk.astype(jnp.float32) + branch[0].astype(jnp.float32)).astype(jnp.bfloat16)
    gathered = lax.all_gather(hidden, "seq", axis=0, tiled=True)
    seq_index = lax.axis_index("seq")
    scores = lax.psum(
        lax.dot_general(
            unembed, gathered, (((1,), (1,)), ((), ())), preferred_element_type=jnp.float32
        ),
        "mp",
    )
    first_vocab = seq_index * block_rows
    squashed = jnp.tanh(scores / soft_cap)
    exponent = jnp.exp(soft_cap * squashed)
    totals = lax.psum(jnp.sum(exponent, axis=0), "seq")
    vocab_ids = first_vocab + lax.iota(jnp.int32, scores.shape[0])
    onehot = (vocab_ids[:, None] == targets[0][None, :]).astype(jnp.float32)
    slope = (
        loss_grad[0][None, :] * (exponent / totals[None, :] - onehot) * (1.0 - squashed * squashed)
    )
    grad_logits = slope.astype(jnp.bfloat16)
    weight_grad = jnp.dot(grad_logits, gathered, preferred_element_type=jnp.float32)
    row_grad = lax.psum_scatter(
        lax.dot_general(
            grad_logits, unembed, (((0,), (0,)), ((), ())), preferred_element_type=jnp.float32
        ),
        "seq",
        scatter_dimension=0,
        tiled=True,
    )
    trunk_sum, unembed_sum = lax.psum((row_grad, weight_grad), "head")
    return (row_grad.astype(jnp.bfloat16)[None], trunk_sum.astype(jnp.bfloat16), unembed_sum)


def solution(mesh):
    in_specs = (
        P("seq", "mp"),
        P("head", "seq", "mp"),
        P("seq", "mp"),
        P("head", None),
        P("head", None),
    )
    out_specs = (P("head", "seq", "mp"), P("seq", "mp"), P("seq", "mp"))
    return jax.shard_map(shards, mesh=mesh, in_specs=in_specs, out_specs=out_specs, check_vma=False)
```

profile of v0, /device:TPU:0, one launch (start us, length us, event | category | flops | bytes accessed | tf_op | source)
XLA Modules:
  0.0 359.2 jit_solution(3892800967753359351)
XLA Ops:
  7.2 0.0 all-gather.2.cloned.1.call-start
  7.2 1.7 fusion.1
  8.9 0.0 all-gather.2.cloned.1.call-update
  8.9 0.0 all-reduce.4.cloned.1.call-start
  8.9 44.8 %all-gather.2.cloned.1.call-done = bf16[128,4096]{1,0:T(8,128)(2,1)} async-done(((bf16[16,4096]{1,0:T(8,128)(2,1)}), bf16[128,4096]{1,0:T(8,128)(2,1)}) %all-gather.2.cloned.1.call-update) | async-done | bytes 1048592 | tf_op jit(solution)/shard_map/all_gather | solution.py:12
  53.7 14.0 %convolution_bitcast_fusion = f32[2304,128]{0,1:T(8,128)} fusion(bf16[128,4096]{1,0:T(8,128)(2,1)} %all-gather.2.cloned.1.call-done, bf16[2304,4096]{1,0:T(8,128)(2,1)} %param.7), kind=kOutput, calls=%fused_computation | convolution fusion | flops 2415919104 | bytes 21102592 | tf_op jit(solution)/shard_map/dot_general | solution.py:15
  67.8 0.0 all-reduce.4.cloned.1.call-update
  67.8 0.0 reduce-scatter.2.cloned.1.call-start
  67.9 41.8 %all-reduce.4.cloned.1.call-done = f32[2304,128]{0,1:T(8,128)} async-done(((f32[2304,128]{0,1:T(8,128)}), f32[2304,128]{0,1:T(8,128)}) %all-reduce.4.cloned.1.call-update) | async-done | bytes 1179664 | tf_op jit(solution)/shard_map/psum | solution.py:14
  109.6 1.8 fusion
  111.4 21.4 %psum.29 = f32[128]{0:T(128)S(1)} all-reduce(f32[128]{0:T(128)S(1)} %fusion), channel_id=1, replica_groups=mesh['head'=2,'seq'=8,'mp'=2] {'seq'}, use_global_device_ids=true, to_apply=%region_2.0 | all-reduce | flops 128 | bytes 1024 | tf_op jit(solution)/shard_map/psum | solution.py:23
  132.7 0.0 copy-done.2
  132.7 0.0 copy-done.3
  132.7 10.8 %fusion.3 = f32[128,4096]{1,0:T(8,128)} fusion(bf16[2304,4096]{1,0:T(8,128)(2,1)} %param.7, f32[2304,128]{0,1:T(8,128)S(1)} %copy-done, s32[2304]{0:T(1024)S(1)} %iota_add_fusion, f32[128]{0:T(128)S(1)} %psum.29, f32[128]{0:T(128)S(1)} %bitcast.13, s32[128]{0:T(128)S(1)} %bitcast.15), kind=kOutput, calls=%fused_computation.10 | convolution fusion | flops 2419163136 | bytes 22161920 | tf_op jit(solution)/shard_map/dot_general | solution.py:32
  143.5 0.0 reduce-scatter.2.cloned.1.call-update
  143.6 0.0 all-reduce.6.cloned.1.call-start
  143.6 1.1 copy-done.1
  144.8 15.9 %fusion.2 = f32[2304,4096]{1,0:T(8,128)} fusion(bf16[128,4096]{1,0:T(8,128)(2,1)S(1)} %copy-done.1, f32[2304,128]{0,1:T(8,128)S(1)} %copy-done, s32[2304]{0:T(1024)S(1)} %iota_add_fusion, f32[128]{0:T(128)S(1)} %psum.29, f32[128]{0:T(128)S(1)} %bitcast.14, s32[128]{0:T(128)S(1)} %bitcast.16), kind=kOutput, calls=%fused_computation.9 | convolution fusion | flops 2419163136 | bytes 39987712 | tf_op jit(solution)/shard_map/dot_general | solution.py:30
  160.6 0.0 all-reduce.6.cloned.1.call-update
  160.7 47.7 %reduce-scatter.2.cloned.1.call-done = f32[16,4096]{1,0:T(8,128)} async-done(((f32[128,4096]{1,0:T(8,128)}), f32[16,4096]{1,0:T(8,128)}) %reduce-scatter.2.cloned.1.call-update) | async-done | bytes 262160 | tf_op jit(solution)/shard_map/reduce_scatter | solution.py:31
  208.4 1.6 convert_bitcast_fusion
  210.0 5.4 %all-reduce.7 = bf16[16,4096]{1,0:T(8,128)(2,1)} all-reduce(f32[16,4096]{1,0:T(8,128)} %reduce-scatter.2.cloned.1.call-done), channel_id=1, replica_groups=mesh['head'=2,'seq'=8,'mp'=2] {'head'}, use_global_device_ids=true, to_apply=%region_4.0 | all-reduce | flops 65536 | bytes 393216 | tf_op jit(solution)/shard_map/psum | solution.py:39
  215.4 110.0 %all-reduce.6.cloned.1.call-done = f32[2304,4096]{1,0:T(8,128)} async-done(((f32[2304,4096]{1,0:T(8,128)}), f32[2304,4096]{1,0:T(8,128)}) %all-reduce.6.cloned.1.call-update) | async-done | bytes 37748752 | tf_op jit(solution)/shard_map/psum | solution.py:39
  325.4 27.3 %copy.12 = f32[2304,4096]{1,0:T(8,128)} copy(f32[2304,4096]{1,0:T(8,128)} %all-reduce.6.cloned.1.call-done) | data formatting | bytes 75497472
  (6 shorter events, 0.0 us)
Async XLA Ops:
  7.2 46.5 %all-gather.2.cloned.1.call-start = ((), (), s32[]{:S(2)}) async-start(), calls=%async_computation.1 | async-start | bytes 1179648 | tf_op jit(solution)/shard_map/all_gather | solution.py:12
  8.9 100.7 %all-reduce.4.cloned.1.call-start = ((), (), s32[]{:S(2)}) async-start(), calls=%async_computation.2 | async-start | bytes 2359296 | tf_op jit(solution)/shard_map/psum | solution.py:14
  67.8 65.0 %copy-start.2 = (f32[1,128]{1,0:T(1,128)S(1)}, f32[1,128]{1,0:T(1,128)}, u32[]{:S(2)}) copy-start(f32[1,128]{1,0:T(1,128)} %param.9) | copy-start | bytes 1540
  67.8 65.0 %copy-start.3 = (s32[1,128]{1,0:T(1,128)S(1)}, s32[1,128]{1,0:T(1,128)}, u32[]{:S(2)}) copy-start(s32[1,128]{1,0:T(1,128)} %param.8) | copy-start | bytes 1540
  67.8 140.6 %reduce-scatter.2.cloned.1.call-start = ((), (), s32[]{:S(2)}) async-start(), calls=%async_computation.3 | async-start | bytes 2359296 | tf_op jit(solution)/shard_map/reduce_scatter | solution.py:31
  109.6 23.1 %copy-start = (f32[2304,128]{0,1:T(8,128)S(1)}, f32[2304,128]{0,1:T(8,128)}, u32[]{:S(2)}) copy-start(f32[2304,128]{0,1:T(8,128)} %all-reduce.4.cloned.1.call-done) | copy-start | bytes 3538948
  143.5 1.2 copy-start.1
  143.6 181.8 %all-reduce.6.cloned.1.call-start = ((), (), s32[]{:S(2)}) async-start(), calls=%async_computation.4 | async-start | bytes 75497472 | tf_op jit(solution)/shard_map/psum | solution.py:39
Sparse Core Ops, SparseCore 0:
  10.7 42.9 all-gather.1
  67.9 41.6 all-reduce.3
  143.7 64.6 reduce-scatter.1
  211.3 114.0 all-reduce.5
where the time goes:
time: 360 us; the launch traced here: 359 us
  waiting for transfers between devices  244 us (68%)
  matrix products  40.7 us (11%)
  local copies, waits for them, and re-layouts  28.4 us (8%)
  blocking collectives  26.8 us (7%)
  between operations  13.8 us (4%)
  other arithmetic  5.04 us (1%)
    psum x1, waiting for transfers between devices, shards(): trunk_sum, unembed_sum = lax.psum((row_grad, weight_grad), 'head')  110 us
    reduce_scatter x1, waiting for transfers between devices, shards(): lax.psum_scatter(lax.dot_general(grad_logits, unembed, (((0,), (0,)), (()...  47.7 us
    all_gather x1, waiting for transfers between devices, shards(): gathered = lax.all_gather(hidden, 'seq', axis=0, tiled=True)  44.8 us
    psum x1, waiting for transfers between devices, shards(): lax.psum(lax.dot_general(unembed, gathered, (((1,), (1,)), ((), ())), pre...  41.8 us
    unnamed x9, local copies, waits for them, and re-layouts  28.4 us
    psum x1, blocking collectives, shards(): totals = lax.psum(jnp.sum(exponent, axis=0), 'seq')  21.4 us
    dot_general x1, matrix products, shards(): jnp.dot(grad_logits, gathered, preferred_element_type=jnp.float32)  15.9 us
    dot_general x1, matrix products, shards(): lax.dot_general(unembed, gathered, (((1,), (1,)), ((), ())), preferred_el...  14 us
  transfers between devices with their start and end apart: 4, of which 4 were waited for; matrix products, arithmetic and copies ran while one was open for 5% of the time, Pallas kernels for 0%

commit v1 on v0

v1 whole, which is shorter than its diff:
```python
import functools

import jax
import jax.numpy as jnp
from jax import lax
from jax.experimental import pallas as pl
from jax.experimental.pallas import tpu as pltpu
from jax.sharding import PartitionSpec as P

soft_cap = 30.0
bf16 = jnp.bfloat16
f32 = jnp.float32
f16 = jnp.float16
VMEM_LIMIT = 60 * 2**20
NX = 3


def params(n=1):
    return pltpu.CompilerParams(
        dimension_semantics=("arbitrary",) * n, vmem_limit_bytes=VMEM_LIMIT
    )


def cost(flops, nbytes):
    return pl.CostEstimate(flops=int(flops), bytes_accessed=int(nbytes), transcendentals=0)


def smem():
    return pl.BlockSpec(memory_space=pltpu.SMEM)


def whole(shape):
    return pl.BlockSpec(shape, lambda *_: (0,) * len(shape))


def scores_kernel(n, pieces, *refs):
    if pieces:
        seq_ref, refs = refs[0], refs[1:]
        parts, (u_ref, o_ref, h_ref, ht_ref) = refs[:n], refs[n:]
        rows = parts[0].shape[0]
    else:
        h_ref, u_ref, o_ref, ht_ref = refs

    @pl.when(pl.program_id(0) == 0)
    def _():
        if pieces:
            for k in range(n):
                at = pl.multiple_of((seq_ref[0] ^ k) * rows, rows)
                h_ref[pl.ds(at, rows), :] = parts[k][...]
        ht_ref[...] = h_ref[...].T

    s = jnp.dot(u_ref[...], ht_ref[...], preferred_element_type=f32)
    o_ref[...] = s.T


def scores_call(seq, hidden, unembed, chunk, block):
    pieces = isinstance(hidden, list)
    rows, width = unembed.shape
    tokens = sum(p.shape[0] for p in hidden) if pieces else hidden.shape[0]
    rows //= NX
    steps = rows // block
    u_spec = pl.BlockSpec((block, width), lambda i: (chunk * steps + i, 0))
    o_spec = pl.BlockSpec((tokens, block), lambda i: (0, i))
    o_shape = jax.ShapeDtypeStruct((tokens, rows), f32)
    est = cost(2 * tokens * rows * width, 2 * rows * width)
    scratch = [pltpu.VMEM((width, tokens), bf16)]
    if pieces:
        return pl.pallas_call(
            functools.partial(scores_kernel, len(hidden), True),
            grid=(steps,),
            in_specs=[smem()] + [whole(p.shape) for p in hidden] + [u_spec],
            out_specs=[o_spec, whole((tokens, width))],
            out_shape=[o_shape, jax.ShapeDtypeStruct((tokens, width), bf16)],
            scratch_shapes=scratch,
            compiler_params=params(),
            cost_estimate=est,
            name="scores_first",
        )(seq, *hidden, unembed)
    return pl.pallas_call(
        functools.partial(scores_kernel, 0, False),
        grid=(steps,),
        in_specs=[whole(hidden.shape), u_spec],
        out_specs=o_spec,
        out_shape=o_shape,
        scratch_shapes=scratch,
        compiler_params=params(),
        cost_estimate=est,
        name="scores_next",
    )(hidden, unembed)


def soften(s):
    squashed = jnp.tanh(s / soft_cap)
    return jnp.exp(soft_cap * squashed), 1.0 - squashed * squashed


def hits(first, targets, shape):
    ids = first + lax.broadcasted_iota(jnp.int32, shape, 1)
    return ids == targets


def numer_kernel(first_ref, s_ref, t_ref, q_ref, stat_ref):
    tokens, rows = s_ref.shape
    sum_e = sum_q = sum_d = 0.0
    step = 128
    for j in range(0, rows, step):
        e, d = soften(s_ref[:, j : j + step])
        hit = hits(first_ref[0] + j, t_ref[...], e.shape)
        q = e * d
        q_ref[:tokens, j : j + step] = jnp.where(hit, 0.0, q).astype(bf16)
        q_ref[tokens:, j : j + step] = jnp.where(hit, 1.0, 0.0).astype(bf16)
        sum_e = sum_e + e
        sum_q = sum_q + jnp.where(hit, q, 0.0)
        sum_d = sum_d + jnp.where(hit, d, 0.0)
    for k, a in enumerate((sum_e, sum_q, sum_d)):
        stat_ref[8 * k : 8 * k + 8, :] = jnp.broadcast_to(
            jnp.sum(a.T, axis=0, keepdims=True), (8, tokens)
        )


def numer_call(first, s, targets):
    tokens, rows = s.shape
    return pl.pallas_call(
        numer_kernel,
        in_specs=[smem(), pl.BlockSpec(memory_space=pltpu.VMEM), pl.BlockSpec(memory_space=pltpu.VMEM)],
        out_specs=[pl.BlockSpec(memory_space=pltpu.VMEM)] * 2,
        out_shape=[
            jax.ShapeDtypeStruct((2 * tokens, rows), bf16),
            jax.ShapeDtypeStruct((24, tokens), f32),
        ],
        compiler_params=pltpu.CompilerParams(vmem_limit_bytes=VMEM_LIMIT),
        cost_estimate=cost(40 * tokens * rows, 8 * tokens * rows),
        name="numer",
    )(first, s, targets)


def rows_kernel(q_ref, u_ref, o_ref):
    o_ref[...] = jnp.dot(q_ref[...], u_ref[...], preferred_element_type=f32)


def rows_call(q, unembed, part, parts, block):
    two, rows = q.shape
    width = unembed.shape[1] // parts
    steps = width // block
    return pl.pallas_call(
        rows_kernel,
        grid=(steps,),
        in_specs=[whole(q.shape), pl.BlockSpec((rows, block), lambda i: (0, part * steps + i))],
        out_specs=pl.BlockSpec((two, block), lambda i: (0, i)),
        out_shape=jax.ShapeDtypeStruct((two, width), f32),
        compiler_params=params(),
        cost_estimate=cost(2 * two * rows * width, 2 * rows * width),
        name="rows",
    )(q, unembed)


def column(row):
    return jnp.broadcast_to(row, (row.shape[1], row.shape[1])).T[:, :1]


def norm_kernel(n, parts, seq_ref, tot_ref, stat_ref, lg_ref, *refs):
    outs = refs[parts:]
    tokens = tot_ref.shape[1]
    rows = tokens // n
    total = tot_ref[...]
    lg = lg_ref[...]
    scale = lg / total
    weight = lg * (stat_ref[8:9, :] / total - stat_ref[16:17, :])
    scale_c, weight_c = column(scale), column(weight)
    sc = outs[-2]
    wc = outs[-1]
    sc[...] = jnp.broadcast_to(scale_c, sc.shape)
    wc[...] = jnp.broadcast_to(weight_c, wc.shape)
    for k in range(n):
        at = pl.multiple_of((seq_ref[0] ^ k) * rows, rows)
        a_s = sc[pl.ds(at, rows), :1]
        a_w = wc[pl.ds(at, rows), :1]
        for p in range(parts):
            width = refs[p].shape[1]
            a = refs[p][pl.ds(at, rows), :]
            u = refs[p][pl.ds(tokens + at, rows), :]
            outs[k][:, p * width : (p + 1) * width] = (a_s * a + a_w * u).astype(bf16)


def norm_call(n, seq, total, stats, loss_grad, sums):
    tokens = total.shape[1]
    width = sum(a.shape[1] for a in sums)
    vm = pl.BlockSpec(memory_space=pltpu.VMEM)
    return pl.pallas_call(
        functools.partial(norm_kernel, n, len(sums)),
        in_specs=[smem()] + [vm] * (3 + len(sums)),
        out_specs=[vm] * n,
        out_shape=[jax.ShapeDtypeStruct((tokens // n, width), bf16)] * n,
        scratch_shapes=[pltpu.VMEM((tokens, 128), f32)] * 2,
        compiler_params=pltpu.CompilerParams(vmem_limit_bytes=VMEM_LIMIT),
        cost_estimate=cost(4 * tokens * width, 10 * tokens * width),
        name="norm",
    )(seq, total, stats, loss_grad, *sums)


def grads_kernel(first_ref, s_ref, t_ref, tot_ref, lg_ref, g_ref):
    tokens, rows = s_ref.shape
    inv = column(1.0 / tot_ref[...])
    lg = column(lg_ref[...])
    step = 128
    for j in range(0, rows, step):
        e, d = soften(s_ref[:, j : j + step])
        hit = hits(first_ref[0] + j, t_ref[...], e.shape)
        g_ref[:, j : j + step] = (
            lg * (e * inv - jnp.where(hit, 1.0, 0.0)) * d
        ).astype(bf16)


def grads_call(first, s, targets, total, loss_grad):
    vm = pl.BlockSpec(memory_space=pltpu.VMEM)
    return pl.pallas_call(
        grads_kernel,
        in_specs=[smem()] + [vm] * 4,
        out_specs=vm,
        out_shape=jax.ShapeDtypeStruct(s.shape, bf16),
        compiler_params=pltpu.CompilerParams(vmem_limit_bytes=VMEM_LIMIT),
        cost_estimate=cost(40 * s.size, 6 * s.size),
        name="grads",
    )(first, s, targets, total, loss_grad)


def weight_kernel(head_ref, g0_ref, g1_ref, h0_ref, h1_ref, *refs):
    o_ref, g_ref, h_ref = refs[-3:]
    tokens = h0_ref.shape[0]
    mine = pl.multiple_of(head_ref[0] * tokens, tokens)
    other = pl.multiple_of((1 - head_ref[0]) * tokens, tokens)

    @pl.when(pl.program_id(0) == 0)
    def _():
        h_ref[pl.ds(mine, tokens), :] = h0_ref[...]
        h_ref[pl.ds(other, tokens), :] = h1_ref[...]

    g_ref[pl.ds(mine, tokens), :] = g0_ref[...]
    g_ref[pl.ds(other, tokens), :] = g1_ref[...]
    o_ref[...] = lax.dot_general(
        g_ref[...], h_ref[...], (((0,), (0,)), ((), ())), preferred_element_type=f32
    )


def weight_call(head, g0, g1, h0, h1, part, parts, block, into):
    tokens, rows = g0.shape
    width = h0.shape[1]
    steps = rows // parts // block
    g_spec = pl.BlockSpec((tokens, block), lambda i: (0, part * steps + i))
    operands = [head, g0, g1, h0, h1]
    specs = [smem(), g_spec, g_spec, whole(h0.shape), whole(h1.shape)]
    alias = {}
    if into is not None:
        operands.append(into)
        specs.append(pl.BlockSpec(memory_space=pl.ANY))
        alias = {5: 0}
    return pl.pallas_call(
        weight_kernel,
        grid=(steps,),
        in_specs=specs,
        out_specs=pl.BlockSpec((block, width), lambda i: (part * steps + i, 0)),
        out_shape=jax.ShapeDtypeStruct((rows, width), f32),
        scratch_shapes=[pltpu.VMEM((2 * tokens, block), bf16), pltpu.VMEM((2 * tokens, width), bf16)],
        input_output_aliases=alias,
        compiler_params=params(),
        cost_estimate=cost(4 * tokens * rows * width / parts, 4 * rows * width / parts),
        name="weight",
    )(*operands)


def swap(x, axis, mask, size):
    return lax.ppermute(x, axis, [(i, i ^ mask) for i in range(size)])


def fast(n, trunk, branch, unembed, targets, loss_grad):
    block_rows = unembed.shape[0]
    seq_index = lax.axis_index("seq")
    seq = seq_index.astype(jnp.int32)[None]
    head = lax.axis_index("head").astype(jnp.int32)[None]
    first = (seq_index * block_rows).astype(jnp.int32)[None]
    targets_c = jnp.broadcast_to(targets[0][:, None], (targets.shape[1], 128))
    hidden = (trunk.astype(f32) + branch[0].astype(f32)).astype(bf16)

    pieces = [None] * n
    pieces[0] = hidden
    for k in (k for k in (2, 6, 4) if k < n):
        pieces[k] = swap(hidden, "seq", k, n)
    for k in (k for k in (0, 2, 6, 4) if k < n):
        pieces[k + 1] = swap(pieces[k], "seq", 1, n)

    block = block_rows // 6
    mine, theirs = [], []
    whole_hidden = None
    for c in range(NX):
        if c == 0:
            s, whole_hidden = scores_call(seq, pieces, unembed, c, block)
        else:
            s = scores_call(seq, whole_hidden, unembed, c, block)
        s = s.astype(f16)
        mine.append(s)
        theirs.append(swap(s, "mp", 1, 2))
    other_hidden = swap(whole_hidden, "head", 1, 2)
    scores = jnp.concatenate([a.astype(f32) + b.astype(f32) for a, b in zip(mine, theirs)], axis=1)

    q, stats = numer_call(first, scores, targets_c)
    total = stats[:1]
    sums = []
    parts = 2
    masks = [1 << i for i in range(n.bit_length() - 1)]
    for mask in masks:
        total = total + swap(total, "seq", mask, n)
    for p in range(parts):
        sums.append(rows_call(q, unembed, p, parts, 512))
    blocks = norm_call(n, seq, total, stats, loss_grad, sums)

    got = []
    for k in (k for k in (2, 6, 4, 0) if k < n):
        theirs = swap(blocks[k + 1], "seq", 1, n)
        both = blocks[k].astype(f32) + theirs.astype(f32)
        if k:
            both = swap(both.astype(bf16), "seq", k, n).astype(f32)
        got.append(both)
    row_grad = functools.reduce(lambda a, b: a + b, got)

    g = grads_call(first, scores, targets_c, total, loss_grad)
    g_other = swap(g, "head", 1, 2)
    d_unembed = None
    for p in range(3):
        d_unembed = weight_call(head, g, g_other, whole_hidden, other_hidden, p, 3, 256, d_unembed)

    d_trunk = row_grad + swap(row_grad, "head", 1, 2)
    return (row_grad.astype(bf16)[None], d_trunk.astype(bf16), d_unembed)


def general(trunk, branch, unembed, targets, loss_grad):
    block_rows = unembed.shape[0]
    hidden = (trunk.astype(f32) + branch[0].astype(f32)).astype(bf16)
    gathered = lax.all_gather(hidden, "seq", axis=0, tiled=True)
    seq_index = lax.axis_index("seq")
    scores = lax.psum(
        lax.dot_general(unembed, gathered, (((1,), (1,)), ((), ())), preferred_element_type=f32),
        "mp",
    )
    exponent, slope = soften(scores)
    totals = lax.psum(jnp.sum(exponent, axis=0), "seq")
    vocab_ids = seq_index * block_rows + lax.iota(jnp.int32, block_rows)
    onehot = (vocab_ids[:, None] == targets[0][None, :]).astype(f32)
    grad_logits = (
        loss_grad[0][None, :] * (exponent / totals[None, :] - onehot) * slope
    ).astype(bf16)
    row_grad = lax.psum_scatter(
        lax.dot_general(grad_logits, unembed, (((0,), (0,)), ((), ())), preferred_element_type=f32),
        "seq",
        scatter_dimension=0,
        tiled=True,
    )
    weight_grad = jnp.dot(grad_logits, gathered, preferred_element_type=f32)
    trunk_sum, unembed_sum = lax.psum((row_grad, weight_grad), "head")
    return (row_grad.astype(bf16)[None], trunk_sum.astype(bf16), unembed_sum)


def solution(mesh):
    in_specs = (
        P("seq", "mp"),
        P("head", "seq", "mp"),
        P("seq", "mp"),
        P("head", None),
        P("head", None),
    )
    out_specs = (P("head", "seq", "mp"), P("seq", "mp"), P("seq", "mp"))
    n = mesh.shape["seq"]
    pairs = mesh.shape["head"] == 2 and mesh.shape["mp"] == 2
    body = functools.partial(fast, n) if pairs and n in (2, 4, 8) else general
    return jax.shard_map(body, mesh=mesh, in_specs=in_specs, out_specs=out_specs, check_vma=False)
```

time: 360 us -> 132 us (0.37)
  waiting for transfers between devices: 244 us -> 27.7 us
  Pallas kernels: 0 us -> 61.9 us
  matrix products: 40.7 us -> 0 us
  starting transfers between devices: 0.16 us -> 27.2 us
  blocking collectives: 26.8 us -> 0 us
  local copies, waits for them, and re-layouts: 28.4 us -> 3.23 us
  between operations: 13.8 us -> 0.79 us
  other arithmetic: 5.04 us -> 10.8 us
    psum x2 -> x0, waiting for transfers between devices: 152 us -> none  [the longest x1 110 us: shards(): trunk_sum, unembed_sum = lax.psum((row_grad, weight_grad), 'head')]
    pallas_call x0 -> x11, Pallas kernels: none -> 61.9 us  [the longest x3 21.9 us: weight_call(): pl.pallas_call(weight_kernel, grid=(steps,), in_specs=specs, out_specs=pl...]
    reduce_scatter x1 -> x0, waiting for transfers between devices: 47.7 us -> none  [shards(): lax.psum_scatter(lax.dot_general(grad_logits, unembed, (((0,), (0,)), (()...]
    all_gather x1 -> x0, waiting for transfers between devices: 44.8 us -> none  [shards(): gathered = lax.all_gather(hidden, 'seq', axis=0, tiled=True)]
    dot_general x3 -> x0, matrix products: 40.7 us -> none  [the longest x1 15.9 us: shards(): jnp.dot(grad_logits, gathered, preferred_element_type=jnp.float32)]
    ppermute x0 -> x23, waiting for transfers between devices: none -> 27.7 us  [swap(): return lax.ppermute(x, axis, [(i, i ^ mask) for i in range(size)])]
    ppermute x0 -> x23, starting transfers between devices: none -> 27.2 us  [swap(): return lax.ppermute(x, axis, [(i, i ^ mask) for i in range(size)])]
    psum x2 -> x0, blocking collectives: 26.8 us -> none  [the longest x1 21.4 us: shards(): totals = lax.psum(jnp.sum(exponent, axis=0), 'seq')]
  transfers between devices with their start and end apart: 4 -> 23, of which waited for: 4 -> 11; matrix products, arithmetic and copies ran while one was open for 5% -> 4% of each run, Pallas kernels for 0% -> 21%
where the time goes in v1:
time: 132 us
  Pallas kernels  61.9 us (47%)
  waiting for transfers between devices  27.7 us (21%)
  starting transfers between devices  27.2 us (21%)
  other arithmetic  10.8 us (8%)
  local copies, waits for them, and re-layouts  3.23 us (2%)
    ppermute x23, waiting for transfers between devices, swap(): return lax.ppermute(x, axis, [(i, i ^ mask) for i in range(size)])  27.7 us
    ppermute x23, starting transfers between devices, swap(): return lax.ppermute(x, axis, [(i, i ^ mask) for i in range(size)])  27.2 us
    pallas_call x3, Pallas kernels, weight_call(): pl.pallas_call(weight_kernel, grid=(steps,), in_specs=specs, out_specs=pl...  21.9 us
    pallas_call x2, Pallas kernels, rows_call(): pl.pallas_call(rows_kernel, grid=(steps,), in_specs=[whole(q.shape), pl.B...  14.5 us
    pallas_call x2, Pallas kernels, scores_call(): pl.pallas_call(functools.partial(scores_kernel, 0, False), grid=(steps,),...  10.6 us
    pallas_call x1, Pallas kernels, scores_call(): pl.pallas_call(functools.partial(scores_kernel, len(hidden), True), grid=...  5.43 us
    pallas_call x1, Pallas kernels, norm_call(): pl.pallas_call(functools.partial(norm_kernel, n, len(sums)), in_specs=[sm...  3.63 us
    pallas_call x1, Pallas kernels, numer_call(): pl.pallas_call(numer_kernel, in_specs=[smem(), pl.BlockSpec(memory_space=...  3.15 us
  transfers between devices with their start and end apart: 23, of which 11 were waited for; matrix products, arithmetic and copies ran while one was open for 4% of the time, Pallas kernels for 21%

profile of v1, /device:TPU:0, one launch (start us, length us, event | category | flops | bytes accessed | tf_op | source)
XLA Modules:
  0.0 131.7 jit_solution(9455547405694861320)
XLA Ops:
  1.6 5.1 %collective-permute-start.5 = (bf16[16,4096]{1,0:T(8,128)(2,1)S(1)}, bf16[16,4096]{1,0:T(8,128)(2,1)S(1)}, u32[]{:S(2)}, u32[]{:S(2)}) collective-permute-start(bf16[16,4096]{1,0:T(8,128)(2,1)S(1)} %fusion.refs_1_), channel_id=1, source_target_pairs={{0,12},{2,14},{4,8},{6,10},{8,4},{10,6},{12,0},{14,2},{1,13},{3,15... | collective-permute-start | bytes 393224 | tf_op jit(solution)/shard_map/ppermute | solution.py:272
  7.4 1.7 %collective-permute-start = (bf16[16,4096]{1,0:T(8,128)(2,1)S(1)}, bf16[16,4096]{1,0:T(8,128)(2,1)S(1)}, u32[]{:S(2)}, u32[]{:S(2)}) collective-permute-start(bf16[16,4096]{1,0:T(8,128)(2,1)S(1)} %fusion.refs_1_), channel_id=1, source_target_pairs={{0,2},{2,0},{4,6},{6,4},{8,10},{10,8},{12,14},{14,12},{1,3},{3,1},... | collective-permute-start | bytes 393224 | tf_op jit(solution)/shard_map/ppermute | solution.py:272
  9.1 2.1 %collective-permute-done.5.refs_7_ = bf16[16,4096]{1,0:T(8,128)(2,1)S(1)} collective-permute-done((bf16[16,4096]{1,0:T(8,128)(2,1)S(1)}, bf16[16,4096]{1,0:T(8,128)(2,1)S(1)}, u32[]{:S(2)}, u32[]{:S(2)}) %collective-permute-start.5) | collective-permute-done | bytes 131104 | tf_op jit(solution)/shard_map/ppermute | solution.py:272
  11.2 1.7 %collective-permute-start.6 = (bf16[16,4096]{1,0:T(8,128)(2,1)S(1)}, bf16[16,4096]{1,0:T(8,128)(2,1)S(1)}, u32[]{:S(2)}, u32[]{:S(2)}) collective-permute-start(bf16[16,4096]{1,0:T(8,128)(2,1)S(1)} %collective-permute-done.5.refs_7_), channel_id=1, source_target_pairs={{0,2},{2,0},{4,6},{6,4},{8,10},{10,8},{12,14},{14,12},{1,3},{3,1},... | collective-permute-start | bytes 393224 | tf_op jit(solution)/shard_map/ppermute | solution.py:272
  12.9 4.9 %collective-permute-done.3.refs_5_ = bf16[16,4096]{1,0:T(8,128)(2,1)S(1)} collective-permute-done((bf16[16,4096]{1,0:T(8,128)(2,1)S(1)}, bf16[16,4096]{1,0:T(8,128)(2,1)S(1)}, u32[]{:S(2)}, u32[]{:S(2)}) %collective-permute-start.3) | collective-permute-done | bytes 131104 | tf_op jit(solution)/shard_map/ppermute | solution.py:272
  19.9 3.9 %collective-permute-done.4.refs_6_ = bf16[16,4096]{1,0:T(8,128)(2,1)S(1)} collective-permute-done((bf16[16,4096]{1,0:T(8,128)(2,1)S(1)}, bf16[16,4096]{1,0:T(8,128)(2,1)S(1)}, u32[]{:S(2)}, u32[]{:S(2)}) %collective-permute-start.4) | collective-permute-done | bytes 131104 | tf_op jit(solution)/shard_map/ppermute | solution.py:272
  25.9 5.4 %scores_first.1 = (f32[128,768]{1,0:T(8,128)}, bf16[128,4096]{1,0:T(8,128)(2,1)}) custom-call(s32[1]{0:T(128)} %bitcast.refs_0_.seq_ref, bf16[16,4096]{1,0:T(8,128)(2,1)} %copy-done.6, bf16[16,4096]{1,0:T(8,128)(2,1)} %copy-done.10, bf16[16,4096]{1,0:T(8,128)(2,1)} %copy-done.9, bf16[16,4096]{1,0:T(8,128)(2,1)} %copy-done.13, bf16[16,4096]{1,0:T(8,128)(2,1)} %copy-done.8, ...), custom_call_target="tpu_custom_call" | custom-call | flops 805306368 | bytes 6291456 | tf_op jit(solution)/shard_map/scores_first/pallas_call | solution.py:68
  33.9 5.3 %scores_next.3 = f32[128,768]{1,0:T(8,128)} custom-call(bf16[128,4096]{1,0:T(8,128)(2,1)} %get-tuple-element.16.refs_0_.h0_ref, bf16[2304,4096]{1,0:T(8,128)(2,1)} %u_ref.3), custom_call_target="tpu_custom_call" | custom-call | flops 805306368 | bytes 6291456 | tf_op jit(solution)/shard_map/scores_next/pallas_call | solution.py:79
  40.9 5.3 %scores_next.2 = f32[128,768]{1,0:T(8,128)} custom-call(bf16[128,4096]{1,0:T(8,128)(2,1)} %get-tuple-element.16.refs_0_.h0_ref, bf16[2304,4096]{1,0:T(8,128)(2,1)} %u_ref.3), custom_call_target="tpu_custom_call" | custom-call | flops 805306368 | bytes 6291456 | tf_op jit(solution)/shard_map/scores_next/pallas_call | solution.py:79
  48.9 4.0 %collective-permute-done.8 = f16[128,768]{1,0:T(8,128)(2,1)S(1)} collective-permute-done((f16[128,768]{1,0:T(8,128)(2,1)S(1)}, f16[128,768]{1,0:T(8,128)(2,1)S(1)}, u32[]{:S(2)}, u32[]{:S(2)}) %collective-permute-start.8) | collective-permute-done | bytes 196640 | tf_op jit(solution)/shard_map/ppermute | solution.py:272
  54.9 3.1 %numer.1 = (bf16[256,2304]{1,0:T(8,128)(2,1)}, f32[24,128]{1,0:T(8,128)}) custom-call(s32[1]{0:T(128)} %bitcast.1.first_ref, f32[128,2304]{1,0:T(8,128)} %pad_maximum_fusion.s_ref, s32[128,128]{1,0:T(8,128)} %broadcast_in_dim.22.t_ref), custom_call_target="tpu_custom_call" | custom-call | flops 11796480 | bytes 2359296 | tf_op jit(solution)/shard_map/numer/pallas_call | solution.py:123
  60.2 2.0 %collective-permute-done.10 = f32[1,128]{1,0:T(1,128)S(1)} collective-permute-done((f32[1,128]{1,0:T(1,128)S(1)}, f32[1,128]{1,0:T(1,128)S(1)}, u32[]{:S(2)}, u32[]{:S(2)}) %collective-permute-start.10) | collective-permute-done | bytes 544 | tf_op jit(solution)/shard_map/ppermute | solution.py:272
  63.8 7.3 %rows.3.refs_1_ = f32[256,2048]{1,0:T(8,128)} custom-call(bf16[256,2304]{1,0:T(8,128)(2,1)} %get-tuple-element.18.q_ref, bf16[2304,4096]{1,0:T(8,128)(2,1)} %u_ref.3), custom_call_target="tpu_custom_call" | custom-call | flops 2415919104 | bytes 9437184 | tf_op jit(solution)/shard_map/rows/pallas_call | solution.py:145
  71.1 2.0 %collective-permute-start.12 = (f32[1,128]{1,0:T(1,128)S(1)}, f32[1,128]{1,0:T(1,128)S(1)}, u32[]{:S(2)}, u32[]{:S(2)}) collective-permute-start(f32[1,128]{1,0:T(1,128)S(1)} %add.50), channel_id=1, source_target_pairs={{0,8},{2,10},{4,12},{6,14},{8,0},{10,2},{12,4},{14,6},{1,9},{3,11}... | collective-permute-start | bytes 1544 | tf_op jit(solution)/shard_map/ppermute | solution.py:272
  73.1 7.2 %rows.2.refs_0_ = f32[256,2048]{1,0:T(8,128)} custom-call(bf16[256,2304]{1,0:T(8,128)(2,1)} %get-tuple-element.18.q_ref, bf16[2304,4096]{1,0:T(8,128)(2,1)} %u_ref.3), custom_call_target="tpu_custom_call" | custom-call | flops 2415919104 | bytes 9437184 | tf_op jit(solution)/shard_map/rows/pallas_call | solution.py:145
  80.9 3.6 %norm.1 = (bf16[16,4096]{1,0:T(8,128)(2,1)}, bf16[16,4096]{1,0:T(8,128)(2,1)}, bf16[16,4096]{1,0:T(8,128)(2,1)}, bf16[16,4096]{1,0:T(8,128)(2,1)}, bf16[16,4096]...) custom-call(s32[1]{0:T(128)} %bitcast.refs_0_.seq_ref, ...), custom_call_target="tpu_custom_call" | custom-call | flops 2097152 | bytes 5242880 | tf_op jit(solution)/shard_map/norm/pallas_call | solution.py:189
  84.5 1.6 %collective-permute-start.13 = (bf16[16,4096]{1,0:T(8,128)(2,1)}, bf16[16,4096]{1,0:T(8,128)(2,1)S(1)}, u32[]{:S(2)}, u32[]{:S(2)}) collective-permute-start(bf16[16,4096]{1,0:T(8,128)(2,1)} %get-tuple-element.20), channel_id=1, source_target_pairs={{0,2},{2,0},{4,6},{6,4},{8,10},{10,8},{12,14},{14,12},{1,3},{3,1},... | collective-permute-start | bytes 393224 | tf_op jit(solution)/shard_map/ppermute | solution.py:272
  92.2 2.0 %collective-permute-start.16 = (bf16[16,4096]{1,0:T(8,128)(2,1)S(1)}, bf16[16,4096]{1,0:T(8,128)(2,1)S(1)}, u32[]{:S(2)}, u32[]{:S(2)}) collective-permute-start(bf16[16,4096]{1,0:T(8,128)(2,1)S(1)} %add_convert_fusion.2), channel_id=1, source_target_pairs={{0,12},{2,14},{4,8},{6,10},{8,4},{10,6},{12,0},{14,2},{1,13},{3,15... | collective-permute-start | bytes 393224 | tf_op jit(solution)/shard_map/ppermute | solution.py:272
  96.3 2.9 %collective-permute-done.16 = bf16[16,4096]{1,0:T(8,128)(2,1)S(1)} collective-permute-done((bf16[16,4096]{1,0:T(8,128)(2,1)S(1)}, bf16[16,4096]{1,0:T(8,128)(2,1)S(1)}, u32[]{:S(2)}, u32[]{:S(2)}) %collective-permute-start.16) | collective-permute-done | bytes 131104 | tf_op jit(solution)/shard_map/ppermute | solution.py:272
  99.1 3.3 %collective-permute-done.18 = bf16[16,4096]{1,0:T(8,128)(2,1)S(1)} collective-permute-done((bf16[16,4096]{1,0:T(8,128)(2,1)S(1)}, bf16[16,4096]{1,0:T(8,128)(2,1)S(1)}, u32[]{:S(2)}, u32[]{:S(2)}) %collective-permute-start.18) | collective-permute-done | bytes 131104 | tf_op jit(solution)/shard_map/ppermute | solution.py:272
  103.7 2.8 %grads.1.g0_ref = bf16[128,2304]{1,0:T(8,128)(2,1)} custom-call(s32[1]{0:T(128)} %bitcast.1.first_ref, f32[128,2304]{1,0:T(8,128)} %pad_maximum_fusion.s_ref, s32[128,128]{1,0:T(8,128)} %broadcast_in_dim.22.t_ref, f32[1,128]{1,0:T(1,128)} %add.51.tot_ref, f32[1,128]{1,0:T(1,128)} %lg_ref.3), custom_call_target="tpu_custom_call" | custom-call | flops 11796480 | bytes 1769472 | tf_op jit(solution)/shard_map/grads/pallas_call | solution.py:216
  109.8 7.3 %weight.3.refs_0_ = f32[2304,4096]{1,0:T(8,128)} custom-call(s32[1]{0:T(128)} %bitcast.5.head_ref, bf16[128,2304]{1,0:T(8,128)(2,1)} %grads.1.g0_ref, bf16[128,2304]{1,0:T(8,128)(2,1)} %copy-done.2, bf16[128,4096]{1,0:T(8,128)(2,1)} %get-tuple-element.16.refs_0_.h0_ref, bf16[128,4096]{1,0:T(8,128)(2,1)} %copy-done.1), custom_call_target="tpu_custom_call" | custom-call | flops 1610612736 | bytes 12582912 | tf_op jit(solution)/shard_map/weight/pallas_call | solution.py:257
  117.1 7.3 %weight.4.refs_0_ = f32[2304,4096]{1,0:T(8,128)} custom-call(s32[1]{0:T(128)} %bitcast.5.head_ref, bf16[128,2304]{1,0:T(8,128)(2,1)} %grads.1.g0_ref, bf16[128,2304]{1,0:T(8,128)(2,1)} %copy-done.2, bf16[128,4096]{1,0:T(8,128)(2,1)} %get-tuple-element.16.refs_0_.h0_ref, bf16[128,4096]{1,0:T(8,128)(2,1)} %copy-done.1, ...), custom_call_target="tpu_custom_call", output_to_operand_aliasing={{}: (5, {})} | custom-call | flops 1610612736 | bytes 12582912 | tf_op jit(solution)/shard_map/weight/pallas_call | solution.py:257
  124.4 7.3 %weight.5 = f32[2304,4096]{1,0:T(8,128)} custom-call(s32[1]{0:T(128)} %bitcast.5.head_ref, bf16[128,2304]{1,0:T(8,128)(2,1)} %grads.1.g0_ref, bf16[128,2304]{1,0:T(8,128)(2,1)} %copy-done.2, bf16[128,4096]{1,0:T(8,128)(2,1)} %get-tuple-element.16.refs_0_.h0_ref, bf16[128,4096]{1,0:T(8,128)(2,1)} %copy-done.1, ...), custom_call_target="tpu_custom_call", output_to_operand_aliasing={{}: (5, {})} | custom-call | flops 1610612736 | bytes 12582912 | tf_op jit(solution)/shard_map/weight/pallas_call | solution.py:257
  (83 shorter events, 31.7 us)
Async XLA Ops:
  1.6 23.6 %copy-start.6 = (bf16[16,4096]{1,0:T(8,128)(2,1)}, bf16[16,4096]{1,0:T(8,128)(2,1)S(1)}, u32[]{:S(2)}) copy-start(bf16[16,4096]{1,0:T(8,128)(2,1)S(1)} %fusion.refs_1_) | copy-start | bytes 393220
  1.6 9.6 %collective-permute-start.5 = (bf16[16,4096]{1,0:T(8,128)(2,1)S(1)}, bf16[16,4096]{1,0:T(8,128)(2,1)S(1)}, u32[]{:S(2)}, u32[]{:S(2)}) collective-permute-start(bf16[16,4096]{1,0:T(8,128)(2,1)S(1)} %fusion.refs_1_), channel_id=1, source_target_pairs={{0,12},{2,14},{4,8},{6,10},{8,4},{10,6},{12,0},{14,2},{1,13},{3,15... | collective-permute-start | bytes 393224 | tf_op jit(solution)/shard_map/ppermute | solution.py:272
  6.8 11.1 %collective-permute-start.3 = (bf16[16,4096]{1,0:T(8,128)(2,1)S(1)}, bf16[16,4096]{1,0:T(8,128)(2,1)S(1)}, u32[]{:S(2)}, u32[]{:S(2)}) collective-permute-start(bf16[16,4096]{1,0:T(8,128)(2,1)S(1)} %fusion.refs_1_), channel_id=1, source_target_pairs={{0,8},{2,10},{4,12},{6,14},{8,0},{10,2},{12,4},{14,6},{1,9},{3,11}... | collective-permute-start | bytes 393224 | tf_op jit(solution)/shard_map/ppermute | solution.py:272
  6.8 12.6 %collective-permute-start.1 = (bf16[16,4096]{1,0:T(8,128)(2,1)S(1)}, bf16[16,4096]{1,0:T(8,128)(2,1)S(1)}, u32[]{:S(2)}, u32[]{:S(2)}) collective-permute-start(bf16[16,4096]{1,0:T(8,128)(2,1)S(1)} %fusion.refs_1_), channel_id=1, source_target_pairs={{0,4},{2,6},{4,0},{6,2},{8,12},{10,14},{12,8},{14,10},{1,5},{3,7},... | collective-permute-start | bytes 393224 | tf_op jit(solution)/shard_map/ppermute | solution.py:272
  7.4 12.5 %collective-permute-start = (bf16[16,4096]{1,0:T(8,128)(2,1)S(1)}, bf16[16,4096]{1,0:T(8,128)(2,1)S(1)}, u32[]{:S(2)}, u32[]{:S(2)}) collective-permute-start(bf16[16,4096]{1,0:T(8,128)(2,1)S(1)} %fusion.refs_1_), channel_id=1, source_target_pairs={{0,2},{2,0},{4,6},{6,4},{8,10},{10,8},{12,14},{14,12},{1,3},{3,1},... | collective-permute-start | bytes 393224 | tf_op jit(solution)/shard_map/ppermute | solution.py:272
  11.2 8.7 %collective-permute-start.6 = (bf16[16,4096]{1,0:T(8,128)(2,1)S(1)}, bf16[16,4096]{1,0:T(8,128)(2,1)S(1)}, u32[]{:S(2)}, u32[]{:S(2)}) collective-permute-start(bf16[16,4096]{1,0:T(8,128)(2,1)S(1)} %collective-permute-done.5.refs_7_), channel_id=1, source_target_pairs={{0,2},{2,0},{4,6},{6,4},{8,10},{10,8},{12,14},{14,12},{1,3},{3,1},... | collective-permute-start | bytes 393224 | tf_op jit(solution)/shard_map/ppermute | solution.py:272
  17.9 6.0 %collective-permute-start.4 = (bf16[16,4096]{1,0:T(8,128)(2,1)S(1)}, bf16[16,4096]{1,0:T(8,128)(2,1)S(1)}, u32[]{:S(2)}, u32[]{:S(2)}) collective-permute-start(bf16[16,4096]{1,0:T(8,128)(2,1)S(1)} %collective-permute-done.3.refs_5_), channel_id=1, source_target_pairs={{0,2},{2,0},{4,6},{6,4},{8,10},{10,8},{12,14},{14,12},{1,3},{3,1},... | collective-permute-start | bytes 393224 | tf_op jit(solution)/shard_map/ppermute | solution.py:272
  19.4 5.9 %collective-permute-start.2 = (bf16[16,4096]{1,0:T(8,128)(2,1)S(1)}, bf16[16,4096]{1,0:T(8,128)(2,1)S(1)}, u32[]{:S(2)}, u32[]{:S(2)}) collective-permute-start(bf16[16,4096]{1,0:T(8,128)(2,1)S(1)} %collective-permute-done.1.refs_3_), channel_id=1, source_target_pairs={{0,2},{2,0},{4,6},{6,4},{8,10},{10,8},{12,14},{14,12},{1,3},{3,1},... | collective-permute-start | bytes 393224 | tf_op jit(solution)/shard_map/ppermute | solution.py:272
  32.3 16.5 %collective-permute-start.7 = (f16[128,768]{1,0:T(8,128)(2,1)S(1)}, f16[128,768]{1,0:T(8,128)(2,1)S(1)}, u32[]{:S(2)}, u32[]{:S(2)}) collective-permute-start(f16[128,768]{1,0:T(8,128)(2,1)S(1)} %convert_element_type.91), channel_id=1, source_target_pairs={{0,1},{1,0},{2,3},{3,2},{4,5},{5,4},{6,7},{7,6},{8,9},{9,8},{10,11... | collective-permute-start | bytes 589832 | tf_op jit(solution)/shard_map/ppermute | solution.py:272
  40.3 8.6 %collective-permute-start.9 = (f16[128,768]{1,0:T(8,128)(2,1)S(1)}, f16[128,768]{1,0:T(8,128)(2,1)S(1)}, u32[]{:S(2)}, u32[]{:S(2)}) collective-permute-start(f16[128,768]{1,0:T(8,128)(2,1)S(1)} %convert_element_type.97), channel_id=1, source_target_pairs={{0,1},{1,0},{2,3},{3,2},{4,5},{5,4},{6,7},{7,6},{8,9},{9,8},{10,11... | collective-permute-start | bytes 589832 | tf_op jit(solution)/shard_map/ppermute | solution.py:272
  47.3 5.7 %collective-permute-start.8 = (f16[128,768]{1,0:T(8,128)(2,1)S(1)}, f16[128,768]{1,0:T(8,128)(2,1)S(1)}, u32[]{:S(2)}, u32[]{:S(2)}) collective-permute-start(f16[128,768]{1,0:T(8,128)(2,1)S(1)} %convert_element_type.94), channel_id=1, source_target_pairs={{0,1},{1,0},{2,3},{3,2},{4,5},{5,4},{6,7},{7,6},{8,9},{9,8},{10,11... | collective-permute-start | bytes 589832 | tf_op jit(solution)/shard_map/ppermute | solution.py:272
  58.7 3.6 %collective-permute-start.10 = (f32[1,128]{1,0:T(1,128)S(1)}, f32[1,128]{1,0:T(1,128)S(1)}, u32[]{:S(2)}, u32[]{:S(2)}) collective-permute-start(f32[1,128]{1,0:T(1,128)S(1)} %slice.3), channel_id=1, source_target_pairs={{0,2},{2,0},{4,6},{6,4},{8,10},{10,8},{12,14},{14,12},{1,3},{3,1},... | collective-permute-start | bytes 1544 | tf_op jit(solution)/shard_map/ppermute | solution.py:272
  62.9 8.2 %collective-permute-start.11 = (f32[1,128]{1,0:T(1,128)S(1)}, f32[1,128]{1,0:T(1,128)S(1)}, u32[]{:S(2)}, u32[]{:S(2)}) collective-permute-start(f32[1,128]{1,0:T(1,128)S(1)} %slice_add_fusion), channel_id=1, source_target_pairs={{0,4},{2,6},{4,0},{6,2},{8,12},{10,14},{12,8},{14,10},{1,5},{3,7},... | collective-permute-start | bytes 1544 | tf_op jit(solution)/shard_map/ppermute | solution.py:272
  71.1 9.3 %collective-permute-start.12 = (f32[1,128]{1,0:T(1,128)S(1)}, f32[1,128]{1,0:T(1,128)S(1)}, u32[]{:S(2)}, u32[]{:S(2)}) collective-permute-start(f32[1,128]{1,0:T(1,128)S(1)} %add.50), channel_id=1, source_target_pairs={{0,8},{2,10},{4,12},{6,14},{8,0},{10,2},{12,4},{14,6},{1,9},{3,11}... | collective-permute-start | bytes 1544 | tf_op jit(solution)/shard_map/ppermute | solution.py:272
  84.5 5.2 %collective-permute-start.13 = (bf16[16,4096]{1,0:T(8,128)(2,1)}, bf16[16,4096]{1,0:T(8,128)(2,1)S(1)}, u32[]{:S(2)}, u32[]{:S(2)}) collective-permute-start(bf16[16,4096]{1,0:T(8,128)(2,1)} %get-tuple-element.20), channel_id=1, source_target_pairs={{0,2},{2,0},{4,6},{6,4},{8,10},{10,8},{12,14},{14,12},{1,3},{3,1},... | collective-permute-start | bytes 393224 | tf_op jit(solution)/shard_map/ppermute | solution.py:272
  86.1 5.2 %collective-permute-start.15 = (bf16[16,4096]{1,0:T(8,128)(2,1)}, bf16[16,4096]{1,0:T(8,128)(2,1)S(1)}, u32[]{:S(2)}, u32[]{:S(2)}) collective-permute-start(bf16[16,4096]{1,0:T(8,128)(2,1)} %get-tuple-element.22), channel_id=1, source_target_pairs={{0,2},{2,0},{4,6},{6,4},{8,10},{10,8},{12,14},{14,12},{1,3},{3,1},... | collective-permute-start | bytes 393224 | tf_op jit(solution)/shard_map/ppermute | solution.py:272
  86.6 7.6 %collective-permute-start.17 = (bf16[16,4096]{1,0:T(8,128)(2,1)}, bf16[16,4096]{1,0:T(8,128)(2,1)S(1)}, u32[]{:S(2)}, u32[]{:S(2)}) collective-permute-start(bf16[16,4096]{1,0:T(8,128)(2,1)} %get-tuple-element.24), channel_id=1, source_target_pairs={{0,2},{2,0},{4,6},{6,4},{8,10},{10,8},{12,14},{14,12},{1,3},{3,1},... | collective-permute-start | bytes 393224 | tf_op jit(solution)/shard_map/ppermute | solution.py:272
  88.1 8.2 %collective-permute-start.19 = (bf16[16,4096]{1,0:T(8,128)(2,1)}, bf16[16,4096]{1,0:T(8,128)(2,1)S(1)}, u32[]{:S(2)}, u32[]{:S(2)}) collective-permute-start(bf16[16,4096]{1,0:T(8,128)(2,1)} %get-tuple-element.26), channel_id=1, source_target_pairs={{0,2},{2,0},{4,6},{6,4},{8,10},{10,8},{12,14},{14,12},{1,3},{3,1},... | collective-permute-start | bytes 393224 | tf_op jit(solution)/shard_map/ppermute | solution.py:272
  90.7 5.6 %collective-permute-start.14 = (bf16[16,4096]{1,0:T(8,128)(2,1)S(1)}, bf16[16,4096]{1,0:T(8,128)(2,1)S(1)}, u32[]{:S(2)}, u32[]{:S(2)}) collective-permute-start(bf16[16,4096]{1,0:T(8,128)(2,1)S(1)} %add_convert_fusion.3), channel_id=1, source_target_pairs={{0,4},{2,6},{4,0},{6,2},{8,12},{10,14},{12,8},{14,10},{1,5},{3,7},... | collective-permute-start | bytes 393224 | tf_op jit(solution)/shard_map/ppermute | solution.py:272
  92.2 6.9 %collective-permute-start.16 = (bf16[16,4096]{1,0:T(8,128)(2,1)S(1)}, bf16[16,4096]{1,0:T(8,128)(2,1)S(1)}, u32[]{:S(2)}, u32[]{:S(2)}) collective-permute-start(bf16[16,4096]{1,0:T(8,128)(2,1)S(1)} %add_convert_fusion.2), channel_id=1, source_target_pairs={{0,12},{2,14},{4,8},{6,10},{8,4},{10,6},{12,0},{14,2},{1,13},{3,15... | collective-permute-start | bytes 393224 | tf_op jit(solution)/shard_map/ppermute | solution.py:272
  95.1 7.3 %collective-permute-start.18 = (bf16[16,4096]{1,0:T(8,128)(2,1)S(1)}, bf16[16,4096]{1,0:T(8,128)(2,1)S(1)}, u32[]{:S(2)}, u32[]{:S(2)}) collective-permute-start(bf16[16,4096]{1,0:T(8,128)(2,1)S(1)} %add_convert_fusion.1), channel_id=1, source_target_pairs={{0,8},{2,10},{4,12},{6,14},{8,0},{10,2},{12,4},{14,6},{1,9},{3,11}... | collective-permute-start | bytes 393224 | tf_op jit(solution)/shard_map/ppermute | solution.py:272
  103.1 3.3 %collective-permute-start.20 = (f32[16,4096]{1,0:T(8,128)S(1)}, f32[16,4096]{1,0:T(8,128)S(1)}, u32[]{:S(2)}, u32[]{:S(2)}) collective-permute-start(f32[16,4096]{1,0:T(8,128)S(1)} %get-tuple-element.28), channel_id=1, source_target_pairs={{0,16},{16,0},{1,17},{17,1},{2,18},{18,2},{3,19},{19,3},{4,20},{20... | collective-permute-start | bytes 786440 | tf_op jit(solution)/shard_map/ppermute | solution.py:272
  103.2 5.5 %collective-permute-start.22 = (bf16[128,4096]{1,0:T(8,128)(2,1)S(1)}, bf16[128,4096]{1,0:T(8,128)(2,1)S(1)}, u32[]{:S(2)}, u32[]{:S(2)}) collective-permute-start(bf16[128,4096]{1,0:T(8,128)(2,1)S(1)} %copy-done), channel_id=1, source_target_pairs={{0,16},{16,0},{1,17},{17,1},{2,18},{18,2},{3,19},{19,3},{4,20},{20... | collective-permute-start | bytes 3145736 | tf_op jit(solution)/shard_map/ppermute | solution.py:272
  106.4 2.2 %collective-permute-start.21 = (bf16[128,2304]{1,0:T(8,128)(2,1)}, bf16[128,2304]{1,0:T(8,128)(2,1)S(1)}, u32[]{:S(2)}, u32[]{:S(2)}) collective-permute-start(bf16[128,2304]{1,0:T(8,128)(2,1)} %grads.1.g0_ref), channel_id=1, source_target_pairs={{0,16},{16,0},{1,17},{17,1},{2,18},{18,2},{3,19},{19,3},{4,20},{20... | collective-permute-start | bytes 1769480 | tf_op jit(solution)/shard_map/ppermute | solution.py:272
  (15 other events, 97.9 us)

commit v2 on v0

v2 whole, which is shorter than its diff:
```python
import functools

import jax
import jax.numpy as jnp
from jax import lax
from jax.experimental import pallas as pl
from jax.experimental.pallas import tpu as pltpu
from jax.sharding import PartitionSpec as P


soft_cap = 30.0
bf16 = jnp.bfloat16
f32 = jnp.float32
f16 = jnp.float16
MIB = 2**20


def params(n, limit=12):
    return pltpu.CompilerParams(
        dimension_semantics=("arbitrary",) * n if n else None, vmem_limit_bytes=limit * MIB
    )


def cost(flops, nbytes):
    return pl.CostEstimate(flops=int(flops), bytes_accessed=int(nbytes), transcendentals=0)


def smem():
    return pl.BlockSpec(memory_space=pltpu.SMEM)


def vmem():
    return pl.BlockSpec(memory_space=pltpu.VMEM)


def stage_kernel(ids_ref, u_ref, o_ref, sem):
    copy = pltpu.make_async_copy(u_ref, o_ref, sem)
    copy.start()
    copy.wait()


def stage_call(ids, unembed):
    return pl.pallas_call(
        stage_kernel,
        in_specs=[smem(), pl.BlockSpec(memory_space=pltpu.HBM)],
        out_specs=vmem(),
        out_shape=jax.ShapeDtypeStruct(unembed.shape, unembed.dtype),
        scratch_shapes=[pltpu.SemaphoreType.DMA],
        compiler_params=params(0, 28),
        cost_estimate=cost(unembed.size, 4 * unembed.size),
        name="stage",
    )(ids, unembed)


def first_kernel(n, ids_ref, *refs):
    parts, (u_ref, o_ref, h_ref, ht_ref) = refs[:n], refs[n:]
    rows = parts[0].shape[0]
    for k in range(n):
        at = pl.multiple_of((ids_ref[0] ^ k) * rows, rows)
        h_ref[pl.ds(at, rows), :] = parts[k][...]
    ht_ref[...] = h_ref[...].T
    count = o_ref.shape[1]
    o_ref[...] = jnp.dot(u_ref[:count, :], ht_ref[...], preferred_element_type=f32).T


def next_kernel(start, ht_ref, u_ref, o_ref):
    count = o_ref.shape[1]
    o_ref[...] = jnp.dot(
        u_ref[start : start + count, :], ht_ref[...], preferred_element_type=f32
    ).T


def first_call(ids, pieces, unembed, count):
    width = unembed.shape[1]
    tokens = sum(p.shape[0] for p in pieces)
    return pl.pallas_call(
        functools.partial(first_kernel, len(pieces)),
        in_specs=[smem()] + [vmem()] * (len(pieces) + 1),
        out_specs=[vmem()] * 3,
        out_shape=[
            jax.ShapeDtypeStruct((tokens, count), f32),
            jax.ShapeDtypeStruct((tokens, width), bf16),
            jax.ShapeDtypeStruct((width, tokens), bf16),
        ],
        compiler_params=params(0),
        cost_estimate=cost(2 * tokens * count * width, 2 * count * width),
        name="scores_first",
    )(ids, *pieces, unembed)


def next_call(turned, unembed, start, count):
    width, tokens = turned.shape
    return pl.pallas_call(
        functools.partial(next_kernel, start),
        in_specs=[vmem()] * 2,
        out_specs=vmem(),
        out_shape=jax.ShapeDtypeStruct((tokens, count), f32),
        compiler_params=params(0),
        cost_estimate=cost(2 * tokens * count * width, 2 * count * width),
        name="scores_next",
    )(turned, unembed)


def soften(s):
    squashed = jnp.tanh(s * (1.0 / soft_cap))
    return jnp.exp(soft_cap * squashed), 1.0 - squashed * squashed


def hits(first, targets, shape):
    ids = first + lax.broadcasted_iota(jnp.int32, shape, 1)
    return ids == targets


def column(row):
    return jnp.broadcast_to(row, (row.shape[1], row.shape[1])).T[:, :1]


def numer_kernel(start, ids_ref, s_ref, t_ref, *refs):
    q_ref, tot_ref, stat_ref = refs[-3:]
    tokens, rows = s_ref.shape
    targets = column(t_ref[...])
    sum_e = sum_q = sum_d = 0.0
    step = 128
    for j in range(0, rows, step):
        e, d = soften(s_ref[:, j : j + step])
        hit = hits(ids_ref[2] + (start + j), targets, e.shape)
        q = e * d
        q_ref[:tokens, j : j + step] = jnp.where(hit, 0.0, q).astype(bf16)
        q_ref[tokens:, j : j + step] = jnp.where(hit, 1.0, 0.0).astype(bf16)
        sum_e = sum_e + e
        sum_q = sum_q + jnp.where(hit, q, 0.0)
        sum_d = sum_d + jnp.where(hit, d, 0.0)
    tot, sq, sd = (jnp.sum(a.T, axis=0, keepdims=True) for a in (sum_e, sum_q, sum_d))
    if len(refs) > 3:
        tot = tot + refs[0][...]
        sq = sq + refs[1][:1, :]
        sd = sd + refs[1][1:2, :]
    tot_ref[...] = tot
    stat_ref[:1, :] = sq
    stat_ref[1:2, :] = sd


def numer_call(start, ids, s, targets, so_far):
    tokens, rows = s.shape
    return pl.pallas_call(
        functools.partial(numer_kernel, start),
        in_specs=[smem()] + [vmem()] * (2 + len(so_far)),
        out_specs=[vmem()] * 3,
        out_shape=[
            jax.ShapeDtypeStruct((2 * tokens, rows), bf16),
            jax.ShapeDtypeStruct((1, tokens), f32),
            jax.ShapeDtypeStruct((2, tokens), f32),
        ],
        compiler_params=params(0),
        cost_estimate=cost(40 * tokens * rows, 8 * tokens * rows),
        name="numer",
    )(ids, s, targets, *so_far)


def rows_kernel(start, block, count, *refs):
    qs, (u_ref, o_ref, q_ref) = refs[:count], refs[count:]

    @pl.when(pl.program_id(0) == 0)
    def _():
        at = 0
        for q in qs:
            q_ref[:, at : at + q.shape[1]] = q[...]
            at += q.shape[1]

    cols = pl.ds(pl.multiple_of(start + pl.program_id(0) * block, block), block)
    o_ref[...] = jnp.dot(q_ref[...], u_ref[:, cols], preferred_element_type=f32)


def rows_call(qs, unembed, start, width, block):
    rows = unembed.shape[0]
    two = qs[0].shape[0]
    return pl.pallas_call(
        functools.partial(rows_kernel, start, block, len(qs)),
        grid=(width // block,),
        in_specs=[vmem()] * (len(qs) + 1),
        out_specs=pl.BlockSpec((two, block), lambda i: (0, i)),
        out_shape=jax.ShapeDtypeStruct((two, width), f32),
        scratch_shapes=[pltpu.VMEM((two, rows), bf16)],
        compiler_params=params(1),
        cost_estimate=cost(2 * two * rows * width, 2 * rows * width),
        name="rows",
    )(*qs, unembed)


def norm_kernel(n, parts, ids_ref, tot_ref, stat_ref, lg_ref, *refs):
    outs = refs[parts : parts + n]
    sc, wc = refs[parts + n :]
    tokens = tot_ref.shape[1]
    rows = tokens // n
    total = tot_ref[...]
    lg = lg_ref[...]
    sc[...] = jnp.broadcast_to(lg / total, (tokens, tokens)).T
    weight = lg * (stat_ref[:1, :] / total - stat_ref[1:2, :])
    wc[...] = jnp.broadcast_to(weight, (tokens, tokens)).T
    for k in range(n):
        at = pl.multiple_of((ids_ref[0] ^ k) * rows, rows)
        a_s = sc[pl.ds(at, rows), :1]
        a_w = wc[pl.ds(at, rows), :1]
        col = 0
        for p in range(parts):
            width = refs[p].shape[1]
            a = refs[p][pl.ds(at, rows), :]
            u = refs[p][pl.ds(tokens + at, rows), :]
            outs[k][:, col : col + width] = (a_s * a + a_w * u).astype(bf16)
            col += width


def norm_call(n, ids, total, stats, loss_grad, sums):
    tokens = total.shape[1]
    width = sum(a.shape[1] for a in sums)
    return pl.pallas_call(
        functools.partial(norm_kernel, n, len(sums)),
        in_specs=[smem()] + [vmem()] * (3 + len(sums)),
        out_specs=[vmem()] * n,
        out_shape=[jax.ShapeDtypeStruct((tokens // n, width), bf16)] * n,
        scratch_shapes=[pltpu.VMEM((tokens, tokens), f32)] * 2,
        compiler_params=params(0),
        cost_estimate=cost(4 * tokens * width, 10 * tokens * width),
        name="norm",
    )(ids, total, stats, loss_grad, *sums)


def grads_kernel(count, ids_ref, t_ref, tot_ref, lg_ref, *refs):
    g_ref = refs[count]
    inv = column(1.0 / tot_ref[...])
    lg = column(lg_ref[...])
    targets = column(t_ref[...])
    step = 128
    at = 0
    for s_ref in refs[:count]:
        for j in range(0, s_ref.shape[1], step):
            e, d = soften(s_ref[:, j : j + step])
            hit = hits(ids_ref[2] + at, targets, e.shape)
            p = jnp.where(hit, e * inv - 1.0, e * inv)
            g_ref[:, at : at + step] = (lg * p * d).astype(bf16)
            at += step


def grads_call(ids, scores, targets, total, loss_grad):
    tokens = total.shape[1]
    rows = sum(s.shape[1] for s in scores)
    return pl.pallas_call(
        functools.partial(grads_kernel, len(scores)),
        in_specs=[smem()] + [vmem()] * (3 + len(scores)),
        out_specs=vmem(),
        out_shape=jax.ShapeDtypeStruct((tokens, rows), bf16),
        compiler_params=params(0),
        cost_estimate=cost(40 * tokens * rows, 6 * tokens * rows),
        name="grads",
    )(ids, targets, total, loss_grad, *scores)


def weight_kernel(ids_ref, g0_ref, g1_ref, h0_ref, h1_ref, *refs):
    o_ref, g_ref, h_ref = refs[-3:]
    tokens = h0_ref.shape[0]
    mine = pl.multiple_of(ids_ref[1] * tokens, tokens)
    other = pl.multiple_of((1 - ids_ref[1]) * tokens, tokens)

    @pl.when(pl.program_id(0) == 0)
    def _():
        h_ref[pl.ds(mine, tokens), :] = h0_ref[...]
        h_ref[pl.ds(other, tokens), :] = h1_ref[...]

    g_ref[pl.ds(mine, tokens), :] = g0_ref[...]
    g_ref[pl.ds(other, tokens), :] = g1_ref[...]
    o_ref[...] = lax.dot_general(
        g_ref[...], h_ref[...], (((0,), (0,)), ((), ())), preferred_element_type=f32
    )


def weight_call(ids, g0, g1, h0, h1, start, count, block, into):
    tokens, rows = g0.shape
    width = h0.shape[1]
    g_spec = pl.BlockSpec((tokens, block), lambda i: (0, start // block + i))
    operands = [ids, g0, g1, h0, h1]
    specs = [smem(), g_spec, g_spec, vmem(), vmem()]
    alias = {}
    if into is not None:
        operands.append(into)
        specs.append(pl.BlockSpec(memory_space=pl.ANY))
        alias = {5: 0}
    return pl.pallas_call(
        weight_kernel,
        grid=(count // block,),
        in_specs=specs,
        out_specs=pl.BlockSpec((block, width), lambda i: (start // block + i, 0)),
        out_shape=jax.ShapeDtypeStruct((rows, width), f32),
        scratch_shapes=[pltpu.VMEM((2 * tokens, block), bf16), pltpu.VMEM((2 * tokens, width), bf16)],
        input_output_aliases=alias,
        compiler_params=params(1, 24),
        cost_estimate=cost(4 * tokens * count * width, 4 * count * width),
        name="weight",
    )(*operands)


def swap(x, axis, mask, size):
    return lax.ppermute(x, axis, [(i, i ^ mask) for i in range(size)])


def split(total, unit):
    tiles = total // unit
    sizes = [1, (tiles - 2) // 2, (tiles - 3) // 2, 2]
    starts = [sum(sizes[:i]) for i in range(len(sizes))]
    return [(a * unit, c * unit) for a, c in zip(starts, sizes)]


def thirds(total, unit):
    tiles = total // unit
    sizes = [(tiles + 2) // 3, (tiles + 1) // 3, tiles // 3]
    starts = [sum(sizes[:i]) for i in range(3)]
    return [(a * unit, c * unit) for a, c in zip(starts, sizes)]


def fast(n, trunk, branch, unembed, targets, loss_grad):
    block_rows, width = unembed.shape
    seq_index = lax.axis_index("seq")
    ids = jnp.stack([seq_index, lax.axis_index("head"), seq_index * block_rows]).astype(jnp.int32)
    hidden = (trunk.astype(f32) + branch[0].astype(f32)).astype(bf16)
    far = [k for k in (2, 6, 4) if k < n]

    pieces = [None] * n
    pieces[0] = hidden
    for k in far:
        pieces[k] = swap(hidden, "seq", k, n)
    for k in [0] + far:
        pieces[k + 1] = swap(pieces[k], "seq", 1, n)

    unembed = stage_call(ids, unembed)
    chunks = split(block_rows, 256)
    scores, qs, so_far = [], [], []
    for c, (start, count) in enumerate(chunks):
        if c == 0:
            s, all_hidden, turned = first_call(ids, pieces, unembed, count)
        else:
            s = next_call(turned, unembed, start, count)
        s = s.astype(f16)
        scores.append(s.astype(f32) + swap(s, "mp", 1, 2).astype(f32))
    other_hidden = swap(all_hidden, "head", 1, 2)
    for c, (start, count) in enumerate(chunks):
        q, *so_far = numer_call(start, ids, scores[c], targets, so_far)
        qs.append(q)
    total, stats = so_far

    for i in range(n.bit_length() - 1):
        total = total + swap(total, "seq", 1 << i, n)
    sums = []
    for start, count in thirds(width, 512):
        sums.append(rows_call(qs, unembed, start, count, 512))
    blocks = norm_call(n, ids, total, stats, loss_grad, sums)

    got = []
    for k in far + [0]:
        theirs = swap(blocks[k + 1], "seq", 1, n)
        both = blocks[k].astype(f32) + theirs.astype(f32)
        if k:
            both = swap(both.astype(bf16), "seq", k, n).astype(f32)
        got.append(both)
    row_grad = functools.reduce(lambda a, b: a + b, got)

    g = grads_call(ids, scores, targets, total, loss_grad)
    g_other = swap(g, "head", 1, 2)
    d_unembed = None
    for start, count in thirds(block_rows, 256):
        d_unembed = weight_call(
            ids, g, g_other, all_hidden, other_hidden, start, count, 256, d_unembed
        )

    d_trunk = row_grad + swap(row_grad, "head", 1, 2)
    return (row_grad.astype(bf16)[None], d_trunk.astype(bf16), d_unembed)


def general(trunk, branch, unembed, targets, loss_grad):
    block_rows = unembed.shape[0]
    hidden = (trunk.astype(f32) + branch[0].astype(f32)).astype(bf16)
    gathered = lax.all_gather(hidden, "seq", axis=0, tiled=True)
    seq_index = lax.axis_index("seq")
    scores = lax.psum(
        lax.dot_general(unembed, gathered, (((1,), (1,)), ((), ())), preferred_element_type=f32),
        "mp",
    )
    exponent, slope = soften(scores)
    totals = lax.psum(jnp.sum(exponent, axis=0), "seq")
    vocab_ids = seq_index * block_rows + lax.iota(jnp.int32, block_rows)
    onehot = (vocab_ids[:, None] == targets[0][None, :]).astype(f32)
    grad_logits = (
        loss_grad[0][None, :] * (exponent / totals[None, :] - onehot) * slope
    ).astype(bf16)
    row_grad = lax.psum_scatter(
        lax.dot_general(grad_logits, unembed, (((0,), (0,)), ((), ())), preferred_element_type=f32),
        "seq",
        scatter_dimension=0,
        tiled=True,
    )
    weight_grad = jnp.dot(grad_logits, gathered, preferred_element_type=f32)
    trunk_sum, unembed_sum = lax.psum((row_grad, weight_grad), "head")
    return (row_grad.astype(bf16)[None], trunk_sum.astype(bf16), unembed_sum)


def solution(mesh):
    in_specs = (
        P("seq", "mp"),
        P("head", "seq", "mp"),
        P("seq", "mp"),
        P("head", None),
        P("head", None),
    )
    out_specs = (P("head", "seq", "mp"), P("seq", "mp"), P("seq", "mp"))
    n = mesh.shape["seq"]
    if mesh.shape["head"] == 2 and mesh.shape["mp"] == 2 and n == 8:

        def body(*args):
            return fast(n, *args)
    else:
        body = general
    step = jax.shard_map(body, mesh=mesh, in_specs=in_specs, out_specs=out_specs, check_vma=False)
    if body is general:
        return step
    return step
```

time: 360 us -> 103 us (0.29)
  waiting for transfers between devices: 244 us -> 25.6 us
  Pallas kernels: 0 us -> 44.8 us
  matrix products: 40.7 us -> 0 us
  local copies, waits for them, and re-layouts: 28.4 us -> 0.01 us
  starting transfers between devices: 0.16 us -> 28.2 us
  blocking collectives: 26.8 us -> 0 us
  between operations: 13.8 us -> 0.88 us
    psum x2 -> x0, waiting for transfers between devices: 152 us -> none  [the longest x1 110 us: shards(): trunk_sum, unembed_sum = lax.psum((row_grad, weight_grad), 'head')]
    reduce_scatter x1 -> x0, waiting for transfers between devices: 47.7 us -> none  [shards(): lax.psum_scatter(lax.dot_general(grad_logits, unembed, (((0,), (0,)), (()...]
    pallas_call x0 -> x17, Pallas kernels: none -> 44.8 us  [the longest x3 18.7 us: weight_call(): pl.pallas_call(weight_kernel, grid=(count // block,), in_specs=specs, out...]
    all_gather x1 -> x0, waiting for transfers between devices: 44.8 us -> none  [shards(): gathered = lax.all_gather(hidden, 'seq', axis=0, tiled=True)]
    dot_general x3 -> x0, matrix products: 40.7 us -> none  [the longest x1 15.9 us: shards(): jnp.dot(grad_logits, gathered, preferred_element_type=jnp.float32)]
    unnamed x9 -> x4, local copies, waits for them, and re-layouts: 28.4 us -> 0.01 us
    ppermute x0 -> x24, starting transfers between devices: none -> 28.2 us  [swap(): return lax.ppermute(x, axis, [(i, i ^ mask) for i in range(size)])]
    psum x2 -> x0, blocking collectives: 26.8 us -> none  [the longest x1 21.4 us: shards(): totals = lax.psum(jnp.sum(exponent, axis=0), 'seq')]
  transfers between devices with their start and end apart: 4 -> 24, of which waited for: 4 -> 13; matrix products, arithmetic and copies ran while one was open for 5% -> 1% of each run, Pallas kernels for 0% -> 18%
where the time goes in v2:
time: 103 us; the launch traced here: 102 us
  Pallas kernels  44.8 us (43%)
  starting transfers between devices  28.2 us (27%)
  waiting for transfers between devices  25.6 us (25%)
  other arithmetic  2.84 us (3%)
    ppermute x24, starting transfers between devices, swap(): return lax.ppermute(x, axis, [(i, i ^ mask) for i in range(size)])  28.2 us
    ppermute x24, waiting for transfers between devices, swap(): return lax.ppermute(x, axis, [(i, i ^ mask) for i in range(size)])  25.6 us
    pallas_call x3, Pallas kernels, weight_call(): pl.pallas_call(weight_kernel, grid=(count // block,), in_specs=specs, out...  18.7 us
    pallas_call x3, Pallas kernels, rows_call(): pl.pallas_call(functools.partial(rows_kernel, start, block, len(qs)), gri...  6.95 us
    pallas_call x1, Pallas kernels, stage_call(): pl.pallas_call(stage_kernel, in_specs=[smem(), pl.BlockSpec(memory_space=...  6.92 us
    pallas_call x3, Pallas kernels, next_call(): pl.pallas_call(functools.partial(next_kernel, start), in_specs=[vmem()] *...  5.02 us
    pallas_call x4, Pallas kernels, numer_call(): pl.pallas_call(functools.partial(numer_kernel, start), in_specs=[smem()]...  3.41 us
  transfers between devices with their start and end apart: 24, of which 13 were waited for; matrix products, arithmetic and copies ran while one was open for 1% of the time, Pallas kernels for 18%

profile of v2, /device:TPU:0, one launch (start us, length us, event | category | flops | bytes accessed | tf_op | source)
XLA Modules:
  0.0 102.3 jit_solution(10631831807444136964)
XLA Ops:
  1.6 5.1 %collective-permute-start.5 = (bf16[16,4096]{1,0:T(8,128)(2,1)S(1)}, bf16[16,4096]{1,0:T(8,128)(2,1)S(1)}, u32[]{:S(2)}, u32[]{:S(2)}) collective-permute-start(bf16[16,4096]{1,0:T(8,128)(2,1)S(1)} %fusion.refs_0_), channel_id=1, source_target_pairs={{0,12},{2,14},{4,8},{6,10},{8,4},{10,6},{12,0},{14,2},{1,13},{3,15... | collective-permute-start | bytes 393224 | tf_op jit(solution)/shard_map/ppermute | solution.py:302
  7.4 1.7 %collective-permute-start = (bf16[16,4096]{1,0:T(8,128)(2,1)S(1)}, bf16[16,4096]{1,0:T(8,128)(2,1)S(1)}, u32[]{:S(2)}, u32[]{:S(2)}) collective-permute-start(bf16[16,4096]{1,0:T(8,128)(2,1)S(1)} %fusion.refs_0_), channel_id=1, source_target_pairs={{0,2},{2,0},{4,6},{6,4},{8,10},{10,8},{12,14},{14,12},{1,3},{3,1},... | collective-permute-start | bytes 393224 | tf_op jit(solution)/shard_map/ppermute | solution.py:302
  9.1 2.1 %collective-permute-done.5.refs_6_ = bf16[16,4096]{1,0:T(8,128)(2,1)S(1)} collective-permute-done((bf16[16,4096]{1,0:T(8,128)(2,1)S(1)}, bf16[16,4096]{1,0:T(8,128)(2,1)S(1)}, u32[]{:S(2)}, u32[]{:S(2)}) %collective-permute-start.5) | collective-permute-done | bytes 131104 | tf_op jit(solution)/shard_map/ppermute | solution.py:302
  11.2 1.7 %collective-permute-start.6 = (bf16[16,4096]{1,0:T(8,128)(2,1)S(1)}, bf16[16,4096]{1,0:T(8,128)(2,1)S(1)}, u32[]{:S(2)}, u32[]{:S(2)}) collective-permute-start(bf16[16,4096]{1,0:T(8,128)(2,1)S(1)} %collective-permute-done.5.refs_6_), channel_id=1, source_target_pairs={{0,2},{2,0},{4,6},{6,4},{8,10},{10,8},{12,14},{14,12},{1,3},{3,1},... | collective-permute-start | bytes 393224 | tf_op jit(solution)/shard_map/ppermute | solution.py:302
  12.9 4.9 %collective-permute-done.3.refs_4_ = bf16[16,4096]{1,0:T(8,128)(2,1)S(1)} collective-permute-done((bf16[16,4096]{1,0:T(8,128)(2,1)S(1)}, bf16[16,4096]{1,0:T(8,128)(2,1)S(1)}, u32[]{:S(2)}, u32[]{:S(2)}) %collective-permute-start.3) | collective-permute-done | bytes 131104 | tf_op jit(solution)/shard_map/ppermute | solution.py:302
  17.9 1.5 %collective-permute-start.4 = (bf16[16,4096]{1,0:T(8,128)(2,1)S(1)}, bf16[16,4096]{1,0:T(8,128)(2,1)S(1)}, u32[]{:S(2)}, u32[]{:S(2)}) collective-permute-start(bf16[16,4096]{1,0:T(8,128)(2,1)S(1)} %collective-permute-done.3.refs_4_), channel_id=1, source_target_pairs={{0,2},{2,0},{4,6},{6,4},{8,10},{10,8},{12,14},{14,12},{1,3},{3,1},... | collective-permute-start | bytes 393224 | tf_op jit(solution)/shard_map/ppermute | solution.py:302
  20.0 6.9 %stage.1.refs_8_.u_ref.refs_4_ = bf16[2304,4096]{1,0:T(8,128)(2,1)S(1)} custom-call(s32[3]{0:T(128)S(1)} %pad_add_fusion.ids_ref, bf16[2304,4096]{1,0:T(8,128)(2,1)} %u_ref.1), custom_call_target="tpu_custom_call" | custom-call | flops 9437184 | bytes 37748736 | tf_op jit(solution)/shard_map/stage/pallas_call | solution.py:43
  29.8 1.8 %scores_next.4 = f32[128,768]{1,0:T(8,128)S(1)} custom-call(bf16[4096,128]{1,0:T(8,128)(2,1)S(1)} %get-tuple-element.26.ht_ref, bf16[2304,4096]{1,0:T(8,128)(2,1)S(1)} %stage.1.refs_8_.u_ref.refs_4_), custom_call_target="tpu_custom_call" | custom-call | flops 805306368 | bytes 6291456 | tf_op jit(solution)/shard_map/scores_next/pallas_call | solution.py:93
  31.6 1.6 %collective-permute-start.10 = (f16[128,256]{1,0:T(8,128)(2,1)S(1)}, f16[128,256]{1,0:T(8,128)(2,1)S(1)}, u32[]{:S(2)}, u32[]{:S(2)}) collective-permute-start(f16[128,256]{1,0:T(8,128)(2,1)S(1)} %convert_element_type.109), channel_id=1, source_target_pairs={{0,1},{1,0},{2,3},{3,2},{4,5},{5,4},{6,7},{7,6},{8,9},{9,8},{10,11... | collective-permute-start | bytes 196616 | tf_op jit(solution)/shard_map/ppermute | solution.py:302
  33.8 1.9 %scores_next.5 = f32[128,768]{1,0:T(8,128)S(1)} custom-call(bf16[4096,128]{1,0:T(8,128)(2,1)S(1)} %get-tuple-element.26.ht_ref, bf16[2304,4096]{1,0:T(8,128)(2,1)S(1)} %stage.1.refs_8_.u_ref.refs_4_), custom_call_target="tpu_custom_call" | custom-call | flops 805306368 | bytes 6291456 | tf_op jit(solution)/shard_map/scores_next/pallas_call | solution.py:93
  35.7 1.6 %collective-permute-start.9 = (f16[128,768]{1,0:T(8,128)(2,1)S(1)}, f16[128,768]{1,0:T(8,128)(2,1)S(1)}, u32[]{:S(2)}, u32[]{:S(2)}) collective-permute-start(f16[128,768]{1,0:T(8,128)(2,1)S(1)} %convert_element_type.106), channel_id=1, source_target_pairs={{0,1},{1,0},{2,3},{3,2},{4,5},{5,4},{6,7},{7,6},{8,9},{9,8},{10,11... | collective-permute-start | bytes 589832 | tf_op jit(solution)/shard_map/ppermute | solution.py:302
  39.7 4.2 %collective-permute-done.9 = f16[128,768]{1,0:T(8,128)(2,1)S(1)} collective-permute-done((f16[128,768]{1,0:T(8,128)(2,1)S(1)}, f16[128,768]{1,0:T(8,128)(2,1)S(1)}, u32[]{:S(2)}, u32[]{:S(2)}) %collective-permute-start.9) | collective-permute-done | bytes 196640 | tf_op jit(solution)/shard_map/ppermute | solution.py:302
  48.0 1.6 %collective-permute-start.11 = (f32[1,128]{1,0:T(1,128)S(1)}, f32[1,128]{1,0:T(1,128)S(1)}, u32[]{:S(2)}, u32[]{:S(2)}) collective-permute-start(f32[1,128]{1,0:T(1,128)S(1)} %get-tuple-element.34), channel_id=1, source_target_pairs={{0,2},{2,0},{4,6},{6,4},{8,10},{10,8},{12,14},{14,12},{1,3},{3,1},... | collective-permute-start | bytes 1544 | tf_op jit(solution)/shard_map/ppermute | solution.py:302
  49.6 2.6 %rows.4.refs_1_ = f32[256,1536]{1,0:T(8,128)S(1)} custom-call(bf16[256,256]{1,0:T(8,128)(2,1)S(1)} %get-tuple-element.36.refs_0_, bf16[256,768]{1,0:T(8,128)(2,1)S(1)} %get-tuple-element.37.refs_1_, bf16[256,768]{1,0:T(8,128)(2,1)S(1)} %get-tuple-element.38.refs_2_, bf16[256,512]{1,0:T(8,128)(2,1)S(1)} %get-tuple-element.39.refs_3_, ...), custom_call_target="tpu_custom_call" | custom-call | flops 1811939328 | bytes 7077888 | tf_op jit(solution)/shard_map/rows/pallas_call | solution.py:177
  52.3 2.6 %rows.3.refs_0_ = f32[256,1536]{1,0:T(8,128)S(1)} custom-call(bf16[256,256]{1,0:T(8,128)(2,1)S(1)} %get-tuple-element.36.refs_0_, bf16[256,768]{1,0:T(8,128)(2,1)S(1)} %get-tuple-element.37.refs_1_, bf16[256,768]{1,0:T(8,128)(2,1)S(1)} %get-tuple-element.38.refs_2_, bf16[256,512]{1,0:T(8,128)(2,1)S(1)} %get-tuple-element.39.refs_3_, ...), custom_call_target="tpu_custom_call" | custom-call | flops 1811939328 | bytes 7077888 | tf_op jit(solution)/shard_map/rows/pallas_call | solution.py:177
  55.9 2.0 %collective-permute-start.13 = (f32[1,128]{1,0:T(1,128)S(1)}, f32[1,128]{1,0:T(1,128)S(1)}, u32[]{:S(2)}, u32[]{:S(2)}) collective-permute-start(f32[1,128]{1,0:T(1,128)S(1)} %add.54), channel_id=1, source_target_pairs={{0,8},{2,10},{4,12},{6,14},{8,0},{10,2},{12,4},{14,6},{1,9},{3,11}... | collective-permute-start | bytes 1544 | tf_op jit(solution)/shard_map/ppermute | solution.py:302
  57.9 1.8 %rows.5.refs_2_ = f32[256,1024]{1,0:T(8,128)S(1)} custom-call(bf16[256,256]{1,0:T(8,128)(2,1)S(1)} %get-tuple-element.36.refs_0_, bf16[256,768]{1,0:T(8,128)(2,1)S(1)} %get-tuple-element.37.refs_1_, bf16[256,768]{1,0:T(8,128)(2,1)S(1)} %get-tuple-element.38.refs_2_, bf16[256,512]{1,0:T(8,128)(2,1)S(1)} %get-tuple-element.39.refs_3_, ...), custom_call_target="tpu_custom_call" | custom-call | flops 1207959552 | bytes 4718592 | tf_op jit(solution)/shard_map/rows/pallas_call | solution.py:177
  65.6 2.1 %collective-permute-done.14 = bf16[16,4096]{1,0:T(8,128)(2,1)S(1)} collective-permute-done((bf16[16,4096]{1,0:T(8,128)(2,1)S(1)}, bf16[16,4096]{1,0:T(8,128)(2,1)S(1)}, u32[]{:S(2)}, u32[]{:S(2)}) %collective-permute-start.14) | collective-permute-done | bytes 131104 | tf_op jit(solution)/shard_map/ppermute | solution.py:302
  69.1 2.0 %collective-permute-start.17 = (bf16[16,4096]{1,0:T(8,128)(2,1)S(1)}, bf16[16,4096]{1,0:T(8,128)(2,1)S(1)}, u32[]{:S(2)}, u32[]{:S(2)}) collective-permute-start(bf16[16,4096]{1,0:T(8,128)(2,1)S(1)} %add_convert_fusion.2), channel_id=1, source_target_pairs={{0,12},{2,14},{4,8},{6,10},{8,4},{10,6},{12,0},{14,2},{1,13},{3,15... | collective-permute-start | bytes 393224 | tf_op jit(solution)/shard_map/ppermute | solution.py:302
  73.6 2.4 %collective-permute-done.17 = bf16[16,4096]{1,0:T(8,128)(2,1)S(1)} collective-permute-done((bf16[16,4096]{1,0:T(8,128)(2,1)S(1)}, bf16[16,4096]{1,0:T(8,128)(2,1)S(1)}, u32[]{:S(2)}, u32[]{:S(2)}) %collective-permute-start.17) | collective-permute-done | bytes 131104 | tf_op jit(solution)/shard_map/ppermute | solution.py:302
  76.1 2.9 %collective-permute-done.19 = bf16[16,4096]{1,0:T(8,128)(2,1)S(1)} collective-permute-done((bf16[16,4096]{1,0:T(8,128)(2,1)S(1)}, bf16[16,4096]{1,0:T(8,128)(2,1)S(1)}, u32[]{:S(2)}, u32[]{:S(2)}) %collective-permute-start.19) | collective-permute-done | bytes 131104 | tf_op jit(solution)/shard_map/ppermute | solution.py:302
  83.6 6.2 %weight.3.refs_0_ = f32[2304,4096]{1,0:T(8,128)} custom-call(s32[3]{0:T(128)S(1)} %pad_add_fusion.ids_ref, bf16[128,2304]{1,0:T(8,128)(2,1)S(1)} %grads.1.g0_ref, bf16[128,2304]{1,0:T(8,128)(2,1)S(1)} %collective-permute-done.22.g1_ref, bf16[128,4096]{1,0:T(8,128)(2,1)S(1)} %get-tuple-element.48.h0_ref, bf16[128,4096]{1,0:T(8,128)(2,1)S(1)} %collective-permute-done.23.h1_ref), custom_call_target="tpu_custom_call" | custom-call | flops 1610612736 | bytes 12582912 | tf_op jit(solution)/shard_map/weight/pallas_call | solution.py:287
  89.9 6.2 %weight.4.refs_0_ = f32[2304,4096]{1,0:T(8,128)} custom-call(s32[3]{0:T(128)S(1)} %pad_add_fusion.ids_ref, bf16[128,2304]{1,0:T(8,128)(2,1)S(1)} %grads.1.g0_ref, bf16[128,2304]{1,0:T(8,128)(2,1)S(1)} %collective-permute-done.22.g1_ref, bf16[128,4096]{1,0:T(8,128)(2,1)S(1)} %get-tuple-element.48.h0_ref, ...), custom_call_target="tpu_custom_call", output_to_operand_aliasing={{}: (5, {})} | custom-call | flops 1610612736 | bytes 12582912 | tf_op jit(solution)/shard_map/weight/pallas_call | solution.py:287
  96.1 6.2 %weight.5 = f32[2304,4096]{1,0:T(8,128)} custom-call(s32[3]{0:T(128)S(1)} %pad_add_fusion.ids_ref, bf16[128,2304]{1,0:T(8,128)(2,1)S(1)} %grads.1.g0_ref, bf16[128,2304]{1,0:T(8,128)(2,1)S(1)} %collective-permute-done.22.g1_ref, bf16[128,4096]{1,0:T(8,128)(2,1)S(1)} %get-tuple-element.48.h0_ref, ...), custom_call_target="tpu_custom_call", output_to_operand_aliasing={{}: (5, {})} | custom-call | flops 1610612736 | bytes 12582912 | tf_op jit(solution)/shard_map/weight/pallas_call | solution.py:287
  (63 shorter events, 27.7 us)
Async XLA Ops:
  1.6 9.6 %collective-permute-start.5 = (bf16[16,4096]{1,0:T(8,128)(2,1)S(1)}, bf16[16,4096]{1,0:T(8,128)(2,1)S(1)}, u32[]{:S(2)}, u32[]{:S(2)}) collective-permute-start(bf16[16,4096]{1,0:T(8,128)(2,1)S(1)} %fusion.refs_0_), channel_id=1, source_target_pairs={{0,12},{2,14},{4,8},{6,10},{8,4},{10,6},{12,0},{14,2},{1,13},{3,15... | collective-permute-start | bytes 393224 | tf_op jit(solution)/shard_map/ppermute | solution.py:302
  6.8 11.1 %collective-permute-start.3 = (bf16[16,4096]{1,0:T(8,128)(2,1)S(1)}, bf16[16,4096]{1,0:T(8,128)(2,1)S(1)}, u32[]{:S(2)}, u32[]{:S(2)}) collective-permute-start(bf16[16,4096]{1,0:T(8,128)(2,1)S(1)} %fusion.refs_0_), channel_id=1, source_target_pairs={{0,8},{2,10},{4,12},{6,14},{8,0},{10,2},{12,4},{14,6},{1,9},{3,11}... | collective-permute-start | bytes 393224 | tf_op jit(solution)/shard_map/ppermute | solution.py:302
  6.8 12.6 %collective-permute-start.1 = (bf16[16,4096]{1,0:T(8,128)(2,1)S(1)}, bf16[16,4096]{1,0:T(8,128)(2,1)S(1)}, u32[]{:S(2)}, u32[]{:S(2)}) collective-permute-start(bf16[16,4096]{1,0:T(8,128)(2,1)S(1)} %fusion.refs_0_), channel_id=1, source_target_pairs={{0,4},{2,6},{4,0},{6,2},{8,12},{10,14},{12,8},{14,10},{1,5},{3,7},... | collective-permute-start | bytes 393224 | tf_op jit(solution)/shard_map/ppermute | solution.py:302
  7.4 19.5 %collective-permute-start = (bf16[16,4096]{1,0:T(8,128)(2,1)S(1)}, bf16[16,4096]{1,0:T(8,128)(2,1)S(1)}, u32[]{:S(2)}, u32[]{:S(2)}) collective-permute-start(bf16[16,4096]{1,0:T(8,128)(2,1)S(1)} %fusion.refs_0_), channel_id=1, source_target_pairs={{0,2},{2,0},{4,6},{6,4},{8,10},{10,8},{12,14},{14,12},{1,3},{3,1},... | collective-permute-start | bytes 393224 | tf_op jit(solution)/shard_map/ppermute | solution.py:302
  11.2 15.7 %collective-permute-start.6 = (bf16[16,4096]{1,0:T(8,128)(2,1)S(1)}, bf16[16,4096]{1,0:T(8,128)(2,1)S(1)}, u32[]{:S(2)}, u32[]{:S(2)}) collective-permute-start(bf16[16,4096]{1,0:T(8,128)(2,1)S(1)} %collective-permute-done.5.refs_6_), channel_id=1, source_target_pairs={{0,2},{2,0},{4,6},{6,4},{8,10},{10,8},{12,14},{14,12},{1,3},{3,1},... | collective-permute-start | bytes 393224 | tf_op jit(solution)/shard_map/ppermute | solution.py:302
  17.9 9.1 %collective-permute-start.4 = (bf16[16,4096]{1,0:T(8,128)(2,1)S(1)}, bf16[16,4096]{1,0:T(8,128)(2,1)S(1)}, u32[]{:S(2)}, u32[]{:S(2)}) collective-permute-start(bf16[16,4096]{1,0:T(8,128)(2,1)S(1)} %collective-permute-done.3.refs_4_), channel_id=1, source_target_pairs={{0,2},{2,0},{4,6},{6,4},{8,10},{10,8},{12,14},{14,12},{1,3},{3,1},... | collective-permute-start | bytes 393224 | tf_op jit(solution)/shard_map/ppermute | solution.py:302
  19.4 7.5 %collective-permute-start.2 = (bf16[16,4096]{1,0:T(8,128)(2,1)S(1)}, bf16[16,4096]{1,0:T(8,128)(2,1)S(1)}, u32[]{:S(2)}, u32[]{:S(2)}) collective-permute-start(bf16[16,4096]{1,0:T(8,128)(2,1)S(1)} %collective-permute-done.1.refs_2_), channel_id=1, source_target_pairs={{0,2},{2,0},{4,6},{6,4},{8,10},{10,8},{12,14},{14,12},{1,3},{3,1},... | collective-permute-start | bytes 393224 | tf_op jit(solution)/shard_map/ppermute | solution.py:302
  31.6 6.2 %collective-permute-start.10 = (f16[128,256]{1,0:T(8,128)(2,1)S(1)}, f16[128,256]{1,0:T(8,128)(2,1)S(1)}, u32[]{:S(2)}, u32[]{:S(2)}) collective-permute-start(f16[128,256]{1,0:T(8,128)(2,1)S(1)} %convert_element_type.109), channel_id=1, source_target_pairs={{0,1},{1,0},{2,3},{3,2},{4,5},{5,4},{6,7},{7,6},{8,9},{9,8},{10,11... | collective-permute-start | bytes 196616 | tf_op jit(solution)/shard_map/ppermute | solution.py:302
  33.2 6.4 %collective-permute-start.7 = (f16[128,512]{1,0:T(8,128)(2,1)S(1)}, f16[128,512]{1,0:T(8,128)(2,1)S(1)}, u32[]{:S(2)}, u32[]{:S(2)}) collective-permute-start(f16[128,512]{1,0:T(8,128)(2,1)S(1)} %convert_element_type.100), channel_id=1, source_target_pairs={{0,1},{1,0},{2,3},{3,2},{4,5},{5,4},{6,7},{7,6},{8,9},{9,8},{10,11... | collective-permute-start | bytes 393224 | tf_op jit(solution)/shard_map/ppermute | solution.py:302
  35.7 8.1 %collective-permute-start.9 = (f16[128,768]{1,0:T(8,128)(2,1)S(1)}, f16[128,768]{1,0:T(8,128)(2,1)S(1)}, u32[]{:S(2)}, u32[]{:S(2)}) collective-permute-start(f16[128,768]{1,0:T(8,128)(2,1)S(1)} %convert_element_type.106), channel_id=1, source_target_pairs={{0,1},{1,0},{2,3},{3,2},{4,5},{5,4},{6,7},{7,6},{8,9},{9,8},{10,11... | collective-permute-start | bytes 589832 | tf_op jit(solution)/shard_map/ppermute | solution.py:302
  37.3 9.0 %collective-permute-start.8 = (f16[128,768]{1,0:T(8,128)(2,1)S(1)}, f16[128,768]{1,0:T(8,128)(2,1)S(1)}, u32[]{:S(2)}, u32[]{:S(2)}) collective-permute-start(f16[128,768]{1,0:T(8,128)(2,1)S(1)} %convert_element_type.103), channel_id=1, source_target_pairs={{0,1},{1,0},{2,3},{3,2},{4,5},{5,4},{6,7},{7,6},{8,9},{9,8},{10,11... | collective-permute-start | bytes 589832 | tf_op jit(solution)/shard_map/ppermute | solution.py:302
  48.0 4.2 %collective-permute-start.11 = (f32[1,128]{1,0:T(1,128)S(1)}, f32[1,128]{1,0:T(1,128)S(1)}, u32[]{:S(2)}, u32[]{:S(2)}) collective-permute-start(f32[1,128]{1,0:T(1,128)S(1)} %get-tuple-element.34), channel_id=1, source_target_pairs={{0,2},{2,0},{4,6},{6,4},{8,10},{10,8},{12,14},{14,12},{1,3},{3,1},... | collective-permute-start | bytes 1544 | tf_op jit(solution)/shard_map/ppermute | solution.py:302
  52.3 3.6 %collective-permute-start.12 = (f32[1,128]{1,0:T(1,128)S(1)}, f32[1,128]{1,0:T(1,128)S(1)}, u32[]{:S(2)}, u32[]{:S(2)}) collective-permute-start(f32[1,128]{1,0:T(1,128)S(1)} %add.53), channel_id=1, source_target_pairs={{0,4},{2,6},{4,0},{6,2},{8,12},{10,14},{12,8},{14,10},{1,5},{3,7},... | collective-permute-start | bytes 1544 | tf_op jit(solution)/shard_map/ppermute | solution.py:302
  55.9 4.5 %collective-permute-start.13 = (f32[1,128]{1,0:T(1,128)S(1)}, f32[1,128]{1,0:T(1,128)S(1)}, u32[]{:S(2)}, u32[]{:S(2)}) collective-permute-start(f32[1,128]{1,0:T(1,128)S(1)} %add.54), channel_id=1, source_target_pairs={{0,8},{2,10},{4,12},{6,14},{8,0},{10,2},{12,4},{14,6},{1,9},{3,11}... | collective-permute-start | bytes 1544 | tf_op jit(solution)/shard_map/ppermute | solution.py:302
  61.5 6.2 %collective-permute-start.14 = (bf16[16,4096]{1,0:T(8,128)(2,1)S(1)}, bf16[16,4096]{1,0:T(8,128)(2,1)S(1)}, u32[]{:S(2)}, u32[]{:S(2)}) collective-permute-start(bf16[16,4096]{1,0:T(8,128)(2,1)S(1)} %get-tuple-element.41), channel_id=1, source_target_pairs={{0,2},{2,0},{4,6},{6,4},{8,10},{10,8},{12,14},{14,12},{1,3},{3,1},... | collective-permute-start | bytes 393224 | tf_op jit(solution)/shard_map/ppermute | solution.py:302
  62.4 6.7 %collective-permute-start.16 = (bf16[16,4096]{1,0:T(8,128)(2,1)S(1)}, bf16[16,4096]{1,0:T(8,128)(2,1)S(1)}, u32[]{:S(2)}, u32[]{:S(2)}) collective-permute-start(bf16[16,4096]{1,0:T(8,128)(2,1)S(1)} %get-tuple-element.43), channel_id=1, source_target_pairs={{0,2},{2,0},{4,6},{6,4},{8,10},{10,8},{12,14},{14,12},{1,3},{3,1},... | collective-permute-start | bytes 393224 | tf_op jit(solution)/shard_map/ppermute | solution.py:302
  63.6 7.6 %collective-permute-start.18 = (bf16[16,4096]{1,0:T(8,128)(2,1)S(1)}, bf16[16,4096]{1,0:T(8,128)(2,1)S(1)}, u32[]{:S(2)}, u32[]{:S(2)}) collective-permute-start(bf16[16,4096]{1,0:T(8,128)(2,1)S(1)} %get-tuple-element.45), channel_id=1, source_target_pairs={{0,2},{2,0},{4,6},{6,4},{8,10},{10,8},{12,14},{14,12},{1,3},{3,1},... | collective-permute-start | bytes 393224 | tf_op jit(solution)/shard_map/ppermute | solution.py:302
  64.4 8.0 %collective-permute-start.20 = (bf16[16,4096]{1,0:T(8,128)(2,1)S(1)}, bf16[16,4096]{1,0:T(8,128)(2,1)S(1)}, u32[]{:S(2)}, u32[]{:S(2)}) collective-permute-start(bf16[16,4096]{1,0:T(8,128)(2,1)S(1)} %get-tuple-element.47), channel_id=1, source_target_pairs={{0,2},{2,0},{4,6},{6,4},{8,10},{10,8},{12,14},{14,12},{1,3},{3,1},... | collective-permute-start | bytes 393224 | tf_op jit(solution)/shard_map/ppermute | solution.py:302
  67.7 5.9 %collective-permute-start.15 = (bf16[16,4096]{1,0:T(8,128)(2,1)S(1)}, bf16[16,4096]{1,0:T(8,128)(2,1)S(1)}, u32[]{:S(2)}, u32[]{:S(2)}) collective-permute-start(bf16[16,4096]{1,0:T(8,128)(2,1)S(1)} %add_convert_fusion.3), channel_id=1, source_target_pairs={{0,4},{2,6},{4,0},{6,2},{8,12},{10,14},{12,8},{14,10},{1,5},{3,7},... | collective-permute-start | bytes 393224 | tf_op jit(solution)/shard_map/ppermute | solution.py:302
  69.1 6.9 %collective-permute-start.17 = (bf16[16,4096]{1,0:T(8,128)(2,1)S(1)}, bf16[16,4096]{1,0:T(8,128)(2,1)S(1)}, u32[]{:S(2)}, u32[]{:S(2)}) collective-permute-start(bf16[16,4096]{1,0:T(8,128)(2,1)S(1)} %add_convert_fusion.2), channel_id=1, source_target_pairs={{0,12},{2,14},{4,8},{6,10},{8,4},{10,6},{12,0},{14,2},{1,13},{3,15... | collective-permute-start | bytes 393224 | tf_op jit(solution)/shard_map/ppermute | solution.py:302
  71.2 7.8 %collective-permute-start.19 = (bf16[16,4096]{1,0:T(8,128)(2,1)S(1)}, bf16[16,4096]{1,0:T(8,128)(2,1)S(1)}, u32[]{:S(2)}, u32[]{:S(2)}) collective-permute-start(bf16[16,4096]{1,0:T(8,128)(2,1)S(1)} %add_convert_fusion.1), channel_id=1, source_target_pairs={{0,8},{2,10},{4,12},{6,14},{8,0},{10,2},{12,4},{14,6},{1,9},{3,11}... | collective-permute-start | bytes 393224 | tf_op jit(solution)/shard_map/ppermute | solution.py:302
  79.7 1.9 %collective-permute-start.21 = (f32[16,4096]{1,0:T(8,128)S(1)}, f32[16,4096]{1,0:T(8,128)S(1)}, u32[]{:S(2)}, u32[]{:S(2)}) collective-permute-start(f32[16,4096]{1,0:T(8,128)S(1)} %get-tuple-element.50), channel_id=1, source_target_pairs={{0,16},{16,0},{1,17},{17,1},{2,18},{18,2},{3,19},{19,3},{4,20},{20... | collective-permute-start | bytes 786440 | tf_op jit(solution)/shard_map/ppermute | solution.py:302
  79.7 3.9 %collective-permute-start.23 = (bf16[128,4096]{1,0:T(8,128)(2,1)S(1)}, bf16[128,4096]{1,0:T(8,128)(2,1)S(1)}, u32[]{:S(2)}, u32[]{:S(2)}) collective-permute-start(bf16[128,4096]{1,0:T(8,128)(2,1)S(1)} %get-tuple-element.48.h0_ref), channel_id=1, source_target_pairs={{0,16},{16,0},{1,17},{17,1},{2,18},{18,2},{3,19},{19,3},{4,20},{20... | collective-permute-start | bytes 3145736 | tf_op jit(solution)/shard_map/ppermute | solution.py:302
  81.5 2.1 %collective-permute-start.22 = (bf16[128,2304]{1,0:T(8,128)(2,1)S(1)}, bf16[128,2304]{1,0:T(8,128)(2,1)S(1)}, u32[]{:S(2)}, u32[]{:S(2)}) collective-permute-start(bf16[128,2304]{1,0:T(8,128)(2,1)S(1)} %grads.1.g0_ref), channel_id=1, source_target_pairs={{0,16},{16,0},{1,17},{17,1},{2,18},{18,2},{3,19},{19,3},{4,20},{20... | collective-permute-start | bytes 1769480 | tf_op jit(solution)/shard_map/ppermute | solution.py:302
  (2 other events, 16.2 us)

commit v3 on v2

--- a/solution.py
+++ b/solution.py
@@ -13,6 +13,7 @@
 f32 = jnp.float32
 f16 = jnp.float16
 MIB = 2**20
+STAGE_LIMIT = 42
 
 
 def params(n, limit=12):
@@ -33,21 +34,22 @@
     return pl.BlockSpec(memory_space=pltpu.VMEM)
 
 
-def stage_kernel(ids_ref, u_ref, o_ref, sem):
-    copy = pltpu.make_async_copy(u_ref, o_ref, sem)
+def stage_kernel(start, ids_ref, u_ref, o_ref, sem):
+    copy = pltpu.make_async_copy(u_ref.at[pl.ds(start, o_ref.shape[0])], o_ref, sem)
     copy.start()
     copy.wait()
 
 
-def stage_call(ids, unembed):
-    return pl.pallas_call(
-        stage_kernel,
+def stage_call(ids, unembed, start, count):
+    shape = (count, unembed.shape[1])
+    return pl.pallas_call(
+        functools.partial(stage_kernel, start),
         in_specs=[smem(), pl.BlockSpec(memory_space=pltpu.HBM)],
         out_specs=vmem(),
-        out_shape=jax.ShapeDtypeStruct(unembed.shape, unembed.dtype),
+        out_shape=jax.ShapeDtypeStruct(shape, unembed.dtype),
         scratch_shapes=[pltpu.SemaphoreType.DMA],
-        compiler_params=params(0, 28),
-        cost_estimate=cost(unembed.size, 4 * unembed.size),
+        compiler_params=params(0, STAGE_LIMIT),
+        cost_estimate=cost(count * shape[1], 4 * count * shape[1]),
         name="stage",
     )(ids, unembed)
 
@@ -59,15 +61,13 @@
         at = pl.multiple_of((ids_ref[0] ^ k) * rows, rows)
         h_ref[pl.ds(at, rows), :] = parts[k][...]
     ht_ref[...] = h_ref[...].T
-    count = o_ref.shape[1]
-    o_ref[...] = jnp.dot(u_ref[:count, :], ht_ref[...], preferred_element_type=f32).T
+    u = u_ref[: o_ref.shape[1], :]
+    o_ref[...] = jnp.dot(u, ht_ref[...], preferred_element_type=f32).T
 
 
 def next_kernel(start, ht_ref, u_ref, o_ref):
-    count = o_ref.shape[1]
-    o_ref[...] = jnp.dot(
-        u_ref[start : start + count, :], ht_ref[...], preferred_element_type=f32
-    ).T
+    u = u_ref[start : start + o_ref.shape[1], :]
+    o_ref[...] = jnp.dot(u, ht_ref[...], preferred_element_type=f32).T
 
 
 def first_call(ids, pieces, unembed, count):
@@ -157,39 +157,38 @@
     )(ids, s, targets, *so_far)
 
 
-def rows_kernel(start, block, count, *refs):
-    qs, (u_ref, o_ref, q_ref) = refs[:count], refs[count:]
-
-    @pl.when(pl.program_id(0) == 0)
-    def _():
-        at = 0
-        for q in qs:
-            q_ref[:, at : at + q.shape[1]] = q[...]
-            at += q.shape[1]
-
-    cols = pl.ds(pl.multiple_of(start + pl.program_id(0) * block, block), block)
-    o_ref[...] = jnp.dot(q_ref[...], u_ref[:, cols], preferred_element_type=f32)
-
-
-def rows_call(qs, unembed, start, width, block):
-    rows = unembed.shape[0]
+def rows_kernel(block, first, *refs):
+    *q_refs, u_ref, o_ref = refs
+    step = pl.program_id(0) * block
+    cols = pl.ds(pl.multiple_of(first + step, block), block)
+    total, row = None, 0
+    for q_ref in q_refs:
+        count = q_ref.shape[1]
+        part = jnp.dot(q_ref[...], u_ref[row : row + count, cols], preferred_element_type=f32)
+        total = part if total is None else total + part
+        row += count
+    o_ref[...] = total
+
+
+def rows_call(qs, unembed, first, width, block):
     two = qs[0].shape[0]
-    return pl.pallas_call(
-        functools.partial(rows_kernel, start, block, len(qs)),
+    rows = sum(q.shape[1] for q in qs)
+    return pl.pallas_call(
+        functools.partial(rows_kernel, block, first),
         grid=(width // block,),
         in_specs=[vmem()] * (len(qs) + 1),
         out_specs=pl.BlockSpec((two, block), lambda i: (0, i)),
         out_shape=jax.ShapeDtypeStruct((two, width), f32),
-        scratch_shapes=[pltpu.VMEM((two, rows), bf16)],
         compiler_params=params(1),
         cost_estimate=cost(2 * two * rows * width, 2 * rows * width),
         name="rows",
     )(*qs, unembed)
 
 
-def norm_kernel(n, parts, ids_ref, tot_ref, stat_ref, lg_ref, *refs):
-    outs = refs[parts : parts + n]
-    sc, wc = refs[parts + n :]
+def norm_kernel(n, groups, ids_ref, tot_ref, stat_ref, lg_ref, *refs):
+    early, late, refs = refs[:2], refs[2:4], refs[4:]
+    keep, send = refs[: n // 2], refs[n // 2 : n // 2 + len(groups)]
+    sc, wc = refs[-2:]
     tokens = tot_ref.shape[1]
     rows = tokens // n
     total = tot_ref[...]
@@ -197,27 +196,36 @@
     sc[...] = jnp.broadcast_to(lg / total, (tokens, tokens)).T
     weight = lg * (stat_ref[:1, :] / total - stat_ref[1:2, :])
     wc[...] = jnp.broadcast_to(weight, (tokens, tokens)).T
-    for k in range(n):
+
+    def block(k, ref, row):
         at = pl.multiple_of((ids_ref[0] ^ k) * rows, rows)
-        a_s = sc[pl.ds(at, rows), :1]
-        a_w = wc[pl.ds(at, rows), :1]
+        scale = sc[pl.ds(at, rows), :1]
+        weight = wc[pl.ds(at, rows), :1]
         col = 0
-        for p in range(parts):
-            width = refs[p].shape[1]
-            a = refs[p][pl.ds(at, rows), :]
-            u = refs[p][pl.ds(tokens + at, rows), :]
-            outs[k][:, col : col + width] = (a_s * a + a_w * u).astype(bf16)
-            col += width
-
-
-def norm_call(n, ids, total, stats, loss_grad, sums):
+        for x, y in zip(early, late):
+            cols = slice(col, col + x.shape[1])
+            a = x[pl.ds(at, rows), :] + y[pl.ds(at, rows), :]
+            u = x[pl.ds(tokens + at, rows), :] + y[pl.ds(tokens + at, rows), :]
+            ref[row : row + rows, cols] = (scale * a + weight * u).astype(ref.dtype)
+            col += x.shape[1]
+
+    for ref, group in zip(send, groups):
+        for i, k in enumerate(group):
+            block(k + 1, ref, i * rows)
+    for k in range(0, n, 2):
+        block(k, keep[k // 2], 0)
+
+
+def norm_call(n, groups, ids, total, stats, loss_grad, sums):
     tokens = total.shape[1]
-    width = sum(a.shape[1] for a in sums)
-    return pl.pallas_call(
-        functools.partial(norm_kernel, n, len(sums)),
+    width = 2 * sums[0].shape[1]
+    rows = tokens // n
+    return pl.pallas_call(
+        functools.partial(norm_kernel, n, groups),
         in_specs=[smem()] + [vmem()] * (3 + len(sums)),
-        out_specs=[vmem()] * n,
-        out_shape=[jax.ShapeDtypeStruct((tokens // n, width), bf16)] * n,
+        out_specs=[vmem()] * (n // 2 + len(groups)),
+        out_shape=[jax.ShapeDtypeStruct((rows, width), f32)] * (n // 2)
+        + [jax.ShapeDtypeStruct((rows * len(g), width), bf16) for g in groups],
         scratch_shapes=[pltpu.VMEM((tokens, tokens), f32)] * 2,
         compiler_params=params(0),
         cost_estimate=cost(4 * tokens * width, 10 * tokens * width),
@@ -255,44 +263,68 @@
     )(ids, targets, total, loss_grad, *scores)
 
 
-def weight_kernel(ids_ref, g0_ref, g1_ref, h0_ref, h1_ref, *refs):
-    o_ref, g_ref, h_ref = refs[-3:]
-    tokens = h0_ref.shape[0]
+def weight_kernel(first, start, block, ids_ref, *refs):
+    g0_ref, g1_ref, refs = refs[0], refs[1], refs[2:]
+    if first:
+        h0_ref, h1_ref, o_ref, h_ref, g_ref, r_ref, sem = refs
+    else:
+        h_ref, _, o_ref, g_ref, r_ref, sem = refs
+    tokens, count = g0_ref.shape[0], g_ref.shape[1]
     mine = pl.multiple_of(ids_ref[1] * tokens, tokens)
     other = pl.multiple_of((1 - ids_ref[1]) * tokens, tokens)
-
-    @pl.when(pl.program_id(0) == 0)
-    def _():
+    if first:
         h_ref[pl.ds(mine, tokens), :] = h0_ref[...]
         h_ref[pl.ds(other, tokens), :] = h1_ref[...]
-
-    g_ref[pl.ds(mine, tokens), :] = g0_ref[...]
-    g_ref[pl.ds(other, tokens), :] = g1_ref[...]
-    o_ref[...] = lax.dot_general(
-        g_ref[...], h_ref[...], (((0,), (0,)), ((), ())), preferred_element_type=f32
-    )
-
-
-def weight_call(ids, g0, g1, h0, h1, start, count, block, into):
+    g_ref[pl.ds(mine, tokens), :] = g0_ref[:, start : start + count]
+    g_ref[pl.ds(other, tokens), :] = g1_ref[:, start : start + count]
+    turned = g_ref[...].T
+    copies = []
+    part = r_ref.shape[2]
+    across = h_ref.shape[1] // part
+    for i in range(r_ref.shape[0]):
+        row, col = i // across * block, i % across * part
+        r_ref[i] = jnp.dot(
+            turned[row : row + block, :],
+            h_ref[:, col : col + part],
+            preferred_element_type=f32,
+        )
+        copies.append(
+            pltpu.make_async_copy(
+                r_ref.at[i],
+                o_ref.at[pl.ds(start + row, block), pl.ds(col, part)],
+                sem.at[i],
+            )
+        )
+        copies[-1].start()
+    for copy in copies:
+        copy.wait()
+
+
+def weight_call(ids, g0, g1, hs, start, count, block, into):
     tokens, rows = g0.shape
-    width = h0.shape[1]
-    g_spec = pl.BlockSpec((tokens, block), lambda i: (0, start // block + i))
-    operands = [ids, g0, g1, h0, h1]
-    specs = [smem(), g_spec, g_spec, vmem(), vmem()]
-    alias = {}
-    if into is not None:
-        operands.append(into)
-        specs.append(pl.BlockSpec(memory_space=pl.ANY))
-        alias = {5: 0}
-    return pl.pallas_call(
-        weight_kernel,
-        grid=(count // block,),
+    width = hs[0].shape[1]
+    hbm = pl.BlockSpec(memory_space=pltpu.HBM)
+    first = into is None
+    operands = [ids, g0, g1, *hs] + ([] if first else [into])
+    specs = [smem()] + [vmem()] * (2 + len(hs)) + ([] if first else [hbm])
+    out_specs = [hbm] + ([vmem()] if first else [])
+    out_shape = [jax.ShapeDtypeStruct((rows, width), f32)]
+    if first:
+        out_shape.append(jax.ShapeDtypeStruct((2 * tokens, width), bf16))
+    across = 4
+    steps = count // block * across
+    return pl.pallas_call(
+        functools.partial(weight_kernel, first, start, block),
         in_specs=specs,
-        out_specs=pl.BlockSpec((block, width), lambda i: (start // block + i, 0)),
-        out_shape=jax.ShapeDtypeStruct((rows, width), f32),
-        scratch_shapes=[pltpu.VMEM((2 * tokens, block), bf16), pltpu.VMEM((2 * tokens, width), bf16)],
-        input_output_aliases=alias,
-        compiler_params=params(1, 24),
+        out_specs=out_specs,
+        out_shape=out_shape,
+        scratch_shapes=[
+            pltpu.VMEM((2 * tokens, count), bf16),
+            pltpu.VMEM((steps, block, width // across), f32),
+            pltpu.SemaphoreType.DMA((steps,)),
+        ],
+        input_output_aliases={} if first else {4: 0},
+        compiler_params=params(0, 32),
         cost_estimate=cost(4 * tokens * count * width, 4 * count * width),
         name="weight",
     )(*operands)
@@ -311,7 +343,7 @@
 
 def thirds(total, unit):
     tiles = total // unit
-    sizes = [(tiles + 2) // 3, (tiles + 1) // 3, tiles // 3]
+    sizes = [tiles // 3, tiles - tiles // 3 - tiles // 4, tiles // 4]
     starts = [sum(sizes[:i]) for i in range(3)]
     return [(a * unit, c * unit) for a, c in zip(starts, sizes)]
 
@@ -321,7 +353,7 @@
     seq_index = lax.axis_index("seq")
     ids = jnp.stack([seq_index, lax.axis_index("head"), seq_index * block_rows]).astype(jnp.int32)
     hidden = (trunk.astype(f32) + branch[0].astype(f32)).astype(bf16)
-    far = [k for k in (2, 6, 4) if k < n]
+    far = [2, 6, 4]
 
     pieces = [None] * n
     pieces[0] = hidden
@@ -330,45 +362,55 @@
     for k in [0] + far:
         pieces[k + 1] = swap(pieces[k], "seq", 1, n)
 
-    unembed = stage_call(ids, unembed)
     chunks = split(block_rows, 256)
-    scores, qs, so_far = [], [], []
+    late = chunks[2][0]
+    staged = []
+    for start, count in ((0, late), (late, block_rows - late)):
+        staged.append(stage_call(ids, unembed, start, count))
+    scores = []
     for c, (start, count) in enumerate(chunks):
         if c == 0:
-            s, all_hidden, turned = first_call(ids, pieces, unembed, count)
+            s, all_hidden, turned = first_call(ids, pieces, staged[0], count)
         else:
-            s = next_call(turned, unembed, start, count)
+            s = next_call(turned, staged[c // 2], start - c // 2 * late, count)
         s = s.astype(f16)
         scores.append(s.astype(f32) + swap(s, "mp", 1, 2).astype(f32))
     other_hidden = swap(all_hidden, "head", 1, 2)
+    so_far, qs = [], []
     for c, (start, count) in enumerate(chunks):
         q, *so_far = numer_call(start, ids, scores[c], targets, so_far)
         qs.append(q)
+    half = width // 2
+    sums = []
+    for r, group in enumerate((qs[:2], qs[2:])):
+        for p in range(2):
+            sums.append(rows_call(group, staged[r], p * half, half, 512))
     total, stats = so_far
-
     for i in range(n.bit_length() - 1):
         total = total + swap(total, "seq", 1 << i, n)
-    sums = []
-    for start, count in thirds(width, 512):
-        sums.append(rows_call(qs, unembed, start, count, 512))
-    blocks = norm_call(n, ids, total, stats, loss_grad, sums)
-
+
+    groups = ((4, 6), (2, 0))
+    blocks = norm_call(n, groups, ids, total, stats, loss_grad, sums)
+    keep, send = blocks[: n // 2], blocks[n // 2 :]
+    rows = hidden.shape[0]
     got = []
-    for k in far + [0]:
-        theirs = swap(blocks[k + 1], "seq", 1, n)
-        both = blocks[k].astype(f32) + theirs.astype(f32)
-        if k:
-            both = swap(both.astype(bf16), "seq", k, n).astype(f32)
-        got.append(both)
+    for i, group in enumerate(groups):
+        theirs = swap(send[i], "seq", 1, n)
+        for j, k in enumerate(group):
+            both = keep[k // 2] + theirs[j * rows : (j + 1) * rows].astype(f32)
+            if k:
+                both = swap(both.astype(bf16), "seq", k, n).astype(f32)
+            got.append(both)
     row_grad = functools.reduce(lambda a, b: a + b, got)
 
     g = grads_call(ids, scores, targets, total, loss_grad)
     g_other = swap(g, "head", 1, 2)
-    d_unembed = None
-    for start, count in thirds(block_rows, 256):
-        d_unembed = weight_call(
-            ids, g, g_other, all_hidden, other_hidden, start, count, 256, d_unembed
-        )
+    d_unembed, hs = None, [all_hidden, other_hidden]
+    for p, (start, count) in enumerate(thirds(block_rows, 256)):
+        out = weight_call(ids, g, g_other, hs, start, count, 256, d_unembed)
+        d_unembed = out[0]
+        if p == 0:
+            hs = out[1:]
 
     d_trunk = row_grad + swap(row_grad, "head", 1, 2)
     return (row_grad.astype(bf16)[None], d_trunk.astype(bf16), d_unembed)

time: 103 us -> 102 us (level)
  starting transfers between devices: 28.2 us -> 24.8 us
  Pallas kernels: 44.8 us -> 46.2 us
  waiting for transfers between devices: 25.6 us -> 26.9 us
    ppermute x24 -> x22, starting transfers between devices: 28.2 us -> 24.8 us  [swap(): return lax.ppermute(x, axis, [(i, i ^ mask) for i in range(size)])]
    ppermute x24 -> x22, waiting for transfers between devices: 25.6 us -> 26.9 us  [swap(): return lax.ppermute(x, axis, [(i, i ^ mask) for i in range(size)])]
    pallas_call x8 -> x10, Pallas kernels: 33.7 us -> 35 us  [the longest x3 16.8 us: weight_call(): pl.pallas_call(functools.partial(weight_kernel, first, start, block), in_...]
  transfers between devices with their start and end apart: 24 -> 22, of which waited for: 13 -> 10; matrix products, arithmetic and copies ran while one was open for 1% -> 1% of each run, Pallas kernels for 18% -> 24%
where the time goes in v3:
time: 102 us
  Pallas kernels  46.2 us (45%)
  waiting for transfers between devices  26.9 us (26%)
  starting transfers between devices  24.8 us (24%)
  other arithmetic  2.84 us (3%)
  between operations  1.08 us (1%)
    ppermute x22, waiting for transfers between devices, swap(): return lax.ppermute(x, axis, [(i, i ^ mask) for i in range(size)])  26.9 us
    ppermute x22, starting transfers between devices, swap(): return lax.ppermute(x, axis, [(i, i ^ mask) for i in range(size)])  24.8 us
    pallas_call x3, Pallas kernels, weight_call(): pl.pallas_call(functools.partial(weight_kernel, first, start, block), in_...  16.8 us
    pallas_call x2, Pallas kernels, stage_call(): pl.pallas_call(functools.partial(stage_kernel, start), in_specs=[smem(),...  8.46 us
    pallas_call x4, Pallas kernels, rows_call(): pl.pallas_call(functools.partial(rows_kernel, block, first), grid=(width...  8.39 us
    pallas_call x3, Pallas kernels, next_call(): pl.pallas_call(functools.partial(next_kernel, start), in_specs=[vmem()] *...  5.02 us
    pallas_call x4, Pallas kernels, numer_call(): pl.pallas_call(functools.partial(numer_kernel, start), in_specs=[smem()]...  3.41 us
  transfers between devices with their start and end apart: 22, of which 10 were waited for; matrix products, arithmetic and copies ran while one was open for 1% of the time, Pallas kernels for 24%

profile of v3, /device:TPU:0, one launch (start us, length us, event | category | flops | bytes accessed | tf_op | source)
XLA Modules:
  0.0 101.8 jit_solution(6224780542458515066)
XLA Ops:
  1.6 5.1 %collective-permute-start.5 = (bf16[16,4096]{1,0:T(8,128)(2,1)S(1)}, bf16[16,4096]{1,0:T(8,128)(2,1)S(1)}, u32[]{:S(2)}, u32[]{:S(2)}) collective-permute-start(bf16[16,4096]{1,0:T(8,128)(2,1)S(1)} %fusion.refs_0_), channel_id=1, source_target_pairs={{0,12},{2,14},{4,8},{6,10},{8,4},{10,6},{12,0},{14,2},{1,13},{3,15... | collective-permute-start | bytes 393224 | tf_op jit(solution)/shard_map/ppermute | solution.py:334
  7.4 1.7 %collective-permute-start = (bf16[16,4096]{1,0:T(8,128)(2,1)S(1)}, bf16[16,4096]{1,0:T(8,128)(2,1)S(1)}, u32[]{:S(2)}, u32[]{:S(2)}) collective-permute-start(bf16[16,4096]{1,0:T(8,128)(2,1)S(1)} %fusion.refs_0_), channel_id=1, source_target_pairs={{0,2},{2,0},{4,6},{6,4},{8,10},{10,8},{12,14},{14,12},{1,3},{3,1},... | collective-permute-start | bytes 393224 | tf_op jit(solution)/shard_map/ppermute | solution.py:334
  9.1 2.1 %collective-permute-done.5.refs_6_ = bf16[16,4096]{1,0:T(8,128)(2,1)S(1)} collective-permute-done((bf16[16,4096]{1,0:T(8,128)(2,1)S(1)}, bf16[16,4096]{1,0:T(8,128)(2,1)S(1)}, u32[]{:S(2)}, u32[]{:S(2)}) %collective-permute-start.5) | collective-permute-done | bytes 131104 | tf_op jit(solution)/shard_map/ppermute | solution.py:334
  11.2 1.7 %collective-permute-start.6 = (bf16[16,4096]{1,0:T(8,128)(2,1)S(1)}, bf16[16,4096]{1,0:T(8,128)(2,1)S(1)}, u32[]{:S(2)}, u32[]{:S(2)}) collective-permute-start(bf16[16,4096]{1,0:T(8,128)(2,1)S(1)} %collective-permute-done.5.refs_6_), channel_id=1, source_target_pairs={{0,2},{2,0},{4,6},{6,4},{8,10},{10,8},{12,14},{14,12},{1,3},{3,1},... | collective-permute-start | bytes 393224 | tf_op jit(solution)/shard_map/ppermute | solution.py:334
  12.9 4.9 %collective-permute-done.3.refs_4_ = bf16[16,4096]{1,0:T(8,128)(2,1)S(1)} collective-permute-done((bf16[16,4096]{1,0:T(8,128)(2,1)S(1)}, bf16[16,4096]{1,0:T(8,128)(2,1)S(1)}, u32[]{:S(2)}, u32[]{:S(2)}) %collective-permute-start.3) | collective-permute-done | bytes 131104 | tf_op jit(solution)/shard_map/ppermute | solution.py:334
  20.0 3.9 %stage.2.refs_8_.u_ref.refs_2_ = bf16[1024,4096]{1,0:T(8,128)(2,1)S(1)} custom-call(s32[3]{0:T(128)S(1)} %pad_add_fusion.ids_ref, bf16[2304,4096]{1,0:T(8,128)(2,1)} %u_ref.3), custom_call_target="tpu_custom_call" | custom-call | flops 4194304 | bytes 16777216 | tf_op jit(solution)/shard_map/stage/pallas_call | solution.py:45
  23.9 4.5 %stage.3.u_ref.refs_2_ = bf16[1280,4096]{1,0:T(8,128)(2,1)S(1)} custom-call(s32[3]{0:T(128)S(1)} %pad_add_fusion.ids_ref, bf16[2304,4096]{1,0:T(8,128)(2,1)} %u_ref.3), custom_call_target="tpu_custom_call" | custom-call | flops 5242880 | bytes 20971520 | tf_op jit(solution)/shard_map/stage/pallas_call | solution.py:45
  30.0 1.6 %collective-permute-start.10 = (f16[128,256]{1,0:T(8,128)(2,1)S(1)}, f16[128,256]{1,0:T(8,128)(2,1)S(1)}, u32[]{:S(2)}, u32[]{:S(2)}) collective-permute-start(f16[128,256]{1,0:T(8,128)(2,1)S(1)} %convert_element_type.97), channel_id=1, source_target_pairs={{0,1},{1,0},{2,3},{3,2},{4,5},{5,4},{6,7},{7,6},{8,9},{9,8},{10,11... | collective-permute-start | bytes 196616 | tf_op jit(solution)/shard_map/ppermute | solution.py:334
  31.6 1.8 %scores_next.5 = f32[128,768]{1,0:T(8,128)S(1)} custom-call(bf16[4096,128]{1,0:T(8,128)(2,1)S(1)} %get-tuple-element.26.ht_ref, bf16[1024,4096]{1,0:T(8,128)(2,1)S(1)} %stage.2.refs_8_.u_ref.refs_2_), custom_call_target="tpu_custom_call" | custom-call | flops 805306368 | bytes 6291456 | tf_op jit(solution)/shard_map/scores_next/pallas_call | solution.py:93
  35.4 1.6 %collective-permute-start.7 = (f16[128,512]{1,0:T(8,128)(2,1)S(1)}, f16[128,512]{1,0:T(8,128)(2,1)S(1)}, u32[]{:S(2)}, u32[]{:S(2)}) collective-permute-start(f16[128,512]{1,0:T(8,128)(2,1)S(1)} %convert_element_type.88), channel_id=1, source_target_pairs={{0,1},{1,0},{2,3},{3,2},{4,5},{5,4},{6,7},{7,6},{8,9},{9,8},{10,11... | collective-permute-start | bytes 393224 | tf_op jit(solution)/shard_map/ppermute | solution.py:334
  37.0 1.8 %scores_next.4 = f32[128,768]{1,0:T(8,128)S(1)} custom-call(bf16[4096,128]{1,0:T(8,128)(2,1)S(1)} %get-tuple-element.26.ht_ref, bf16[1280,4096]{1,0:T(8,128)(2,1)S(1)} %stage.3.u_ref.refs_2_), custom_call_target="tpu_custom_call" | custom-call | flops 805306368 | bytes 6291456 | tf_op jit(solution)/shard_map/scores_next/pallas_call | solution.py:93
  40.3 3.3 %collective-permute-done.7 = f16[128,512]{1,0:T(8,128)(2,1)S(1)} collective-permute-done((f16[128,512]{1,0:T(8,128)(2,1)S(1)}, f16[128,512]{1,0:T(8,128)(2,1)S(1)}, u32[]{:S(2)}, u32[]{:S(2)}) %collective-permute-start.7) | collective-permute-done | bytes 131104 | tf_op jit(solution)/shard_map/ppermute | solution.py:334
  47.4 1.6 %collective-permute-start.11 = (f32[1,128]{1,0:T(1,128)S(1)}, f32[1,128]{1,0:T(1,128)S(1)}, u32[]{:S(2)}, u32[]{:S(2)}) collective-permute-start(f32[1,128]{1,0:T(1,128)S(1)} %get-tuple-element.34), channel_id=1, source_target_pairs={{0,2},{2,0},{4,6},{6,4},{8,10},{10,8},{12,14},{14,12},{1,3},{3,1},... | collective-permute-start | bytes 1544 | tf_op jit(solution)/shard_map/ppermute | solution.py:334
  49.0 2.2 %rows.7.refs_3_ = f32[256,2048]{1,0:T(8,128)S(1)} custom-call(bf16[256,768]{1,0:T(8,128)(2,1)S(1)} %get-tuple-element.38.refs_0_, bf16[256,512]{1,0:T(8,128)(2,1)S(1)} %get-tuple-element.39.refs_1_, bf16[1280,4096]{1,0:T(8,128)(2,1)S(1)} %stage.3.u_ref.refs_2_), custom_call_target="tpu_custom_call" | custom-call | flops 1342177280 | bytes 5242880 | tf_op jit(solution)/shard_map/rows/pallas_call | solution.py:176
  51.3 2.3 %rows.6.refs_2_ = f32[256,2048]{1,0:T(8,128)S(1)} custom-call(bf16[256,768]{1,0:T(8,128)(2,1)S(1)} %get-tuple-element.38.refs_0_, bf16[256,512]{1,0:T(8,128)(2,1)S(1)} %get-tuple-element.39.refs_1_, bf16[1280,4096]{1,0:T(8,128)(2,1)S(1)} %stage.3.u_ref.refs_2_), custom_call_target="tpu_custom_call" | custom-call | flops 1342177280 | bytes 5242880 | tf_op jit(solution)/shard_map/rows/pallas_call | solution.py:176
  53.6 2.0 %rows.5.refs_1_ = f32[256,2048]{1,0:T(8,128)S(1)} custom-call(bf16[256,256]{1,0:T(8,128)(2,1)S(1)} %get-tuple-element.36.refs_0_, bf16[256,768]{1,0:T(8,128)(2,1)S(1)} %get-tuple-element.37.refs_1_, bf16[1024,4096]{1,0:T(8,128)(2,1)S(1)} %stage.2.refs_8_.u_ref.refs_2_), custom_call_target="tpu_custom_call" | custom-call | flops 1073741824 | bytes 4194304 | tf_op jit(solution)/shard_map/rows/pallas_call | solution.py:176
  55.6 1.6 %collective-permute-done.12 = f32[1,128]{1,0:T(1,128)S(1)} collective-permute-done((f32[1,128]{1,0:T(1,128)S(1)}, f32[1,128]{1,0:T(1,128)S(1)}, u32[]{:S(2)}, u32[]{:S(2)}) %collective-permute-start.12) | collective-permute-done | bytes 544 | tf_op jit(solution)/shard_map/ppermute | solution.py:334
  58.6 1.9 %rows.4.refs_0_ = f32[256,2048]{1,0:T(8,128)S(1)} custom-call(bf16[256,256]{1,0:T(8,128)(2,1)S(1)} %get-tuple-element.36.refs_0_, bf16[256,768]{1,0:T(8,128)(2,1)S(1)} %get-tuple-element.37.refs_1_, bf16[1024,4096]{1,0:T(8,128)(2,1)S(1)} %stage.2.refs_8_.u_ref.refs_2_), custom_call_target="tpu_custom_call" | custom-call | flops 1073741824 | bytes 4194304 | tf_op jit(solution)/shard_map/rows/pallas_call | solution.py:176
  65.1 4.9 %collective-permute-done.14 = bf16[32,4096]{1,0:T(8,128)(2,1)S(1)} collective-permute-done((bf16[32,4096]{1,0:T(8,128)(2,1)S(1)}, bf16[32,4096]{1,0:T(8,128)(2,1)S(1)}, u32[]{:S(2)}, u32[]{:S(2)}) %collective-permute-start.14) | collective-permute-done | bytes 262176 | tf_op jit(solution)/shard_map/ppermute | solution.py:334
  70.1 1.7 %collective-permute-start.15 = (bf16[16,4096]{1,0:T(8,128)(2,1)S(1)}, bf16[16,4096]{1,0:T(8,128)(2,1)S(1)}, u32[]{:S(2)}, u32[]{:S(2)}) collective-permute-start(bf16[16,4096]{1,0:T(8,128)(2,1)S(1)} %get-tuple-element.51), channel_id=1, source_target_pairs={{0,8},{2,10},{4,12},{6,14},{8,0},{10,2},{12,4},{14,6},{1,9},{3,11}... | collective-permute-start | bytes 393224 | tf_op jit(solution)/shard_map/ppermute | solution.py:334
  73.7 5.2 %collective-permute-done.15 = bf16[16,4096]{1,0:T(8,128)(2,1)S(1)} collective-permute-done((bf16[16,4096]{1,0:T(8,128)(2,1)S(1)}, bf16[16,4096]{1,0:T(8,128)(2,1)S(1)}, u32[]{:S(2)}, u32[]{:S(2)}) %collective-permute-start.15) | collective-permute-done | bytes 131104 | tf_op jit(solution)/shard_map/ppermute | solution.py:334
  84.8 5.7 %weight.3 = (f32[2304,4096]{1,0:T(8,128)}, bf16[256,4096]{1,0:T(8,128)(2,1)S(1)}) custom-call(s32[3]{0:T(128)S(1)} %pad_add_fusion.ids_ref, bf16[128,2304]{1,0:T(8,128)(2,1)S(1)} %grads.1.refs_0_, bf16[128,2304]{1,0:T(8,128)(2,1)S(1)} %collective-permute-done.20.refs_1_, bf16[128,4096]{1,0:T(8,128)(2,1)S(1)} %get-tuple-element.46.refs_2_, ...), custom_call_target="tpu_custom_call" | custom-call | flops 1610612736 | bytes 12582912 | tf_op jit(solution)/shard_map/weight/pallas_call | solution.py:316
  90.5 6.9 %weight.4.refs_3_ = f32[2304,4096]{1,0:T(8,128)} custom-call(s32[3]{0:T(128)S(1)} %pad_add_fusion.ids_ref, bf16[128,2304]{1,0:T(8,128)(2,1)S(1)} %grads.1.refs_0_, bf16[128,2304]{1,0:T(8,128)(2,1)S(1)} %collective-permute-done.20.refs_1_, bf16[256,4096]{1,0:T(8,128)(2,1)S(1)} %get-tuple-element.47.refs_2_, ...), custom_call_target="tpu_custom_call", output_to_operand_aliasing={{}: (4, {})} | custom-call | flops 2147483648 | bytes 16777216 | tf_op jit(solution)/shard_map/weight/pallas_call | solution.py:316
  97.4 4.3 %weight.5 = f32[2304,4096]{1,0:T(8,128)} custom-call(s32[3]{0:T(128)S(1)} %pad_add_fusion.ids_ref, bf16[128,2304]{1,0:T(8,128)(2,1)S(1)} %grads.1.refs_0_, bf16[128,2304]{1,0:T(8,128)(2,1)S(1)} %collective-permute-done.20.refs_1_, bf16[256,4096]{1,0:T(8,128)(2,1)S(1)} %get-tuple-element.47.refs_2_, ...), custom_call_target="tpu_custom_call", output_to_operand_aliasing={{}: (4, {})} | custom-call | flops 1073741824 | bytes 8388608 | tf_op jit(solution)/shard_map/weight/pallas_call | solution.py:316
  (60 shorter events, 26.5 us)
Async XLA Ops:
  1.6 9.6 %collective-permute-start.5 = (bf16[16,4096]{1,0:T(8,128)(2,1)S(1)}, bf16[16,4096]{1,0:T(8,128)(2,1)S(1)}, u32[]{:S(2)}, u32[]{:S(2)}) collective-permute-start(bf16[16,4096]{1,0:T(8,128)(2,1)S(1)} %fusion.refs_0_), channel_id=1, source_target_pairs={{0,12},{2,14},{4,8},{6,10},{8,4},{10,6},{12,0},{14,2},{1,13},{3,15... | collective-permute-start | bytes 393224 | tf_op jit(solution)/shard_map/ppermute | solution.py:334
  6.8 11.1 %collective-permute-start.3 = (bf16[16,4096]{1,0:T(8,128)(2,1)S(1)}, bf16[16,4096]{1,0:T(8,128)(2,1)S(1)}, u32[]{:S(2)}, u32[]{:S(2)}) collective-permute-start(bf16[16,4096]{1,0:T(8,128)(2,1)S(1)} %fusion.refs_0_), channel_id=1, source_target_pairs={{0,8},{2,10},{4,12},{6,14},{8,0},{10,2},{12,4},{14,6},{1,9},{3,11}... | collective-permute-start | bytes 393224 | tf_op jit(solution)/shard_map/ppermute | solution.py:334
  6.8 12.6 %collective-permute-start.1 = (bf16[16,4096]{1,0:T(8,128)(2,1)S(1)}, bf16[16,4096]{1,0:T(8,128)(2,1)S(1)}, u32[]{:S(2)}, u32[]{:S(2)}) collective-permute-start(bf16[16,4096]{1,0:T(8,128)(2,1)S(1)} %fusion.refs_0_), channel_id=1, source_target_pairs={{0,4},{2,6},{4,0},{6,2},{8,12},{10,14},{12,8},{14,10},{1,5},{3,7},... | collective-permute-start | bytes 393224 | tf_op jit(solution)/shard_map/ppermute | solution.py:334
  7.4 21.0 %collective-permute-start = (bf16[16,4096]{1,0:T(8,128)(2,1)S(1)}, bf16[16,4096]{1,0:T(8,128)(2,1)S(1)}, u32[]{:S(2)}, u32[]{:S(2)}) collective-permute-start(bf16[16,4096]{1,0:T(8,128)(2,1)S(1)} %fusion.refs_0_), channel_id=1, source_target_pairs={{0,2},{2,0},{4,6},{6,4},{8,10},{10,8},{12,14},{14,12},{1,3},{3,1},... | collective-permute-start | bytes 393224 | tf_op jit(solution)/shard_map/ppermute | solution.py:334
  11.2 17.2 %collective-permute-start.6 = (bf16[16,4096]{1,0:T(8,128)(2,1)S(1)}, bf16[16,4096]{1,0:T(8,128)(2,1)S(1)}, u32[]{:S(2)}, u32[]{:S(2)}) collective-permute-start(bf16[16,4096]{1,0:T(8,128)(2,1)S(1)} %collective-permute-done.5.refs_6_), channel_id=1, source_target_pairs={{0,2},{2,0},{4,6},{6,4},{8,10},{10,8},{12,14},{14,12},{1,3},{3,1},... | collective-permute-start | bytes 393224 | tf_op jit(solution)/shard_map/ppermute | solution.py:334
  17.9 10.6 %collective-permute-start.4 = (bf16[16,4096]{1,0:T(8,128)(2,1)S(1)}, bf16[16,4096]{1,0:T(8,128)(2,1)S(1)}, u32[]{:S(2)}, u32[]{:S(2)}) collective-permute-start(bf16[16,4096]{1,0:T(8,128)(2,1)S(1)} %collective-permute-done.3.refs_4_), channel_id=1, source_target_pairs={{0,2},{2,0},{4,6},{6,4},{8,10},{10,8},{12,14},{14,12},{1,3},{3,1},... | collective-permute-start | bytes 393224 | tf_op jit(solution)/shard_map/ppermute | solution.py:334
  19.4 9.1 %collective-permute-start.2 = (bf16[16,4096]{1,0:T(8,128)(2,1)S(1)}, bf16[16,4096]{1,0:T(8,128)(2,1)S(1)}, u32[]{:S(2)}, u32[]{:S(2)}) collective-permute-start(bf16[16,4096]{1,0:T(8,128)(2,1)S(1)} %collective-permute-done.1.refs_2_), channel_id=1, source_target_pairs={{0,2},{2,0},{4,6},{6,4},{8,10},{10,8},{12,14},{14,12},{1,3},{3,1},... | collective-permute-start | bytes 393224 | tf_op jit(solution)/shard_map/ppermute | solution.py:334
  30.0 9.4 %collective-permute-start.10 = (f16[128,256]{1,0:T(8,128)(2,1)S(1)}, f16[128,256]{1,0:T(8,128)(2,1)S(1)}, u32[]{:S(2)}, u32[]{:S(2)}) collective-permute-start(f16[128,256]{1,0:T(8,128)(2,1)S(1)} %convert_element_type.97), channel_id=1, source_target_pairs={{0,1},{1,0},{2,3},{3,2},{4,5},{5,4},{6,7},{7,6},{8,9},{9,8},{10,11... | collective-permute-start | bytes 196616 | tf_op jit(solution)/shard_map/ppermute | solution.py:334
  33.4 10.2 %collective-permute-start.9 = (f16[128,768]{1,0:T(8,128)(2,1)S(1)}, f16[128,768]{1,0:T(8,128)(2,1)S(1)}, u32[]{:S(2)}, u32[]{:S(2)}) collective-permute-start(f16[128,768]{1,0:T(8,128)(2,1)S(1)} %convert_element_type.94), channel_id=1, source_target_pairs={{0,1},{1,0},{2,3},{3,2},{4,5},{5,4},{6,7},{7,6},{8,9},{9,8},{10,11... | collective-permute-start | bytes 589832 | tf_op jit(solution)/shard_map/ppermute | solution.py:334
  35.4 4.1 %copy-start = (s32[1,128]{1,0:T(1,128)S(1)}, s32[1,128]{1,0:T(1,128)}, u32[]{:S(2)}) copy-start(s32[1,128]{1,0:T(1,128)} %t_ref.9) | copy-start | bytes 1540
  35.4 8.2 %collective-permute-start.7 = (f16[128,512]{1,0:T(8,128)(2,1)S(1)}, f16[128,512]{1,0:T(8,128)(2,1)S(1)}, u32[]{:S(2)}, u32[]{:S(2)}) collective-permute-start(f16[128,512]{1,0:T(8,128)(2,1)S(1)} %convert_element_type.88), channel_id=1, source_target_pairs={{0,1},{1,0},{2,3},{3,2},{4,5},{5,4},{6,7},{7,6},{8,9},{9,8},{10,11... | collective-permute-start | bytes 393224 | tf_op jit(solution)/shard_map/ppermute | solution.py:334
  38.8 6.8 %collective-permute-start.8 = (f16[128,768]{1,0:T(8,128)(2,1)S(1)}, f16[128,768]{1,0:T(8,128)(2,1)S(1)}, u32[]{:S(2)}, u32[]{:S(2)}) collective-permute-start(f16[128,768]{1,0:T(8,128)(2,1)S(1)} %convert_element_type.91), channel_id=1, source_target_pairs={{0,1},{1,0},{2,3},{3,2},{4,5},{5,4},{6,7},{7,6},{8,9},{9,8},{10,11... | collective-permute-start | bytes 589832 | tf_op jit(solution)/shard_map/ppermute | solution.py:334
  47.4 6.1 %collective-permute-start.11 = (f32[1,128]{1,0:T(1,128)S(1)}, f32[1,128]{1,0:T(1,128)S(1)}, u32[]{:S(2)}, u32[]{:S(2)}) collective-permute-start(f32[1,128]{1,0:T(1,128)S(1)} %get-tuple-element.34), channel_id=1, source_target_pairs={{0,2},{2,0},{4,6},{6,4},{8,10},{10,8},{12,14},{14,12},{1,3},{3,1},... | collective-permute-start | bytes 1544 | tf_op jit(solution)/shard_map/ppermute | solution.py:334
  53.5 3.6 %collective-permute-start.12 = (f32[1,128]{1,0:T(1,128)S(1)}, f32[1,128]{1,0:T(1,128)S(1)}, u32[]{:S(2)}, u32[]{:S(2)}) collective-permute-start(f32[1,128]{1,0:T(1,128)S(1)} %add.53), channel_id=1, source_target_pairs={{0,4},{2,6},{4,0},{6,2},{8,12},{10,14},{12,8},{14,10},{1,5},{3,7},... | collective-permute-start | bytes 1544 | tf_op jit(solution)/shard_map/ppermute | solution.py:334
  53.6 8.0 %copy-start.1 = (f32[1,128]{1,0:T(1,128)S(1)}, f32[1,128]{1,0:T(1,128)}, u32[]{:S(2)}) copy-start(f32[1,128]{1,0:T(1,128)} %lg_ref.3) | copy-start | bytes 1540
  57.2 4.5 %collective-permute-start.13 = (f32[1,128]{1,0:T(1,128)S(1)}, f32[1,128]{1,0:T(1,128)S(1)}, u32[]{:S(2)}, u32[]{:S(2)}) collective-permute-start(f32[1,128]{1,0:T(1,128)S(1)} %add.54), channel_id=1, source_target_pairs={{0,8},{2,10},{4,12},{6,14},{8,0},{10,2},{12,4},{14,6},{1,9},{3,11}... | collective-permute-start | bytes 1544 | tf_op jit(solution)/shard_map/ppermute | solution.py:334
  63.0 7.0 %collective-permute-start.14 = (bf16[32,4096]{1,0:T(8,128)(2,1)S(1)}, bf16[32,4096]{1,0:T(8,128)(2,1)S(1)}, u32[]{:S(2)}, u32[]{:S(2)}) collective-permute-start(bf16[32,4096]{1,0:T(8,128)(2,1)S(1)} %get-tuple-element.41), channel_id=1, source_target_pairs={{0,2},{2,0},{4,6},{6,4},{8,10},{10,8},{12,14},{14,12},{1,3},{3,1},... | collective-permute-start | bytes 786440 | tf_op jit(solution)/shard_map/ppermute | solution.py:334
  63.6 9.7 %collective-permute-start.17 = (bf16[32,4096]{1,0:T(8,128)(2,1)S(1)}, bf16[32,4096]{1,0:T(8,128)(2,1)S(1)}, u32[]{:S(2)}, u32[]{:S(2)}) collective-permute-start(bf16[32,4096]{1,0:T(8,128)(2,1)S(1)} %get-tuple-element.44), channel_id=1, source_target_pairs={{0,2},{2,0},{4,6},{6,4},{8,10},{10,8},{12,14},{14,12},{1,3},{3,1},... | collective-permute-start | bytes 786440 | tf_op jit(solution)/shard_map/ppermute | solution.py:334
  70.1 8.8 %collective-permute-start.15 = (bf16[16,4096]{1,0:T(8,128)(2,1)S(1)}, bf16[16,4096]{1,0:T(8,128)(2,1)S(1)}, u32[]{:S(2)}, u32[]{:S(2)}) collective-permute-start(bf16[16,4096]{1,0:T(8,128)(2,1)S(1)} %get-tuple-element.51), channel_id=1, source_target_pairs={{0,8},{2,10},{4,12},{6,14},{8,0},{10,2},{12,4},{14,6},{1,9},{3,11}... | collective-permute-start | bytes 393224 | tf_op jit(solution)/shard_map/ppermute | solution.py:334
  71.8 7.2 %collective-permute-start.16 = (bf16[16,4096]{1,0:T(8,128)(2,1)S(1)}, bf16[16,4096]{1,0:T(8,128)(2,1)S(1)}, u32[]{:S(2)}, u32[]{:S(2)}) collective-permute-start(bf16[16,4096]{1,0:T(8,128)(2,1)S(1)} %get-tuple-element.52), channel_id=1, source_target_pairs={{0,12},{2,14},{4,8},{6,10},{8,4},{10,6},{12,0},{14,2},{1,13},{3,15... | collective-permute-start | bytes 393224 | tf_op jit(solution)/shard_map/ppermute | solution.py:334
  73.3 6.9 %collective-permute-start.18 = (bf16[16,4096]{1,0:T(8,128)(2,1)S(1)}, bf16[16,4096]{1,0:T(8,128)(2,1)S(1)}, u32[]{:S(2)}, u32[]{:S(2)}) collective-permute-start(bf16[16,4096]{1,0:T(8,128)(2,1)S(1)} %add_convert_fusion.1), channel_id=1, source_target_pairs={{0,4},{2,6},{4,0},{6,2},{8,12},{10,14},{12,8},{14,10},{1,5},{3,7},... | collective-permute-start | bytes 393224 | tf_op jit(solution)/shard_map/ppermute | solution.py:334
  81.0 1.9 %collective-permute-start.19 = (f32[16,4096]{1,0:T(8,128)S(1)}, f32[16,4096]{1,0:T(8,128)S(1)}, u32[]{:S(2)}, u32[]{:S(2)}) collective-permute-start(f32[16,4096]{1,0:T(8,128)S(1)} %get-tuple-element.50), channel_id=1, source_target_pairs={{0,16},{16,0},{1,17},{17,1},{2,18},{18,2},{3,19},{19,3},{4,20},{20... | collective-permute-start | bytes 786440 | tf_op jit(solution)/shard_map/ppermute | solution.py:334
  81.0 3.9 %collective-permute-start.21 = (bf16[128,4096]{1,0:T(8,128)(2,1)S(1)}, bf16[128,4096]{1,0:T(8,128)(2,1)S(1)}, u32[]{:S(2)}, u32[]{:S(2)}) collective-permute-start(bf16[128,4096]{1,0:T(8,128)(2,1)S(1)} %get-tuple-element.46.refs_2_), channel_id=1, source_target_pairs={{0,16},{16,0},{1,17},{17,1},{2,18},{18,2},{3,19},{19,3},{4,20},{20... | collective-permute-start | bytes 3145736 | tf_op jit(solution)/shard_map/ppermute | solution.py:334
  82.7 2.1 %collective-permute-start.20 = (bf16[128,2304]{1,0:T(8,128)(2,1)S(1)}, bf16[128,2304]{1,0:T(8,128)(2,1)S(1)}, u32[]{:S(2)}, u32[]{:S(2)}) collective-permute-start(bf16[128,2304]{1,0:T(8,128)(2,1)S(1)} %grads.1.refs_0_), channel_id=1, source_target_pairs={{0,16},{16,0},{1,17},{17,1},{2,18},{18,2},{3,19},{19,3},{4,20},{20... | collective-permute-start | bytes 1769480 | tf_op jit(solution)/shard_map/ppermute | solution.py:334

commit v4 on v3

--- a/solution.py
+++ b/solution.py
@@ -32,6 +32,11 @@
 
 def vmem():
     return pl.BlockSpec(memory_space=pltpu.VMEM)
+
+
+def owner(me, k, n):
+    half = n // 2
+    return (((me >> 1) + k // 2) & (half - 1)) * 2 + ((me ^ k) & 1)
 
 
 def stage_kernel(start, ids_ref, u_ref, o_ref, sem):
@@ -58,7 +63,7 @@
     parts, (u_ref, o_ref, h_ref, ht_ref) = refs[:n], refs[n:]
     rows = parts[0].shape[0]
     for k in range(n):
-        at = pl.multiple_of((ids_ref[0] ^ k) * rows, rows)
+        at = pl.multiple_of(owner(ids_ref[0], k, n) * rows, rows)
         h_ref[pl.ds(at, rows), :] = parts[k][...]
     ht_ref[...] = h_ref[...].T
     u = u_ref[: o_ref.shape[1], :]
@@ -115,78 +120,90 @@
     return jnp.broadcast_to(row, (row.shape[1], row.shape[1])).T[:, :1]
 
 
-def numer_kernel(start, ids_ref, s_ref, t_ref, *refs):
-    q_ref, tot_ref, stat_ref = refs[-3:]
+def numer_kernel(start, first, last, ids_ref, s_ref, *refs):
     tokens, rows = s_ref.shape
-    targets = column(t_ref[...])
-    sum_e = sum_q = sum_d = 0.0
-    step = 128
-    for j in range(0, rows, step):
-        e, d = soften(s_ref[:, j : j + step])
+    lane = 128
+    if first:
+        t_ref, refs = refs[0], refs[1:]
+        targets = jnp.broadcast_to(column(t_ref[...]), (tokens, lane))
+        sums = [jnp.zeros((tokens, lane), f32)] * 3
+    else:
+        spread_ref, so_far_ref, refs = refs[0], refs[1], refs[2:]
+        targets = spread_ref[...]
+        sums = [so_far_ref[k] for k in range(3)]
+    q_ref, refs = refs[0], refs[1:]
+    for j in range(0, rows, lane):
+        e, d = soften(s_ref[:, j : j + lane])
         hit = hits(ids_ref[2] + (start + j), targets, e.shape)
         q = e * d
-        q_ref[:tokens, j : j + step] = jnp.where(hit, 0.0, q).astype(bf16)
-        q_ref[tokens:, j : j + step] = jnp.where(hit, 1.0, 0.0).astype(bf16)
-        sum_e = sum_e + e
-        sum_q = sum_q + jnp.where(hit, q, 0.0)
-        sum_d = sum_d + jnp.where(hit, d, 0.0)
-    tot, sq, sd = (jnp.sum(a.T, axis=0, keepdims=True) for a in (sum_e, sum_q, sum_d))
-    if len(refs) > 3:
-        tot = tot + refs[0][...]
-        sq = sq + refs[1][:1, :]
-        sd = sd + refs[1][1:2, :]
-    tot_ref[...] = tot
-    stat_ref[:1, :] = sq
-    stat_ref[1:2, :] = sd
-
-
-def numer_call(start, ids, s, targets, so_far):
+        q_ref[:tokens, j : j + lane] = jnp.where(hit, 0.0, q).astype(bf16)
+        q_ref[tokens:, j : j + lane] = jnp.where(hit, 1.0, 0.0).astype(bf16)
+        sums[0] = sums[0] + e
+        sums[1] = sums[1] + jnp.where(hit, q, 0.0)
+        sums[2] = sums[2] + jnp.where(hit, d, 0.0)
+    if last:
+        tot_ref, stat_ref = refs
+        tot, sq, sd = (jnp.sum(a.T, axis=0, keepdims=True) for a in sums)
+        tot_ref[...] = tot
+        stat_ref[:1, :] = sq
+        stat_ref[1:2, :] = sd
+    else:
+        if first:
+            refs[1][...] = targets
+        for k in range(3):
+            refs[0][k] = sums[k]
+
+
+def numer_call(start, first, last, ids, s, operands):
     tokens, rows = s.shape
-    return pl.pallas_call(
-        functools.partial(numer_kernel, start),
-        in_specs=[smem()] + [vmem()] * (2 + len(so_far)),
-        out_specs=[vmem()] * 3,
-        out_shape=[
-            jax.ShapeDtypeStruct((2 * tokens, rows), bf16),
-            jax.ShapeDtypeStruct((1, tokens), f32),
-            jax.ShapeDtypeStruct((2, tokens), f32),
-        ],
+    out_shape = [jax.ShapeDtypeStruct((2 * tokens, rows), bf16)]
+    if last:
+        out_shape.append(jax.ShapeDtypeStruct((1, tokens), f32))
+        out_shape.append(jax.ShapeDtypeStruct((2, tokens), f32))
+    else:
+        out_shape.append(jax.ShapeDtypeStruct((3, tokens, 128), f32))
+    if first:
+        out_shape.append(jax.ShapeDtypeStruct((tokens, 128), jnp.int32))
+    return pl.pallas_call(
+        functools.partial(numer_kernel, start, first, last),
+        in_specs=[smem()] + [vmem()] * (1 + len(operands)),
+        out_specs=[vmem()] * len(out_shape),
+        out_shape=out_shape,
         compiler_params=params(0),
         cost_estimate=cost(40 * tokens * rows, 8 * tokens * rows),
         name="numer",
-    )(ids, s, targets, *so_far)
-
-
-def rows_kernel(block, first, *refs):
-    *q_refs, u_ref, o_ref = refs
+    )(ids, s, *operands)
+
+
+def rows_kernel(block, first, places, *refs):
+    q_refs, u_refs, o_ref = refs[: len(places)], refs[len(places) : -1], refs[-1]
     step = pl.program_id(0) * block
     cols = pl.ds(pl.multiple_of(first + step, block), block)
-    total, row = None, 0
-    for q_ref in q_refs:
-        count = q_ref.shape[1]
-        part = jnp.dot(q_ref[...], u_ref[row : row + count, cols], preferred_element_type=f32)
+    total = None
+    for q_ref, (which, row) in zip(q_refs, places):
+        u = u_refs[which][row : row + q_ref.shape[1], cols]
+        part = jnp.dot(q_ref[...], u, preferred_element_type=f32)
         total = part if total is None else total + part
-        row += count
     o_ref[...] = total
 
 
-def rows_call(qs, unembed, first, width, block):
+def rows_call(qs, staged, places, first, width, block):
     two = qs[0].shape[0]
     rows = sum(q.shape[1] for q in qs)
     return pl.pallas_call(
-        functools.partial(rows_kernel, block, first),
+        functools.partial(rows_kernel, block, first, places),
         grid=(width // block,),
-        in_specs=[vmem()] * (len(qs) + 1),
+        in_specs=[vmem()] * (len(qs) + len(staged)),
         out_specs=pl.BlockSpec((two, block), lambda i: (0, i)),
         out_shape=jax.ShapeDtypeStruct((two, width), f32),
         compiler_params=params(1),
         cost_estimate=cost(2 * two * rows * width, 2 * rows * width),
         name="rows",
-    )(*qs, unembed)
-
-
-def norm_kernel(n, groups, ids_ref, tot_ref, stat_ref, lg_ref, *refs):
-    early, late, refs = refs[:2], refs[2:4], refs[4:]
+    )(*qs, *staged)
+
+
+def norm_kernel(n, groups, parts, ids_ref, tot_ref, stat_ref, lg_ref, *refs):
+    sums, refs = refs[:parts], refs[parts:]
     keep, send = refs[: n // 2], refs[n // 2 : n // 2 + len(groups)]
     sc, wc = refs[-2:]
     tokens = tot_ref.shape[1]
@@ -198,14 +215,14 @@
     wc[...] = jnp.broadcast_to(weight, (tokens, tokens)).T
 
     def block(k, ref, row):
-        at = pl.multiple_of((ids_ref[0] ^ k) * rows, rows)
+        at = pl.multiple_of(owner(ids_ref[0], k, n) * rows, rows)
         scale = sc[pl.ds(at, rows), :1]
         weight = wc[pl.ds(at, rows), :1]
         col = 0
-        for x, y in zip(early, late):
+        for x in sums:
             cols = slice(col, col + x.shape[1])
-            a = x[pl.ds(at, rows), :] + y[pl.ds(at, rows), :]
-            u = x[pl.ds(tokens + at, rows), :] + y[pl.ds(tokens + at, rows), :]
+            a = x[pl.ds(at, rows), :]
+            u = x[pl.ds(tokens + at, rows), :]
             ref[row : row + rows, cols] = (scale * a + weight * u).astype(ref.dtype)
             col += x.shape[1]
 
@@ -218,10 +235,10 @@
 
 def norm_call(n, groups, ids, total, stats, loss_grad, sums):
     tokens = total.shape[1]
-    width = 2 * sums[0].shape[1]
+    width = sum(x.shape[1] for x in sums)
     rows = tokens // n
     return pl.pallas_call(
-        functools.partial(norm_kernel, n, groups),
+        functools.partial(norm_kernel, n, groups, len(sums)),
         in_specs=[smem()] + [vmem()] * (3 + len(sums)),
         out_specs=[vmem()] * (n // 2 + len(groups)),
         out_shape=[jax.ShapeDtypeStruct((rows, width), f32)] * (n // 2)
@@ -237,7 +254,7 @@
     g_ref = refs[count]
     inv = column(1.0 / tot_ref[...])
     lg = column(lg_ref[...])
-    targets = column(t_ref[...])
+    targets = t_ref[...]
     step = 128
     at = 0
     for s_ref in refs[:count]:
@@ -330,6 +347,11 @@
     )(*operands)
 
 
+def slide(x, by, n):
+    half = n // 2
+    return lax.ppermute(x, "seq", [(i, (i // 2 + by) % half * 2 + i % 2) for i in range(n)])
+
+
 def swap(x, axis, mask, size):
     return lax.ppermute(x, axis, [(i, i ^ mask) for i in range(size)])
 
@@ -341,10 +363,17 @@
     return [(a * unit, c * unit) for a, c in zip(starts, sizes)]
 
 
-def thirds(total, unit):
+def portions(total, unit):
     tiles = total // unit
-    sizes = [tiles // 3, tiles - tiles // 3 - tiles // 4, tiles // 4]
-    starts = [sum(sizes[:i]) for i in range(3)]
+    sizes = [tiles - tiles // 3 - 2, 1, tiles // 3, 1]
+    starts = [sum(sizes[:i]) for i in range(len(sizes))]
+    return [(a * unit, c * unit) for a, c in zip(starts, sizes)]
+
+
+def sides(total, unit):
+    tiles = total // unit
+    sizes = [(tiles + 1) // 3, tiles // 4, tiles - (tiles + 1) // 3 - tiles // 4]
+    starts = [sum(sizes[:i]) for i in range(len(sizes))]
     return [(a * unit, c * unit) for a, c in zip(starts, sizes)]
 
 
@@ -353,43 +382,49 @@
     seq_index = lax.axis_index("seq")
     ids = jnp.stack([seq_index, lax.axis_index("head"), seq_index * block_rows]).astype(jnp.int32)
     hidden = (trunk.astype(f32) + branch[0].astype(f32)).astype(bf16)
-    far = [2, 6, 4]
+    far = [2 * (i + 1) for i in range(n // 2 - 1)]
+    far = far[:1] + far[1:][::-1]
 
     pieces = [None] * n
     pieces[0] = hidden
     for k in far:
-        pieces[k] = swap(hidden, "seq", k, n)
+        pieces[k] = slide(hidden, -k // 2, n)
     for k in [0] + far:
         pieces[k + 1] = swap(pieces[k], "seq", 1, n)
 
     chunks = split(block_rows, 256)
     late = chunks[2][0]
     staged = []
-    for start, count in ((0, late), (late, block_rows - late)):
+    for start, count in ((0, late), *chunks[2:]):
         staged.append(stage_call(ids, unembed, start, count))
+    places = ((0, 0), (0, chunks[1][0]), (1, 0), (2, 0))
     scores = []
     for c, (start, count) in enumerate(chunks):
         if c == 0:
             s, all_hidden, turned = first_call(ids, pieces, staged[0], count)
         else:
-            s = next_call(turned, staged[c // 2], start - c // 2 * late, count)
+            s = next_call(turned, staged[places[c][0]], places[c][1], count)
         s = s.astype(f16)
         scores.append(s.astype(f32) + swap(s, "mp", 1, 2).astype(f32))
     other_hidden = swap(all_hidden, "head", 1, 2)
-    so_far, qs = [], []
+    qs, spread, so_far = [], None, None
     for c, (start, count) in enumerate(chunks):
-        q, *so_far = numer_call(start, ids, scores[c], targets, so_far)
+        last = c == len(chunks) - 1
+        operands = [spread, so_far] if c else [targets]
+        q, *out = numer_call(start, c == 0, last, ids, scores[c], operands)
         qs.append(q)
-    half = width // 2
+        if c == 0:
+            so_far, spread = out
+        elif not last:
+            so_far = out[0]
+    total, stats = out
     sums = []
-    for r, group in enumerate((qs[:2], qs[2:])):
-        for p in range(2):
-            sums.append(rows_call(group, staged[r], p * half, half, 512))
-    total, stats = so_far
+    for start, count in sides(width, 512):
+        sums.append(rows_call(qs, staged, places, start, count, 512))
     for i in range(n.bit_length() - 1):
         total = total + swap(total, "seq", 1 << i, n)
 
-    groups = ((4, 6), (2, 0))
+    groups = ((4, 2), (6, 0))
     blocks = norm_call(n, groups, ids, total, stats, loss_grad, sums)
     keep, send = blocks[: n // 2], blocks[n // 2 :]
     rows = hidden.shape[0]
@@ -399,14 +434,14 @@
         for j, k in enumerate(group):
             both = keep[k // 2] + theirs[j * rows : (j + 1) * rows].astype(f32)
             if k:
-                both = swap(both.astype(bf16), "seq", k, n).astype(f32)
+                both = slide(both.astype(bf16), k // 2, n).astype(f32)
             got.append(both)
     row_grad = functools.reduce(lambda a, b: a + b, got)
 
-    g = grads_call(ids, scores, targets, total, loss_grad)
+    g = grads_call(ids, scores, spread, total, loss_grad)
     g_other = swap(g, "head", 1, 2)
     d_unembed, hs = None, [all_hidden, other_hidden]
-    for p, (start, count) in enumerate(thirds(block_rows, 256)):
+    for p, (start, count) in enumerate(portions(block_rows, 256)):
         out = weight_call(ids, g, g_other, hs, start, count, 256, d_unembed)
         d_unembed = out[0]
         if p == 0:

time: 102 us -> 104 us (1.020)
  starting transfers between devices: 24.8 us -> 29.2 us
  waiting for transfers between devices: 26.9 us -> 23.7 us
    ppermute x22 -> x16, waiting for transfers between devices: 26.9 us -> 15 us  [swap(): return lax.ppermute(x, axis, [(i, i ^ mask) for i in range(size)])]
    ppermute x0 -> x6, starting transfers between devices: none -> 11.2 us  [slide(): lax.ppermute(x, 'seq', [(i, (i // 2 + by) % half * 2 + i % 2) for i in ra...]
    ppermute x0 -> x6, waiting for transfers between devices: none -> 8.75 us  [slide(): lax.ppermute(x, 'seq', [(i, (i // 2 + by) % half * 2 + i % 2) for i in ra...]
    ppermute x22 -> x16, starting transfers between devices: 24.8 us -> 18 us  [swap(): return lax.ppermute(x, axis, [(i, i ^ mask) for i in range(size)])]
    pallas_call x9 -> x8, Pallas kernels: 13.1 us -> 10.8 us  [the longest x3 6.63 us: rows_call(): pl.pallas_call(functools.partial(rows_kernel, block, first, places), grid...]
    pallas_call x3 -> x4, Pallas kernels: 16.8 us -> 18.4 us  [weight_call(): pl.pallas_call(functools.partial(weight_kernel, first, start, block), in_...]
    pallas_call x2 -> x3, Pallas kernels: 8.46 us -> 10 us  [stage_call(): pl.pallas_call(functools.partial(stage_kernel, start), in_specs=[smem(),...]
  transfers between devices with their start and end apart: 22 -> 22, of which waited for: 10 -> 10; matrix products, arithmetic and copies ran while one was open for 1% -> 1% of each run, Pallas kernels for 24% -> 23%
where the time goes in v4:
time: 104 us
  Pallas kernels  46.9 us (45%)
  starting transfers between devices  29.2 us (28%)
  waiting for transfers between devices  23.7 us (23%)
  other arithmetic  2.84 us (3%)
  between operations  1.09 us (1%)
    pallas_call x4, Pallas kernels, weight_call(): pl.pallas_call(functools.partial(weight_kernel, first, start, block), in_...  18.4 us
    ppermute x16, starting transfers between devices, swap(): return lax.ppermute(x, axis, [(i, i ^ mask) for i in range(size)])  18 us
    ppermute x16, waiting for transfers between devices, swap(): return lax.ppermute(x, axis, [(i, i ^ mask) for i in range(size)])  15 us
    ppermute x6, starting transfers between devices, slide(): lax.ppermute(x, 'seq', [(i, (i // 2 + by) % half * 2 + i % 2) for i in ra...  11.2 us
    pallas_call x3, Pallas kernels, stage_call(): pl.pallas_call(functools.partial(stage_kernel, start), in_specs=[smem(),...  10 us
    ppermute x6, waiting for transfers between devices, slide(): lax.ppermute(x, 'seq', [(i, (i // 2 + by) % half * 2 + i % 2) for i in ra...  8.75 us
    pallas_call x3, Pallas kernels, rows_call(): pl.pallas_call(functools.partial(rows_kernel, block, first, places), grid...  6.63 us
    pallas_call x3, Pallas kernels, next_call(): pl.pallas_call(functools.partial(next_kernel, start), in_specs=[vmem()] *...  5.02 us
  transfers between devices with their start and end apart: 22, of which 10 were waited for; matrix products, arithmetic and copies ran while one was open for 1% of the time, Pallas kernels for 23%

profile of v4, /device:TPU:0, one launch (start us, length us, event | category | flops | bytes accessed | tf_op | source)
XLA Modules:
  0.0 103.8 jit_solution(1436921639077061655)
XLA Ops:
  1.6 3.1 %collective-permute-start.5 = (bf16[16,4096]{1,0:T(8,128)(2,1)S(1)}, bf16[16,4096]{1,0:T(8,128)(2,1)S(1)}, u32[]{:S(2)}, u32[]{:S(2)}) collective-permute-start(bf16[16,4096]{1,0:T(8,128)(2,1)S(1)} %fusion.refs_0_), channel_id=1, source_target_pairs={{0,4},{2,6},{4,8},{6,10},{8,12},{10,14},{12,0},{14,2},{1,5},{3,7},... | collective-permute-start | bytes 393224 | tf_op jit(solution)/shard_map/ppermute | solution.py:352
  4.7 2.6 %collective-permute-start.3 = (bf16[16,4096]{1,0:T(8,128)(2,1)S(1)}, bf16[16,4096]{1,0:T(8,128)(2,1)S(1)}, u32[]{:S(2)}, u32[]{:S(2)}) collective-permute-start(bf16[16,4096]{1,0:T(8,128)(2,1)S(1)} %fusion.refs_0_), channel_id=1, source_target_pairs={{0,8},{2,10},{4,12},{6,14},{8,0},{10,2},{12,4},{14,6},{1,9},{3,11}... | collective-permute-start | bytes 393224 | tf_op jit(solution)/shard_map/ppermute | solution.py:352
  11.2 1.7 %collective-permute-start.6 = (bf16[16,4096]{1,0:T(8,128)(2,1)S(1)}, bf16[16,4096]{1,0:T(8,128)(2,1)S(1)}, u32[]{:S(2)}, u32[]{:S(2)}) collective-permute-start(bf16[16,4096]{1,0:T(8,128)(2,1)S(1)} %collective-permute-done.5.refs_6_), channel_id=1, source_target_pairs={{0,2},{2,0},{4,6},{6,4},{8,10},{10,8},{12,14},{14,12},{1,3},{3,1},... | collective-permute-start | bytes 393224 | tf_op jit(solution)/shard_map/ppermute | solution.py:356
  13.0 3.0 %collective-permute-done.3.refs_4_ = bf16[16,4096]{1,0:T(8,128)(2,1)S(1)} collective-permute-done((bf16[16,4096]{1,0:T(8,128)(2,1)S(1)}, bf16[16,4096]{1,0:T(8,128)(2,1)S(1)}, u32[]{:S(2)}, u32[]{:S(2)}) %collective-permute-start.3) | collective-permute-done | bytes 131104 | tf_op jit(solution)/shard_map/ppermute | solution.py:352
  18.1 2.7 %stage.4.u_ref.refs_6_ = bf16[512,4096]{1,0:T(8,128)(2,1)S(1)} custom-call(s32[3]{0:T(128)S(1)} %pad_add_fusion.ids_ref, bf16[2304,4096]{1,0:T(8,128)(2,1)} %u_ref.5), custom_call_target="tpu_custom_call" | custom-call | flops 2097152 | bytes 8388608 | tf_op jit(solution)/shard_map/stage/pallas_call | solution.py:50
  20.8 3.3 %stage.5.u_ref.refs_5_ = bf16[768,4096]{1,0:T(8,128)(2,1)S(1)} custom-call(s32[3]{0:T(128)S(1)} %pad_add_fusion.ids_ref, bf16[2304,4096]{1,0:T(8,128)(2,1)} %u_ref.5), custom_call_target="tpu_custom_call" | custom-call | flops 3145728 | bytes 12582912 | tf_op jit(solution)/shard_map/stage/pallas_call | solution.py:50
  24.2 3.9 %stage.3.refs_8_.u_ref.refs_4_ = bf16[1024,4096]{1,0:T(8,128)(2,1)S(1)} custom-call(s32[3]{0:T(128)S(1)} %pad_add_fusion.ids_ref, bf16[2304,4096]{1,0:T(8,128)(2,1)} %u_ref.5), custom_call_target="tpu_custom_call" | custom-call | flops 4194304 | bytes 16777216 | tf_op jit(solution)/shard_map/stage/pallas_call | solution.py:50
  33.2 1.8 %scores_next.4 = f32[128,768]{1,0:T(8,128)S(1)} custom-call(bf16[4096,128]{1,0:T(8,128)(2,1)S(1)} %get-tuple-element.24.ht_ref, bf16[768,4096]{1,0:T(8,128)(2,1)S(1)} %stage.5.u_ref.refs_5_), custom_call_target="tpu_custom_call" | custom-call | flops 805306368 | bytes 6291456 | tf_op jit(solution)/shard_map/scores_next/pallas_call | solution.py:98
  35.1 1.8 %scores_next.5 = f32[128,768]{1,0:T(8,128)S(1)} custom-call(bf16[4096,128]{1,0:T(8,128)(2,1)S(1)} %get-tuple-element.24.ht_ref, bf16[1024,4096]{1,0:T(8,128)(2,1)S(1)} %stage.3.refs_8_.u_ref.refs_4_), custom_call_target="tpu_custom_call" | custom-call | flops 805306368 | bytes 6291456 | tf_op jit(solution)/shard_map/scores_next/pallas_call | solution.py:98
  36.9 1.6 %collective-permute-start.10 = (f16[128,768]{1,0:T(8,128)(2,1)S(1)}, f16[128,768]{1,0:T(8,128)(2,1)S(1)}, u32[]{:S(2)}, u32[]{:S(2)}) collective-permute-start(f16[128,768]{1,0:T(8,128)(2,1)S(1)} %convert_element_type.97), channel_id=1, source_target_pairs={{0,1},{1,0},{2,3},{3,2},{4,5},{5,4},{6,7},{7,6},{8,9},{9,8},{10,11... | collective-permute-start | bytes 589832 | tf_op jit(solution)/shard_map/ppermute | solution.py:356
  39.8 4.9 %collective-permute-done.10 = f16[128,768]{1,0:T(8,128)(2,1)S(1)} collective-permute-done((f16[128,768]{1,0:T(8,128)(2,1)S(1)}, f16[128,768]{1,0:T(8,128)(2,1)S(1)}, u32[]{:S(2)}, u32[]{:S(2)}) %collective-permute-start.10) | collective-permute-done | bytes 196640 | tf_op jit(solution)/shard_map/ppermute | solution.py:356
  48.5 1.6 %collective-permute-start.11 = (f32[1,128]{1,0:T(1,128)S(1)}, f32[1,128]{1,0:T(1,128)S(1)}, u32[]{:S(2)}, u32[]{:S(2)}) collective-permute-start(f32[1,128]{1,0:T(1,128)S(1)} %get-tuple-element.30), channel_id=1, source_target_pairs={{0,2},{2,0},{4,6},{6,4},{8,10},{10,8},{12,14},{14,12},{1,3},{3,1},... | collective-permute-start | bytes 1544 | tf_op jit(solution)/shard_map/ppermute | solution.py:356
  50.1 2.5 %rows.5.refs_2_ = f32[256,1536]{1,0:T(8,128)S(1)} custom-call(bf16[256,256]{1,0:T(8,128)(2,1)S(1)} %get-tuple-element.32.refs_0_, bf16[256,768]{1,0:T(8,128)(2,1)S(1)} %get-tuple-element.33.refs_1_, bf16[256,768]{1,0:T(8,128)(2,1)S(1)} %get-tuple-element.34.refs_2_, bf16[256,512]{1,0:T(8,128)(2,1)S(1)} %get-tuple-element.35.refs_3_, ...), custom_call_target="tpu_custom_call" | custom-call | flops 1811939328 | bytes 7077888 | tf_op jit(solution)/shard_map/rows/pallas_call | solution.py:193
  52.6 2.7 %collective-permute-start.12 = (f32[1,128]{1,0:T(1,128)S(1)}, f32[1,128]{1,0:T(1,128)S(1)}, u32[]{:S(2)}, u32[]{:S(2)}) collective-permute-start(f32[1,128]{1,0:T(1,128)S(1)} %add.53), channel_id=1, source_target_pairs={{0,4},{2,6},{4,0},{6,2},{8,12},{10,14},{12,8},{14,10},{1,5},{3,7},... | collective-permute-start | bytes 1544 | tf_op jit(solution)/shard_map/ppermute | solution.py:356
  55.3 2.5 %rows.3.refs_0_ = f32[256,1536]{1,0:T(8,128)S(1)} custom-call(bf16[256,256]{1,0:T(8,128)(2,1)S(1)} %get-tuple-element.32.refs_0_, bf16[256,768]{1,0:T(8,128)(2,1)S(1)} %get-tuple-element.33.refs_1_, bf16[256,768]{1,0:T(8,128)(2,1)S(1)} %get-tuple-element.34.refs_2_, bf16[256,512]{1,0:T(8,128)(2,1)S(1)} %get-tuple-element.35.refs_3_, ...), custom_call_target="tpu_custom_call" | custom-call | flops 1811939328 | bytes 7077888 | tf_op jit(solution)/shard_map/rows/pallas_call | solution.py:193
  57.8 1.6 %collective-permute-start.13 = (f32[1,128]{1,0:T(1,128)S(1)}, f32[1,128]{1,0:T(1,128)S(1)}, u32[]{:S(2)}, u32[]{:S(2)}) collective-permute-start(f32[1,128]{1,0:T(1,128)S(1)} %add.54), channel_id=1, source_target_pairs={{0,8},{2,10},{4,12},{6,14},{8,0},{10,2},{12,4},{14,6},{1,9},{3,11}... | collective-permute-start | bytes 1544 | tf_op jit(solution)/shard_map/ppermute | solution.py:356
  59.4 1.7 %rows.4.refs_1_ = f32[256,1024]{1,0:T(8,128)S(1)} custom-call(bf16[256,256]{1,0:T(8,128)(2,1)S(1)} %get-tuple-element.32.refs_0_, bf16[256,768]{1,0:T(8,128)(2,1)S(1)} %get-tuple-element.33.refs_1_, bf16[256,768]{1,0:T(8,128)(2,1)S(1)} %get-tuple-element.34.refs_2_, bf16[256,512]{1,0:T(8,128)(2,1)S(1)} %get-tuple-element.35.refs_3_, ...), custom_call_target="tpu_custom_call" | custom-call | flops 1207959552 | bytes 4718592 | tf_op jit(solution)/shard_map/rows/pallas_call | solution.py:193
  65.5 5.1 %collective-permute-done.14 = bf16[32,4096]{1,0:T(8,128)(2,1)S(1)} collective-permute-done((bf16[32,4096]{1,0:T(8,128)(2,1)S(1)}, bf16[32,4096]{1,0:T(8,128)(2,1)S(1)}, u32[]{:S(2)}, u32[]{:S(2)}) %collective-permute-start.14) | collective-permute-done | bytes 262176 | tf_op jit(solution)/shard_map/ppermute | solution.py:356
  73.5 2.4 %collective-permute-start.18 = (bf16[16,4096]{1,0:T(8,128)(2,1)S(1)}, bf16[16,4096]{1,0:T(8,128)(2,1)S(1)}, u32[]{:S(2)}, u32[]{:S(2)}) collective-permute-start(bf16[16,4096]{1,0:T(8,128)(2,1)S(1)} %add_convert_fusion.1), channel_id=1, source_target_pairs={{0,12},{2,14},{4,0},{6,2},{8,4},{10,6},{12,8},{14,10},{1,13},{3,15... | collective-permute-start | bytes 393224 | tf_op jit(solution)/shard_map/ppermute | solution.py:352
  75.9 3.4 %collective-permute-done.15 = bf16[16,4096]{1,0:T(8,128)(2,1)S(1)} collective-permute-done((bf16[16,4096]{1,0:T(8,128)(2,1)S(1)}, bf16[16,4096]{1,0:T(8,128)(2,1)S(1)}, u32[]{:S(2)}, u32[]{:S(2)}) %collective-permute-start.15) | collective-permute-done | bytes 131104 | tf_op jit(solution)/shard_map/ppermute | solution.py:352
  85.2 7.0 %weight.4 = (f32[2304,4096]{1,0:T(8,128)}, bf16[256,4096]{1,0:T(8,128)(2,1)S(1)}) custom-call(s32[3]{0:T(128)S(1)} %pad_add_fusion.ids_ref, bf16[128,2304]{1,0:T(8,128)(2,1)S(1)} %grads.1.refs_0_, bf16[128,2304]{1,0:T(8,128)(2,1)S(1)} %collective-permute-done.20.refs_1_, bf16[128,4096]{1,0:T(8,128)(2,1)S(1)} %get-tuple-element.42.refs_2_, ...), custom_call_target="tpu_custom_call" | custom-call | flops 2147483648 | bytes 16777216 | tf_op jit(solution)/shard_map/weight/pallas_call | solution.py:333
  92.2 2.9 %weight.5.refs_3_ = f32[2304,4096]{1,0:T(8,128)} custom-call(s32[3]{0:T(128)S(1)} %pad_add_fusion.ids_ref, bf16[128,2304]{1,0:T(8,128)(2,1)S(1)} %grads.1.refs_0_, bf16[128,2304]{1,0:T(8,128)(2,1)S(1)} %collective-permute-done.20.refs_1_, bf16[256,4096]{1,0:T(8,128)(2,1)S(1)} %get-tuple-element.43.refs_2_, ...), custom_call_target="tpu_custom_call", output_to_operand_aliasing={{}: (4, {})} | custom-call | flops 536870912 | bytes 4194304 | tf_op jit(solution)/shard_map/weight/pallas_call | solution.py:333
  95.2 5.6 %weight.6.refs_3_ = f32[2304,4096]{1,0:T(8,128)} custom-call(s32[3]{0:T(128)S(1)} %pad_add_fusion.ids_ref, bf16[128,2304]{1,0:T(8,128)(2,1)S(1)} %grads.1.refs_0_, bf16[128,2304]{1,0:T(8,128)(2,1)S(1)} %collective-permute-done.20.refs_1_, bf16[256,4096]{1,0:T(8,128)(2,1)S(1)} %get-tuple-element.43.refs_2_, ...), custom_call_target="tpu_custom_call", output_to_operand_aliasing={{}: (4, {})} | custom-call | flops 1610612736 | bytes 12582912 | tf_op jit(solution)/shard_map/weight/pallas_call | solution.py:333
  100.7 2.9 %weight.7 = f32[2304,4096]{1,0:T(8,128)} custom-call(s32[3]{0:T(128)S(1)} %pad_add_fusion.ids_ref, bf16[128,2304]{1,0:T(8,128)(2,1)S(1)} %grads.1.refs_0_, bf16[128,2304]{1,0:T(8,128)(2,1)S(1)} %collective-permute-done.20.refs_1_, bf16[256,4096]{1,0:T(8,128)(2,1)S(1)} %get-tuple-element.43.refs_2_, ...), custom_call_target="tpu_custom_call", output_to_operand_aliasing={{}: (4, {})} | custom-call | flops 536870912 | bytes 4194304 | tf_op jit(solution)/shard_map/weight/pallas_call | solution.py:333
  (61 shorter events, 30.3 us)
Async XLA Ops:
  1.6 9.6 %collective-permute-start.5 = (bf16[16,4096]{1,0:T(8,128)(2,1)S(1)}, bf16[16,4096]{1,0:T(8,128)(2,1)S(1)}, u32[]{:S(2)}, u32[]{:S(2)}) collective-permute-start(bf16[16,4096]{1,0:T(8,128)(2,1)S(1)} %fusion.refs_0_), channel_id=1, source_target_pairs={{0,4},{2,6},{4,8},{6,10},{8,12},{10,14},{12,0},{14,2},{1,5},{3,7},... | collective-permute-start | bytes 393224 | tf_op jit(solution)/shard_map/ppermute | solution.py:352
  4.7 11.2 %collective-permute-start.3 = (bf16[16,4096]{1,0:T(8,128)(2,1)S(1)}, bf16[16,4096]{1,0:T(8,128)(2,1)S(1)}, u32[]{:S(2)}, u32[]{:S(2)}) collective-permute-start(bf16[16,4096]{1,0:T(8,128)(2,1)S(1)} %fusion.refs_0_), channel_id=1, source_target_pairs={{0,8},{2,10},{4,12},{6,14},{8,0},{10,2},{12,4},{14,6},{1,9},{3,11}... | collective-permute-start | bytes 393224 | tf_op jit(solution)/shard_map/ppermute | solution.py:352
  7.3 10.2 %collective-permute-start.1 = (bf16[16,4096]{1,0:T(8,128)(2,1)S(1)}, bf16[16,4096]{1,0:T(8,128)(2,1)S(1)}, u32[]{:S(2)}, u32[]{:S(2)}) collective-permute-start(bf16[16,4096]{1,0:T(8,128)(2,1)S(1)} %fusion.refs_0_), channel_id=1, source_target_pairs={{0,12},{2,14},{4,0},{6,2},{8,4},{10,6},{12,8},{14,10},{1,13},{3,15... | collective-permute-start | bytes 393224 | tf_op jit(solution)/shard_map/ppermute | solution.py:352
  8.7 19.4 %collective-permute-start = (bf16[16,4096]{1,0:T(8,128)(2,1)S(1)}, bf16[16,4096]{1,0:T(8,128)(2,1)S(1)}, u32[]{:S(2)}, u32[]{:S(2)}) collective-permute-start(bf16[16,4096]{1,0:T(8,128)(2,1)S(1)} %fusion.refs_0_), channel_id=1, source_target_pairs={{0,2},{2,0},{4,6},{6,4},{8,10},{10,8},{12,14},{14,12},{1,3},{3,1},... | collective-permute-start | bytes 393224 | tf_op jit(solution)/shard_map/ppermute | solution.py:356
  11.2 16.9 %collective-permute-start.6 = (bf16[16,4096]{1,0:T(8,128)(2,1)S(1)}, bf16[16,4096]{1,0:T(8,128)(2,1)S(1)}, u32[]{:S(2)}, u32[]{:S(2)}) collective-permute-start(bf16[16,4096]{1,0:T(8,128)(2,1)S(1)} %collective-permute-done.5.refs_6_), channel_id=1, source_target_pairs={{0,2},{2,0},{4,6},{6,4},{8,10},{10,8},{12,14},{14,12},{1,3},{3,1},... | collective-permute-start | bytes 393224 | tf_op jit(solution)/shard_map/ppermute | solution.py:356
  16.0 12.2 %collective-permute-start.4 = (bf16[16,4096]{1,0:T(8,128)(2,1)S(1)}, bf16[16,4096]{1,0:T(8,128)(2,1)S(1)}, u32[]{:S(2)}, u32[]{:S(2)}) collective-permute-start(bf16[16,4096]{1,0:T(8,128)(2,1)S(1)} %collective-permute-done.3.refs_4_), channel_id=1, source_target_pairs={{0,2},{2,0},{4,6},{6,4},{8,10},{10,8},{12,14},{14,12},{1,3},{3,1},... | collective-permute-start | bytes 393224 | tf_op jit(solution)/shard_map/ppermute | solution.py:356
  17.5 10.6 %collective-permute-start.2 = (bf16[16,4096]{1,0:T(8,128)(2,1)S(1)}, bf16[16,4096]{1,0:T(8,128)(2,1)S(1)}, u32[]{:S(2)}, u32[]{:S(2)}) collective-permute-start(bf16[16,4096]{1,0:T(8,128)(2,1)S(1)} %collective-permute-done.1.refs_2_), channel_id=1, source_target_pairs={{0,2},{2,0},{4,6},{6,4},{8,10},{10,8},{12,14},{14,12},{1,3},{3,1},... | collective-permute-start | bytes 393224 | tf_op jit(solution)/shard_map/ppermute | solution.py:356
  29.7 9.4 %collective-permute-start.8 = (f16[128,256]{1,0:T(8,128)(2,1)S(1)}, f16[128,256]{1,0:T(8,128)(2,1)S(1)}, u32[]{:S(2)}, u32[]{:S(2)}) collective-permute-start(f16[128,256]{1,0:T(8,128)(2,1)S(1)} %convert_element_type.91), channel_id=1, source_target_pairs={{0,1},{1,0},{2,3},{3,2},{4,5},{5,4},{6,7},{7,6},{8,9},{9,8},{10,11... | collective-permute-start | bytes 196616 | tf_op jit(solution)/shard_map/ppermute | solution.py:356
  32.6 6.5 %copy-start.1 = (s32[1,128]{1,0:T(1,128)S(1)}, s32[1,128]{1,0:T(1,128)}, u32[]{:S(2)}) copy-start(s32[1,128]{1,0:T(1,128)} %refs_0_.1) | copy-start | bytes 1540
  32.6 7.2 %collective-permute-start.7 = (f16[128,512]{1,0:T(8,128)(2,1)S(1)}, f16[128,512]{1,0:T(8,128)(2,1)S(1)}, u32[]{:S(2)}, u32[]{:S(2)}) collective-permute-start(f16[128,512]{1,0:T(8,128)(2,1)S(1)} %convert_element_type.88), channel_id=1, source_target_pairs={{0,1},{1,0},{2,3},{3,2},{4,5},{5,4},{6,7},{7,6},{8,9},{9,8},{10,11... | collective-permute-start | bytes 393224 | tf_op jit(solution)/shard_map/ppermute | solution.py:356
  36.9 7.8 %collective-permute-start.10 = (f16[128,768]{1,0:T(8,128)(2,1)S(1)}, f16[128,768]{1,0:T(8,128)(2,1)S(1)}, u32[]{:S(2)}, u32[]{:S(2)}) collective-permute-start(f16[128,768]{1,0:T(8,128)(2,1)S(1)} %convert_element_type.97), channel_id=1, source_target_pairs={{0,1},{1,0},{2,3},{3,2},{4,5},{5,4},{6,7},{7,6},{8,9},{9,8},{10,11... | collective-permute-start | bytes 589832 | tf_op jit(solution)/shard_map/ppermute | solution.py:356
  38.5 8.3 %collective-permute-start.9 = (f16[128,768]{1,0:T(8,128)(2,1)S(1)}, f16[128,768]{1,0:T(8,128)(2,1)S(1)}, u32[]{:S(2)}, u32[]{:S(2)}) collective-permute-start(f16[128,768]{1,0:T(8,128)(2,1)S(1)} %convert_element_type.94), channel_id=1, source_target_pairs={{0,1},{1,0},{2,3},{3,2},{4,5},{5,4},{6,7},{7,6},{8,9},{9,8},{10,11... | collective-permute-start | bytes 589832 | tf_op jit(solution)/shard_map/ppermute | solution.py:356
  48.5 4.1 %collective-permute-start.11 = (f32[1,128]{1,0:T(1,128)S(1)}, f32[1,128]{1,0:T(1,128)S(1)}, u32[]{:S(2)}, u32[]{:S(2)}) collective-permute-start(f32[1,128]{1,0:T(1,128)S(1)} %get-tuple-element.30), channel_id=1, source_target_pairs={{0,2},{2,0},{4,6},{6,4},{8,10},{10,8},{12,14},{14,12},{1,3},{3,1},... | collective-permute-start | bytes 1544 | tf_op jit(solution)/shard_map/ppermute | solution.py:356
  52.6 5.2 %collective-permute-start.12 = (f32[1,128]{1,0:T(1,128)S(1)}, f32[1,128]{1,0:T(1,128)S(1)}, u32[]{:S(2)}, u32[]{:S(2)}) collective-permute-start(f32[1,128]{1,0:T(1,128)S(1)} %add.53), channel_id=1, source_target_pairs={{0,4},{2,6},{4,0},{6,2},{8,12},{10,14},{12,8},{14,10},{1,5},{3,7},... | collective-permute-start | bytes 1544 | tf_op jit(solution)/shard_map/ppermute | solution.py:356
  57.8 4.6 %copy-start = (f32[1,128]{1,0:T(1,128)S(1)}, f32[1,128]{1,0:T(1,128)}, u32[]{:S(2)}) copy-start(f32[1,128]{1,0:T(1,128)} %lg_ref.3) | copy-start | bytes 1540
  57.8 4.5 %collective-permute-start.13 = (f32[1,128]{1,0:T(1,128)S(1)}, f32[1,128]{1,0:T(1,128)S(1)}, u32[]{:S(2)}, u32[]{:S(2)}) collective-permute-start(f32[1,128]{1,0:T(1,128)S(1)} %add.54), channel_id=1, source_target_pairs={{0,8},{2,10},{4,12},{6,14},{8,0},{10,2},{12,4},{14,6},{1,9},{3,11}... | collective-permute-start | bytes 1544 | tf_op jit(solution)/shard_map/ppermute | solution.py:356
  63.4 7.2 %collective-permute-start.14 = (bf16[32,4096]{1,0:T(8,128)(2,1)S(1)}, bf16[32,4096]{1,0:T(8,128)(2,1)S(1)}, u32[]{:S(2)}, u32[]{:S(2)}) collective-permute-start(bf16[32,4096]{1,0:T(8,128)(2,1)S(1)} %get-tuple-element.37), channel_id=1, source_target_pairs={{0,2},{2,0},{4,6},{6,4},{8,10},{10,8},{12,14},{14,12},{1,3},{3,1},... | collective-permute-start | bytes 786440 | tf_op jit(solution)/shard_map/ppermute | solution.py:356
  64.6 8.9 %collective-permute-start.17 = (bf16[32,4096]{1,0:T(8,128)(2,1)S(1)}, bf16[32,4096]{1,0:T(8,128)(2,1)S(1)}, u32[]{:S(2)}, u32[]{:S(2)}) collective-permute-start(bf16[32,4096]{1,0:T(8,128)(2,1)S(1)} %get-tuple-element.40), channel_id=1, source_target_pairs={{0,2},{2,0},{4,6},{6,4},{8,10},{10,8},{12,14},{14,12},{1,3},{3,1},... | collective-permute-start | bytes 786440 | tf_op jit(solution)/shard_map/ppermute | solution.py:356
  70.7 8.6 %collective-permute-start.15 = (bf16[16,4096]{1,0:T(8,128)(2,1)S(1)}, bf16[16,4096]{1,0:T(8,128)(2,1)S(1)}, u32[]{:S(2)}, u32[]{:S(2)}) collective-permute-start(bf16[16,4096]{1,0:T(8,128)(2,1)S(1)} %get-tuple-element.47), channel_id=1, source_target_pairs={{0,8},{2,10},{4,12},{6,14},{8,0},{10,2},{12,4},{14,6},{1,9},{3,11}... | collective-permute-start | bytes 393224 | tf_op jit(solution)/shard_map/ppermute | solution.py:352
  71.8 7.5 %collective-permute-start.16 = (bf16[16,4096]{1,0:T(8,128)(2,1)S(1)}, bf16[16,4096]{1,0:T(8,128)(2,1)S(1)}, u32[]{:S(2)}, u32[]{:S(2)}) collective-permute-start(bf16[16,4096]{1,0:T(8,128)(2,1)S(1)} %get-tuple-element.48), channel_id=1, source_target_pairs={{0,4},{2,6},{4,8},{6,10},{8,12},{10,14},{12,0},{14,2},{1,5},{3,7},... | collective-permute-start | bytes 393224 | tf_op jit(solution)/shard_map/ppermute | solution.py:352
  73.5 7.1 %collective-permute-start.18 = (bf16[16,4096]{1,0:T(8,128)(2,1)S(1)}, bf16[16,4096]{1,0:T(8,128)(2,1)S(1)}, u32[]{:S(2)}, u32[]{:S(2)}) collective-permute-start(bf16[16,4096]{1,0:T(8,128)(2,1)S(1)} %add_convert_fusion.1), channel_id=1, source_target_pairs={{0,12},{2,14},{4,0},{6,2},{8,4},{10,6},{12,8},{14,10},{1,13},{3,15... | collective-permute-start | bytes 393224 | tf_op jit(solution)/shard_map/ppermute | solution.py:352
  81.4 1.8 %collective-permute-start.19 = (f32[16,4096]{1,0:T(8,128)S(1)}, f32[16,4096]{1,0:T(8,128)S(1)}, u32[]{:S(2)}, u32[]{:S(2)}) collective-permute-start(f32[16,4096]{1,0:T(8,128)S(1)} %get-tuple-element.46), channel_id=1, source_target_pairs={{0,16},{16,0},{1,17},{17,1},{2,18},{18,2},{3,19},{19,3},{4,20},{20... | collective-permute-start | bytes 786440 | tf_op jit(solution)/shard_map/ppermute | solution.py:356
  81.4 3.9 %collective-permute-start.21 = (bf16[128,4096]{1,0:T(8,128)(2,1)S(1)}, bf16[128,4096]{1,0:T(8,128)(2,1)S(1)}, u32[]{:S(2)}, u32[]{:S(2)}) collective-permute-start(bf16[128,4096]{1,0:T(8,128)(2,1)S(1)} %get-tuple-element.42.refs_2_), channel_id=1, source_target_pairs={{0,16},{16,0},{1,17},{17,1},{2,18},{18,2},{3,19},{19,3},{4,20},{20... | collective-permute-start | bytes 3145736 | tf_op jit(solution)/shard_map/ppermute | solution.py:356
  83.1 2.2 %collective-permute-start.20 = (bf16[128,2304]{1,0:T(8,128)(2,1)S(1)}, bf16[128,2304]{1,0:T(8,128)(2,1)S(1)}, u32[]{:S(2)}, u32[]{:S(2)}) collective-permute-start(bf16[128,2304]{1,0:T(8,128)(2,1)S(1)} %grads.1.refs_0_), channel_id=1, source_target_pairs={{0,16},{16,0},{1,17},{17,1},{2,18},{18,2},{3,19},{19,3},{4,20},{20... | collective-permute-start | bytes 1769480 | tf_op jit(solution)/shard_map/ppermute | solution.py:356

commit v5 on v4

--- a/solution.py
+++ b/solution.py
@@ -13,7 +13,6 @@
 f32 = jnp.float32
 f16 = jnp.float16
 MIB = 2**20
-STAGE_LIMIT = 42
 
 
 def params(n, limit=12):
@@ -39,34 +38,56 @@
     return (((me >> 1) + k // 2) & (half - 1)) * 2 + ((me ^ k) & 1)
 
 
-def stage_kernel(start, ids_ref, u_ref, o_ref, sem):
-    copy = pltpu.make_async_copy(u_ref.at[pl.ds(start, o_ref.shape[0])], o_ref, sem)
-    copy.start()
-    copy.wait()
-
-
-def stage_call(ids, unembed, start, count):
-    shape = (count, unembed.shape[1])
-    return pl.pallas_call(
-        functools.partial(stage_kernel, start),
-        in_specs=[smem(), pl.BlockSpec(memory_space=pltpu.HBM)],
+def tick_kernel(ids_ref, o_ref):
+    for k in range(ids_ref.shape[0]):
+        o_ref[k] = ids_ref[k]
+
+
+def tick_call(ids, nbytes):
+    return pl.pallas_call(
+        tick_kernel,
+        in_specs=[smem()],
+        out_specs=smem(),
+        out_shape=jax.ShapeDtypeStruct(ids.shape, ids.dtype),
+        compiler_params=params(0),
+        cost_estimate=cost(1000 * nbytes, nbytes),
+        name="tick",
+    )(ids)
+
+
+def part_kernel(start, *refs):
+    parts, (u_ref, o_ref, h_ref) = refs[:-3], refs[-3:]
+    at = 0
+    for part in parts:
+        h_ref[at : at + part.shape[0], :] = part[...]
+        at += part.shape[0]
+    u = u_ref[start : start + o_ref.shape[1], :]
+    o_ref[...] = jnp.dot(u, h_ref[...].T, preferred_element_type=f32).T
+
+
+def part_call(pieces, unembed, start, count):
+    width = unembed.shape[1]
+    tokens = sum(p.shape[0] for p in pieces)
+    return pl.pallas_call(
+        functools.partial(part_kernel, start),
+        in_specs=[vmem()] * (len(pieces) + 1),
         out_specs=vmem(),
-        out_shape=jax.ShapeDtypeStruct(shape, unembed.dtype),
-        scratch_shapes=[pltpu.SemaphoreType.DMA],
-        compiler_params=params(0, STAGE_LIMIT),
-        cost_estimate=cost(count * shape[1], 4 * count * shape[1]),
-        name="stage",
-    )(ids, unembed)
-
-
-def first_kernel(n, ids_ref, *refs):
+        out_shape=jax.ShapeDtypeStruct((tokens, count), f32),
+        scratch_shapes=[pltpu.VMEM((tokens, width), bf16)],
+        compiler_params=params(0),
+        cost_estimate=cost(2 * tokens * count * width, 2 * count * width),
+        name="scores_part",
+    )(*pieces, unembed)
+
+
+def first_kernel(n, start, ids_ref, *refs):
     parts, (u_ref, o_ref, h_ref, ht_ref) = refs[:n], refs[n:]
     rows = parts[0].shape[0]
     for k in range(n):
         at = pl.multiple_of(owner(ids_ref[0], k, n) * rows, rows)
         h_ref[pl.ds(at, rows), :] = parts[k][...]
     ht_ref[...] = h_ref[...].T
-    u = u_ref[: o_ref.shape[1], :]
+    u = u_ref[start : start + o_ref.shape[1], :]
     o_ref[...] = jnp.dot(u, ht_ref[...], preferred_element_type=f32).T
 
 
@@ -75,11 +96,11 @@
     o_ref[...] = jnp.dot(u, ht_ref[...], preferred_element_type=f32).T
 
 
-def first_call(ids, pieces, unembed, count):
+def first_call(ids, pieces, unembed, start, count):
     width = unembed.shape[1]
     tokens = sum(p.shape[0] for p in pieces)
     return pl.pallas_call(
-        functools.partial(first_kernel, len(pieces)),
+        functools.partial(first_kernel, len(pieces), start),
         in_specs=[smem()] + [vmem()] * (len(pieces) + 1),
         out_specs=[vmem()] * 3,
         out_shape=[
@@ -120,9 +141,17 @@
     return jnp.broadcast_to(row, (row.shape[1], row.shape[1])).T[:, :1]
 
 
-def numer_kernel(start, first, last, ids_ref, s_ref, *refs):
+def numer_kernel(start, first, last, n, groups, ids_ref, s_ref, *refs):
+    lane = 128
+    if groups:
+        rest_ref, refs, full_ref = refs[0], refs[1:-1], refs[-1]
+        for ref, group in zip((s_ref, rest_ref), groups):
+            rows = ref.shape[0] // len(group)
+            for i, k in enumerate(group):
+                at = pl.multiple_of(owner(ids_ref[0], k, n) * rows, rows)
+                full_ref[pl.ds(at, rows), :] = ref[i * rows : (i + 1) * rows, :]
+        s_ref = full_ref
     tokens, rows = s_ref.shape
-    lane = 128
     if first:
         t_ref, refs = refs[0], refs[1:]
         targets = jnp.broadcast_to(column(t_ref[...]), (tokens, lane))
@@ -154,8 +183,8 @@
             refs[0][k] = sums[k]
 
 
-def numer_call(start, first, last, ids, s, operands):
-    tokens, rows = s.shape
+def numer_call(start, first, last, n, groups, ids, scores, operands):
+    tokens, rows = sum(s.shape[0] for s in scores), scores[0].shape[1]
     out_shape = [jax.ShapeDtypeStruct((2 * tokens, rows), bf16)]
     if last:
         out_shape.append(jax.ShapeDtypeStruct((1, tokens), f32))
@@ -164,15 +193,17 @@
         out_shape.append(jax.ShapeDtypeStruct((3, tokens, 128), f32))
     if first:
         out_shape.append(jax.ShapeDtypeStruct((tokens, 128), jnp.int32))
-    return pl.pallas_call(
-        functools.partial(numer_kernel, start, first, last),
-        in_specs=[smem()] + [vmem()] * (1 + len(operands)),
+    if groups:
+        out_shape.append(jax.ShapeDtypeStruct((tokens, rows), f32))
+    return pl.pallas_call(
+        functools.partial(numer_kernel, start, first, last, n, groups),
+        in_specs=[smem()] + [vmem()] * (len(scores) + len(operands)),
         out_specs=[vmem()] * len(out_shape),
         out_shape=out_shape,
         compiler_params=params(0),
         cost_estimate=cost(40 * tokens * rows, 8 * tokens * rows),
         name="numer",
-    )(ids, s, *operands)
+    )(ids, *scores, *operands)
 
 
 def rows_kernel(block, first, places, *refs):
@@ -358,7 +389,8 @@
 
 def split(total, unit):
     tiles = total // unit
-    sizes = [1, (tiles - 2) // 2, (tiles - 3) // 2, 2]
+    sizes = [tiles // 3, (tiles - tiles // 3 - 1) // 2, 0, 1]
+    sizes[2] = tiles - sum(sizes)
     starts = [sum(sizes[:i]) for i in range(len(sizes))]
     return [(a * unit, c * unit) for a, c in zip(starts, sizes)]
 
@@ -394,26 +426,41 @@
 
     chunks = split(block_rows, 256)
     late = chunks[2][0]
-    staged = []
-    for start, count in ((0, late), *chunks[2:]):
-        staged.append(stage_call(ids, unembed, start, count))
-    places = ((0, 0), (0, chunks[1][0]), (1, 0), (2, 0))
-    scores = []
-    for c, (start, count) in enumerate(chunks):
+    staged = [unembed]
+    ids = tick_call(ids, 8 * unembed.size)
+    places = tuple((0, start) for start, _ in chunks)
+
+    def exchange(s):
+        s = s.astype(f16)
+        return s.astype(f32) + swap(s, "mp", 1, 2).astype(f32)
+
+    late = [far[-1] + 1]
+    soon = [k for k in range(n) if k not in late]
+    order = (0, 1, 2, 3)
+    scores = [None] * 4
+    part = part_call([pieces[k] for k in soon], unembed, *chunks[0])
+    most = exchange(part)
+    for c in order[1:]:
+        if c == 3:
+            part = part_call([pieces[k] for k in late], unembed, *chunks[0])
+            rest = exchange(part)
+        if c == 1:
+            s, all_hidden, turned = first_call(ids, pieces, unembed, *chunks[c])
+        else:
+            s = next_call(turned, unembed, *chunks[c])
+        scores[c] = exchange(s)
+    other_hidden = swap(all_hidden, "head", 1, 2)
+    qs, spread, so_far = [None] * 4, None, None
+    for c in (1, 2, 0, 3):
+        first, last = c == 1, c == 3
+        operands = [targets] if first else [spread, so_far]
+        parts, groups = ([most, rest], (soon, late)) if c == 0 else ([scores[c]], None)
+        qs[c], *out = numer_call(
+            chunks[c][0], first, last, n, groups, ids, parts, operands
+        )
         if c == 0:
-            s, all_hidden, turned = first_call(ids, pieces, staged[0], count)
-        else:
-            s = next_call(turned, staged[places[c][0]], places[c][1], count)
-        s = s.astype(f16)
-        scores.append(s.astype(f32) + swap(s, "mp", 1, 2).astype(f32))
-    other_hidden = swap(all_hidden, "head", 1, 2)
-    qs, spread, so_far = [], None, None
-    for c, (start, count) in enumerate(chunks):
-        last = c == len(chunks) - 1
-        operands = [spread, so_far] if c else [targets]
-        q, *out = numer_call(start, c == 0, last, ids, scores[c], operands)
-        qs.append(q)
-        if c == 0:
+            scores[0] = out.pop()
+        if first:
             so_far, spread = out
         elif not last:
             so_far = out[0]

time: 104 us -> 98.8 us (0.950)
  Pallas kernels: 46.9 us -> 40 us
  starting transfers between devices: 29.2 us -> 32.6 us
  waiting for transfers between devices: 23.7 us -> 22.2 us
    pallas_call x8, Pallas kernels: 14.6 us -> 10 us  [the longest x2 3.66 us: part_call(): pl.pallas_call(functools.partial(part_kernel, start), in_specs=[vmem()] *...]
    pallas_call x3 -> x2, Pallas kernels: 5.02 us -> 2.62 us  [next_call(): pl.pallas_call(functools.partial(next_kernel, start), in_specs=[vmem()] *...]
    ppermute x6, starting transfers between devices: 11.2 us -> 13.1 us  [slide(): lax.ppermute(x, 'seq', [(i, (i // 2 + by) % half * 2 + i % 2) for i in ra...]
    ppermute x16 -> x17, starting transfers between devices: 18 us -> 19.4 us  [swap(): return lax.ppermute(x, axis, [(i, i ^ mask) for i in range(size)])]
    ppermute x16 -> x17, waiting for transfers between devices: 15 us -> 14.3 us  [swap(): return lax.ppermute(x, axis, [(i, i ^ mask) for i in range(size)])]
  transfers between devices with their start and end apart: 22 -> 23, of which waited for: 10 -> 12; matrix products, arithmetic and copies ran while one was open for 1% -> 1% of each run, Pallas kernels for 23% -> 18%
where the time goes in v5:
time: 98.8 us; the launch traced here: 98.7 us
  Pallas kernels  40 us (40%)
  starting transfers between devices  32.6 us (33%)
  waiting for transfers between devices  22.2 us (22%)
  other arithmetic  2.84 us (3%)
  between operations  1.07 us (1%)
    ppermute x17, starting transfers between devices, swap(): return lax.ppermute(x, axis, [(i, i ^ mask) for i in range(size)])  19.4 us
    pallas_call x4, Pallas kernels, weight_call(): pl.pallas_call(functools.partial(weight_kernel, first, start, block), in_...  18.4 us
    ppermute x17, waiting for transfers between devices, swap(): return lax.ppermute(x, axis, [(i, i ^ mask) for i in range(size)])  14.3 us
    ppermute x6, starting transfers between devices, slide(): lax.ppermute(x, 'seq', [(i, (i // 2 + by) % half * 2 + i % 2) for i in ra...  13.1 us
    ppermute x6, waiting for transfers between devices, slide(): lax.ppermute(x, 'seq', [(i, (i // 2 + by) % half * 2 + i % 2) for i in ra...  7.95 us
    pallas_call x3, Pallas kernels, rows_call(): pl.pallas_call(functools.partial(rows_kernel, block, first, places), grid...  6.69 us
    pallas_call x2, Pallas kernels, part_call(): pl.pallas_call(functools.partial(part_kernel, start), in_specs=[vmem()] *...  3.66 us
    pallas_call x4, Pallas kernels, numer_call(): pl.pallas_call(functools.partial(numer_kernel, start, first, last, n, gro...  3.16 us
  transfers between devices with their start and end apart: 23, of which 12 were waited for; matrix products, arithmetic and copies ran while one was open for 1% of the time, Pallas kernels for 18%

profile of v5, /device:TPU:0, one launch (start us, length us, event | category | flops | bytes accessed | tf_op | source)
XLA Modules:
  0.0 98.7 jit_solution(13186888345598547022)
XLA Ops:
  1.6 3.1 %collective-permute-start.5 = (bf16[16,4096]{1,0:T(8,128)(2,1)S(1)}, bf16[16,4096]{1,0:T(8,128)(2,1)S(1)}, u32[]{:S(2)}, u32[]{:S(2)}) collective-permute-start(bf16[16,4096]{1,0:T(8,128)(2,1)S(1)} %fusion.refs_0_), channel_id=1, source_target_pairs={{0,4},{2,6},{4,8},{6,10},{8,12},{10,14},{12,0},{14,2},{1,5},{3,7},... | collective-permute-start | bytes 393224 | tf_op jit(solution)/shard_map/ppermute | solution.py:383
  4.7 2.6 %collective-permute-start.3 = (bf16[16,4096]{1,0:T(8,128)(2,1)S(1)}, bf16[16,4096]{1,0:T(8,128)(2,1)S(1)}, u32[]{:S(2)}, u32[]{:S(2)}) collective-permute-start(bf16[16,4096]{1,0:T(8,128)(2,1)S(1)} %fusion.refs_0_), channel_id=1, source_target_pairs={{0,8},{2,10},{4,12},{6,14},{8,0},{10,2},{12,4},{14,6},{1,9},{3,11}... | collective-permute-start | bytes 393224 | tf_op jit(solution)/shard_map/ppermute | solution.py:383
  11.2 1.7 %collective-permute-start.6 = (bf16[16,4096]{1,0:T(8,128)(2,1)S(1)}, bf16[16,4096]{1,0:T(8,128)(2,1)S(1)}, u32[]{:S(2)}, u32[]{:S(2)}) collective-permute-start(bf16[16,4096]{1,0:T(8,128)(2,1)S(1)} %collective-permute-done.5.refs_6_.refs_5_), channel_id=1, source_target_pairs={{0,2},{2,0},{4,6},{6,4},{8,10},{10,8},{12,14},{14,12},{1,3},{3,1},... | collective-permute-start | bytes 393224 | tf_op jit(solution)/shard_map/ppermute | solution.py:387
  13.0 3.0 %collective-permute-done.3.refs_4_ = bf16[16,4096]{1,0:T(8,128)(2,1)S(1)} collective-permute-done((bf16[16,4096]{1,0:T(8,128)(2,1)S(1)}, bf16[16,4096]{1,0:T(8,128)(2,1)S(1)}, u32[]{:S(2)}, u32[]{:S(2)}) %collective-permute-start.3) | collective-permute-done | bytes 131104 | tf_op jit(solution)/shard_map/ppermute | solution.py:383
  19.1 3.2 %collective-permute-done.4.refs_5_.refs_0_ = bf16[16,4096]{1,0:T(8,128)(2,1)S(1)} collective-permute-done((bf16[16,4096]{1,0:T(8,128)(2,1)S(1)}, bf16[16,4096]{1,0:T(8,128)(2,1)S(1)}, u32[]{:S(2)}, u32[]{:S(2)}) %collective-permute-start.4) | collective-permute-done | bytes 131104 | tf_op jit(solution)/shard_map/ppermute | solution.py:387
  22.4 1.8 %scores_part.3 = f32[16,768]{1,0:T(8,128)S(1)} custom-call(bf16[16,4096]{1,0:T(8,128)(2,1)S(1)} %collective-permute-done.4.refs_5_.refs_0_, bf16[2304,4096]{1,0:T(8,128)(2,1)S(1)} %bitcast.9), custom_call_target="tpu_custom_call" | custom-call | flops 100663296 | bytes 6291456 | tf_op jit(solution)/shard_map/scores_part/pallas_call | solution.py:71
  25.8 1.9 %scores_part.2 = f32[112,768]{1,0:T(8,128)S(1)} custom-call(bf16[16,4096]{1,0:T(8,128)(2,1)S(1)} %fusion.refs_0_, bf16[16,4096]{1,0:T(8,128)(2,1)S(1)} %collective-permute-done.refs_1_, bf16[16,4096]{1,0:T(8,128)(2,1)S(1)} %collective-permute-done.1.refs_2_, bf16[16,4096]{1,0:T(8,128)(2,1)S(1)} %collective-permute-done.2.refs_3_, ...), custom_call_target="tpu_custom_call" | custom-call | flops 704643072 | bytes 6291456 | tf_op jit(solution)/shard_map/scores_part/pallas_call | solution.py:71
  28.3 2.0 %scores_first.1 = (f32[128,512]{1,0:T(8,128)S(1)}, bf16[128,4096]{1,0:T(8,128)(2,1)S(1)}, bf16[4096,128]{1,0:T(8,128)(2,1)S(1)}) custom-call(s32[3]{0:T(128)S(1)} %tick.1.ids_ref, bf16[16,4096]{1,0:T(8,128)(2,1)S(1)} %fusion.refs_0_, bf16[16,4096]{1,0:T(8,128)(2,1)S(1)} %collective-permute-done.refs_1_, bf16[16,4096]{1,0:T(8,128)(2,1)S(1)} %collective-permute-done.1.refs_2_, ...), custom_call_target="tpu_custom_call" | custom-call | flops 536870912 | bytes 4194304 | tf_op jit(solution)/shard_map/scores_first/pallas_call | solution.py:102
  30.3 1.9 %scores_next.3 = f32[128,768]{1,0:T(8,128)S(1)} custom-call(bf16[4096,128]{1,0:T(8,128)(2,1)S(1)} %get-tuple-element.25.ht_ref, bf16[2304,4096]{1,0:T(8,128)(2,1)S(1)} %bitcast.9), custom_call_target="tpu_custom_call" | custom-call | flops 805306368 | bytes 6291456 | tf_op jit(solution)/shard_map/scores_next/pallas_call | solution.py:119
  33.0 1.6 %collective-permute-start.7 = (f16[128,256]{1,0:T(8,128)(2,1)S(1)}, f16[128,256]{1,0:T(8,128)(2,1)S(1)}, u32[]{:S(2)}, u32[]{:S(2)}) collective-permute-start(f16[128,256]{1,0:T(8,128)(2,1)S(1)} %convert_element_type.97), channel_id=1, source_target_pairs={{0,1},{1,0},{2,3},{3,2},{4,5},{5,4},{6,7},{7,6},{8,9},{9,8},{10,11... | collective-permute-start | bytes 196616 | tf_op jit(solution)/shard_map/ppermute | solution.py:387
  38.0 2.0 %collective-permute-done.8 = f16[128,512]{1,0:T(8,128)(2,1)S(1)} collective-permute-done((f16[128,512]{1,0:T(8,128)(2,1)S(1)}, f16[128,512]{1,0:T(8,128)(2,1)S(1)}, u32[]{:S(2)}, u32[]{:S(2)}) %collective-permute-start.8) | collective-permute-done | bytes 131104 | tf_op jit(solution)/shard_map/ppermute | solution.py:387
  44.6 1.6 %collective-permute-start.12 = (f32[1,128]{1,0:T(1,128)S(1)}, f32[1,128]{1,0:T(1,128)S(1)}, u32[]{:S(2)}, u32[]{:S(2)}) collective-permute-start(f32[1,128]{1,0:T(1,128)S(1)} %get-tuple-element.31), channel_id=1, source_target_pairs={{0,2},{2,0},{4,6},{6,4},{8,10},{10,8},{12,14},{14,12},{1,3},{3,1},... | collective-permute-start | bytes 1544 | tf_op jit(solution)/shard_map/ppermute | solution.py:387
  46.2 2.5 %rows.5.refs_2_ = f32[256,1536]{1,0:T(8,128)S(1)} custom-call(bf16[256,768]{1,0:T(8,128)(2,1)S(1)} %get-tuple-element.33.refs_0_, bf16[256,512]{1,0:T(8,128)(2,1)S(1)} %get-tuple-element.34.refs_1_, bf16[256,768]{1,0:T(8,128)(2,1)S(1)} %get-tuple-element.35.refs_2_, bf16[256,256]{1,0:T(8,128)(2,1)S(1)} %get-tuple-element.36.refs_3_, ...), custom_call_target="tpu_custom_call" | custom-call | flops 1811939328 | bytes 7077888 | tf_op jit(solution)/shard_map/rows/pallas_call | solution.py:224
  48.7 2.0 %collective-permute-start.13 = (f32[1,128]{1,0:T(1,128)S(1)}, f32[1,128]{1,0:T(1,128)S(1)}, u32[]{:S(2)}, u32[]{:S(2)}) collective-permute-start(f32[1,128]{1,0:T(1,128)S(1)} %add.57), channel_id=1, source_target_pairs={{0,4},{2,6},{4,0},{6,2},{8,12},{10,14},{12,8},{14,10},{1,5},{3,7},... | collective-permute-start | bytes 1544 | tf_op jit(solution)/shard_map/ppermute | solution.py:387
  50.7 2.5 %rows.3.refs_0_ = f32[256,1536]{1,0:T(8,128)S(1)} custom-call(bf16[256,768]{1,0:T(8,128)(2,1)S(1)} %get-tuple-element.33.refs_0_, bf16[256,512]{1,0:T(8,128)(2,1)S(1)} %get-tuple-element.34.refs_1_, bf16[256,768]{1,0:T(8,128)(2,1)S(1)} %get-tuple-element.35.refs_2_, bf16[256,256]{1,0:T(8,128)(2,1)S(1)} %get-tuple-element.36.refs_3_, ...), custom_call_target="tpu_custom_call" | custom-call | flops 1811939328 | bytes 7077888 | tf_op jit(solution)/shard_map/rows/pallas_call | solution.py:224
  53.2 2.0 %collective-permute-start.14 = (f32[1,128]{1,0:T(1,128)S(1)}, f32[1,128]{1,0:T(1,128)S(1)}, u32[]{:S(2)}, u32[]{:S(2)}) collective-permute-start(f32[1,128]{1,0:T(1,128)S(1)} %add.58), channel_id=1, source_target_pairs={{0,8},{2,10},{4,12},{6,14},{8,0},{10,2},{12,4},{14,6},{1,9},{3,11}... | collective-permute-start | bytes 1544 | tf_op jit(solution)/shard_map/ppermute | solution.py:387
  55.2 1.7 %rows.4.refs_1_ = f32[256,1024]{1,0:T(8,128)S(1)} custom-call(bf16[256,768]{1,0:T(8,128)(2,1)S(1)} %get-tuple-element.33.refs_0_, bf16[256,512]{1,0:T(8,128)(2,1)S(1)} %get-tuple-element.34.refs_1_, bf16[256,768]{1,0:T(8,128)(2,1)S(1)} %get-tuple-element.35.refs_2_, bf16[256,256]{1,0:T(8,128)(2,1)S(1)} %get-tuple-element.36.refs_3_, ...), custom_call_target="tpu_custom_call" | custom-call | flops 1207959552 | bytes 4718592 | tf_op jit(solution)/shard_map/rows/pallas_call | solution.py:224
  60.9 4.3 %collective-permute-done.15 = bf16[32,4096]{1,0:T(8,128)(2,1)S(1)} collective-permute-done((bf16[32,4096]{1,0:T(8,128)(2,1)S(1)}, bf16[32,4096]{1,0:T(8,128)(2,1)S(1)}, u32[]{:S(2)}, u32[]{:S(2)}) %collective-permute-start.15) | collective-permute-done | bytes 262176 | tf_op jit(solution)/shard_map/ppermute | solution.py:387
  65.3 2.0 %collective-permute-start.16 = (bf16[16,4096]{1,0:T(8,128)(2,1)S(1)}, bf16[16,4096]{1,0:T(8,128)(2,1)S(1)}, u32[]{:S(2)}, u32[]{:S(2)}) collective-permute-start(bf16[16,4096]{1,0:T(8,128)(2,1)S(1)} %get-tuple-element.49), channel_id=1, source_target_pairs={{0,8},{2,10},{4,12},{6,14},{8,0},{10,2},{12,4},{14,6},{1,9},{3,11}... | collective-permute-start | bytes 393224 | tf_op jit(solution)/shard_map/ppermute | solution.py:383
  68.4 3.1 %collective-permute-start.19 = (bf16[16,4096]{1,0:T(8,128)(2,1)S(1)}, bf16[16,4096]{1,0:T(8,128)(2,1)S(1)}, u32[]{:S(2)}, u32[]{:S(2)}) collective-permute-start(bf16[16,4096]{1,0:T(8,128)(2,1)S(1)} %add_convert_fusion.1), channel_id=1, source_target_pairs={{0,12},{2,14},{4,0},{6,2},{8,4},{10,6},{12,8},{14,10},{1,13},{3,15... | collective-permute-start | bytes 393224 | tf_op jit(solution)/shard_map/ppermute | solution.py:383
  80.1 7.0 %weight.4 = (f32[2304,4096]{1,0:T(8,128)}, bf16[256,4096]{1,0:T(8,128)(2,1)S(1)}) custom-call(s32[3]{0:T(128)S(1)} %tick.1.ids_ref, bf16[128,2304]{1,0:T(8,128)(2,1)S(1)} %grads.1.refs_0_, bf16[128,2304]{1,0:T(8,128)(2,1)S(1)} %collective-permute-done.21.refs_1_, bf16[128,4096]{1,0:T(8,128)(2,1)S(1)} %get-tuple-element.44.refs_2_, ...), custom_call_target="tpu_custom_call" | custom-call | flops 2147483648 | bytes 16777216 | tf_op jit(solution)/shard_map/weight/pallas_call | solution.py:364
  87.1 2.9 %weight.5.refs_3_ = f32[2304,4096]{1,0:T(8,128)} custom-call(s32[3]{0:T(128)S(1)} %tick.1.ids_ref, bf16[128,2304]{1,0:T(8,128)(2,1)S(1)} %grads.1.refs_0_, bf16[128,2304]{1,0:T(8,128)(2,1)S(1)} %collective-permute-done.21.refs_1_, bf16[256,4096]{1,0:T(8,128)(2,1)S(1)} %get-tuple-element.45.refs_2_, ...), custom_call_target="tpu_custom_call", output_to_operand_aliasing={{}: (4, {})} | custom-call | flops 536870912 | bytes 4194304 | tf_op jit(solution)/shard_map/weight/pallas_call | solution.py:364
  90.0 5.6 %weight.6.refs_3_ = f32[2304,4096]{1,0:T(8,128)} custom-call(s32[3]{0:T(128)S(1)} %tick.1.ids_ref, bf16[128,2304]{1,0:T(8,128)(2,1)S(1)} %grads.1.refs_0_, bf16[128,2304]{1,0:T(8,128)(2,1)S(1)} %collective-permute-done.21.refs_1_, bf16[256,4096]{1,0:T(8,128)(2,1)S(1)} %get-tuple-element.45.refs_2_, ...), custom_call_target="tpu_custom_call", output_to_operand_aliasing={{}: (4, {})} | custom-call | flops 1610612736 | bytes 12582912 | tf_op jit(solution)/shard_map/weight/pallas_call | solution.py:364
  95.6 2.9 %weight.7 = f32[2304,4096]{1,0:T(8,128)} custom-call(s32[3]{0:T(128)S(1)} %tick.1.ids_ref, bf16[128,2304]{1,0:T(8,128)(2,1)S(1)} %grads.1.refs_0_, bf16[128,2304]{1,0:T(8,128)(2,1)S(1)} %collective-permute-done.21.refs_1_, bf16[256,4096]{1,0:T(8,128)(2,1)S(1)} %get-tuple-element.45.refs_2_, f32[2304,4096]{1,0:T(8,128)} %weight.6.refs_3_), custom_call_target="tpu_custom_call", output_to_operand_aliasing={{}: (4, {})} | custom-call | flops 536870912 | bytes 4194304 | tf_op jit(solution)/shard_map/weight/pallas_call | solution.py:364
  (75 shorter events, 32.7 us)
Async XLA Ops:
  1.6 9.6 %collective-permute-start.5 = (bf16[16,4096]{1,0:T(8,128)(2,1)S(1)}, bf16[16,4096]{1,0:T(8,128)(2,1)S(1)}, u32[]{:S(2)}, u32[]{:S(2)}) collective-permute-start(bf16[16,4096]{1,0:T(8,128)(2,1)S(1)} %fusion.refs_0_), channel_id=1, source_target_pairs={{0,4},{2,6},{4,8},{6,10},{8,12},{10,14},{12,0},{14,2},{1,5},{3,7},... | collective-permute-start | bytes 393224 | tf_op jit(solution)/shard_map/ppermute | solution.py:383
  4.7 11.2 %collective-permute-start.3 = (bf16[16,4096]{1,0:T(8,128)(2,1)S(1)}, bf16[16,4096]{1,0:T(8,128)(2,1)S(1)}, u32[]{:S(2)}, u32[]{:S(2)}) collective-permute-start(bf16[16,4096]{1,0:T(8,128)(2,1)S(1)} %fusion.refs_0_), channel_id=1, source_target_pairs={{0,8},{2,10},{4,12},{6,14},{8,0},{10,2},{12,4},{14,6},{1,9},{3,11}... | collective-permute-start | bytes 393224 | tf_op jit(solution)/shard_map/ppermute | solution.py:383
  7.3 10.2 %collective-permute-start.1 = (bf16[16,4096]{1,0:T(8,128)(2,1)S(1)}, bf16[16,4096]{1,0:T(8,128)(2,1)S(1)}, u32[]{:S(2)}, u32[]{:S(2)}) collective-permute-start(bf16[16,4096]{1,0:T(8,128)(2,1)S(1)} %fusion.refs_0_), channel_id=1, source_target_pairs={{0,12},{2,14},{4,0},{6,2},{8,4},{10,6},{12,8},{14,10},{1,13},{3,15... | collective-permute-start | bytes 393224 | tf_op jit(solution)/shard_map/ppermute | solution.py:383
  8.7 17.1 %collective-permute-start = (bf16[16,4096]{1,0:T(8,128)(2,1)S(1)}, bf16[16,4096]{1,0:T(8,128)(2,1)S(1)}, u32[]{:S(2)}, u32[]{:S(2)}) collective-permute-start(bf16[16,4096]{1,0:T(8,128)(2,1)S(1)} %fusion.refs_0_), channel_id=1, source_target_pairs={{0,2},{2,0},{4,6},{6,4},{8,10},{10,8},{12,14},{14,12},{1,3},{3,1},... | collective-permute-start | bytes 393224 | tf_op jit(solution)/shard_map/ppermute | solution.py:387
  11.2 14.5 %collective-permute-start.6 = (bf16[16,4096]{1,0:T(8,128)(2,1)S(1)}, bf16[16,4096]{1,0:T(8,128)(2,1)S(1)}, u32[]{:S(2)}, u32[]{:S(2)}) collective-permute-start(bf16[16,4096]{1,0:T(8,128)(2,1)S(1)} %collective-permute-done.5.refs_6_.refs_5_), channel_id=1, source_target_pairs={{0,2},{2,0},{4,6},{6,4},{8,10},{10,8},{12,14},{14,12},{1,3},{3,1},... | collective-permute-start | bytes 393224 | tf_op jit(solution)/shard_map/ppermute | solution.py:387
  16.0 6.4 %collective-permute-start.4 = (bf16[16,4096]{1,0:T(8,128)(2,1)S(1)}, bf16[16,4096]{1,0:T(8,128)(2,1)S(1)}, u32[]{:S(2)}, u32[]{:S(2)}) collective-permute-start(bf16[16,4096]{1,0:T(8,128)(2,1)S(1)} %collective-permute-done.3.refs_4_), channel_id=1, source_target_pairs={{0,2},{2,0},{4,6},{6,4},{8,10},{10,8},{12,14},{14,12},{1,3},{3,1},... | collective-permute-start | bytes 393224 | tf_op jit(solution)/shard_map/ppermute | solution.py:387
  17.5 8.3 %collective-permute-start.2 = (bf16[16,4096]{1,0:T(8,128)(2,1)S(1)}, bf16[16,4096]{1,0:T(8,128)(2,1)S(1)}, u32[]{:S(2)}, u32[]{:S(2)}) collective-permute-start(bf16[16,4096]{1,0:T(8,128)(2,1)S(1)} %collective-permute-done.1.refs_2_), channel_id=1, source_target_pairs={{0,2},{2,0},{4,6},{6,4},{8,10},{10,8},{12,14},{14,12},{1,3},{3,1},... | collective-permute-start | bytes 393224 | tf_op jit(solution)/shard_map/ppermute | solution.py:387
  24.2 12.5 %collective-permute-start.10 = (f16[16,768]{1,0:T(8,128)(2,1)S(1)}, f16[16,768]{1,0:T(8,128)(2,1)S(1)}, u32[]{:S(2)}, u32[]{:S(2)}) collective-permute-start(f16[16,768]{1,0:T(8,128)(2,1)S(1)} %convert_element_type.106), channel_id=1, source_target_pairs={{0,1},{1,0},{2,3},{3,2},{4,5},{5,4},{6,7},{7,6},{8,9},{9,8},{10,11... | collective-permute-start | bytes 73736 | tf_op jit(solution)/shard_map/ppermute | solution.py:387
  27.7 13.2 %collective-permute-start.9 = (f16[112,768]{1,0:T(8,128)(2,1)S(1)}, f16[112,768]{1,0:T(8,128)(2,1)S(1)}, u32[]{:S(2)}, u32[]{:S(2)}) collective-permute-start(f16[112,768]{1,0:T(8,128)(2,1)S(1)} %convert_element_type.103), channel_id=1, source_target_pairs={{0,1},{1,0},{2,3},{3,2},{4,5},{5,4},{6,7},{7,6},{8,9},{9,8},{10,11... | collective-permute-start | bytes 516104 | tf_op jit(solution)/shard_map/ppermute | solution.py:387
  32.9 24.8 %copy-start = (f32[1,128]{1,0:T(1,128)S(1)}, f32[1,128]{1,0:T(1,128)}, u32[]{:S(2)}) copy-start(f32[1,128]{1,0:T(1,128)} %lg_ref.3) | copy-start | bytes 1540
  33.0 5.0 %collective-permute-start.7 = (f16[128,256]{1,0:T(8,128)(2,1)S(1)}, f16[128,256]{1,0:T(8,128)(2,1)S(1)}, u32[]{:S(2)}, u32[]{:S(2)}) collective-permute-start(f16[128,256]{1,0:T(8,128)(2,1)S(1)} %convert_element_type.97), channel_id=1, source_target_pairs={{0,1},{1,0},{2,3},{3,2},{4,5},{5,4},{6,7},{7,6},{8,9},{9,8},{10,11... | collective-permute-start | bytes 196616 | tf_op jit(solution)/shard_map/ppermute | solution.py:387
  34.5 5.5 %collective-permute-start.8 = (f16[128,512]{1,0:T(8,128)(2,1)S(1)}, f16[128,512]{1,0:T(8,128)(2,1)S(1)}, u32[]{:S(2)}, u32[]{:S(2)}) collective-permute-start(f16[128,512]{1,0:T(8,128)(2,1)S(1)} %convert_element_type.100), channel_id=1, source_target_pairs={{0,1},{1,0},{2,3},{3,2},{4,5},{5,4},{6,7},{7,6},{8,9},{9,8},{10,11... | collective-permute-start | bytes 393224 | tf_op jit(solution)/shard_map/ppermute | solution.py:387
  35.2 7.0 %collective-permute-start.11 = (f16[128,768]{1,0:T(8,128)(2,1)S(1)}, f16[128,768]{1,0:T(8,128)(2,1)S(1)}, u32[]{:S(2)}, u32[]{:S(2)}) collective-permute-start(f16[128,768]{1,0:T(8,128)(2,1)S(1)} %convert_element_type.109), channel_id=1, source_target_pairs={{0,1},{1,0},{2,3},{3,2},{4,5},{5,4},{6,7},{7,6},{8,9},{9,8},{10,11... | collective-permute-start | bytes 589832 | tf_op jit(solution)/shard_map/ppermute | solution.py:387
  44.6 4.1 %collective-permute-start.12 = (f32[1,128]{1,0:T(1,128)S(1)}, f32[1,128]{1,0:T(1,128)S(1)}, u32[]{:S(2)}, u32[]{:S(2)}) collective-permute-start(f32[1,128]{1,0:T(1,128)S(1)} %get-tuple-element.31), channel_id=1, source_target_pairs={{0,2},{2,0},{4,6},{6,4},{8,10},{10,8},{12,14},{14,12},{1,3},{3,1},... | collective-permute-start | bytes 1544 | tf_op jit(solution)/shard_map/ppermute | solution.py:387
  48.7 4.5 %collective-permute-start.13 = (f32[1,128]{1,0:T(1,128)S(1)}, f32[1,128]{1,0:T(1,128)S(1)}, u32[]{:S(2)}, u32[]{:S(2)}) collective-permute-start(f32[1,128]{1,0:T(1,128)S(1)} %add.57), channel_id=1, source_target_pairs={{0,4},{2,6},{4,0},{6,2},{8,12},{10,14},{12,8},{14,10},{1,5},{3,7},... | collective-permute-start | bytes 1544 | tf_op jit(solution)/shard_map/ppermute | solution.py:387
  53.2 4.5 %collective-permute-start.14 = (f32[1,128]{1,0:T(1,128)S(1)}, f32[1,128]{1,0:T(1,128)S(1)}, u32[]{:S(2)}, u32[]{:S(2)}) collective-permute-start(f32[1,128]{1,0:T(1,128)S(1)} %add.58), channel_id=1, source_target_pairs={{0,8},{2,10},{4,12},{6,14},{8,0},{10,2},{12,4},{14,6},{1,9},{3,11}... | collective-permute-start | bytes 1544 | tf_op jit(solution)/shard_map/ppermute | solution.py:387
  58.8 6.4 %collective-permute-start.15 = (bf16[32,4096]{1,0:T(8,128)(2,1)S(1)}, bf16[32,4096]{1,0:T(8,128)(2,1)S(1)}, u32[]{:S(2)}, u32[]{:S(2)}) collective-permute-start(bf16[32,4096]{1,0:T(8,128)(2,1)S(1)} %get-tuple-element.38), channel_id=1, source_target_pairs={{0,2},{2,0},{4,6},{6,4},{8,10},{10,8},{12,14},{14,12},{1,3},{3,1},... | collective-permute-start | bytes 786440 | tf_op jit(solution)/shard_map/ppermute | solution.py:387
  59.9 8.5 %collective-permute-start.18 = (bf16[32,4096]{1,0:T(8,128)(2,1)S(1)}, bf16[32,4096]{1,0:T(8,128)(2,1)S(1)}, u32[]{:S(2)}, u32[]{:S(2)}) collective-permute-start(bf16[32,4096]{1,0:T(8,128)(2,1)S(1)} %get-tuple-element.41), channel_id=1, source_target_pairs={{0,2},{2,0},{4,6},{6,4},{8,10},{10,8},{12,14},{14,12},{1,3},{3,1},... | collective-permute-start | bytes 786440 | tf_op jit(solution)/shard_map/ppermute | solution.py:387
  65.3 7.4 %collective-permute-start.16 = (bf16[16,4096]{1,0:T(8,128)(2,1)S(1)}, bf16[16,4096]{1,0:T(8,128)(2,1)S(1)}, u32[]{:S(2)}, u32[]{:S(2)}) collective-permute-start(bf16[16,4096]{1,0:T(8,128)(2,1)S(1)} %get-tuple-element.49), channel_id=1, source_target_pairs={{0,8},{2,10},{4,12},{6,14},{8,0},{10,2},{12,4},{14,6},{1,9},{3,11}... | collective-permute-start | bytes 393224 | tf_op jit(solution)/shard_map/ppermute | solution.py:383
  67.4 6.9 %collective-permute-start.17 = (bf16[16,4096]{1,0:T(8,128)(2,1)S(1)}, bf16[16,4096]{1,0:T(8,128)(2,1)S(1)}, u32[]{:S(2)}, u32[]{:S(2)}) collective-permute-start(bf16[16,4096]{1,0:T(8,128)(2,1)S(1)} %get-tuple-element.50), channel_id=1, source_target_pairs={{0,4},{2,6},{4,8},{6,10},{8,12},{10,14},{12,0},{14,2},{1,5},{3,7},... | collective-permute-start | bytes 393224 | tf_op jit(solution)/shard_map/ppermute | solution.py:383
  68.4 7.1 %collective-permute-start.19 = (bf16[16,4096]{1,0:T(8,128)(2,1)S(1)}, bf16[16,4096]{1,0:T(8,128)(2,1)S(1)}, u32[]{:S(2)}, u32[]{:S(2)}) collective-permute-start(bf16[16,4096]{1,0:T(8,128)(2,1)S(1)} %add_convert_fusion.1), channel_id=1, source_target_pairs={{0,12},{2,14},{4,0},{6,2},{8,4},{10,6},{12,8},{14,10},{1,13},{3,15... | collective-permute-start | bytes 393224 | tf_op jit(solution)/shard_map/ppermute | solution.py:383
  76.2 1.8 %collective-permute-start.20 = (f32[16,4096]{1,0:T(8,128)S(1)}, f32[16,4096]{1,0:T(8,128)S(1)}, u32[]{:S(2)}, u32[]{:S(2)}) collective-permute-start(f32[16,4096]{1,0:T(8,128)S(1)} %get-tuple-element.48), channel_id=1, source_target_pairs={{0,16},{16,0},{1,17},{17,1},{2,18},{18,2},{3,19},{19,3},{4,20},{20... | collective-permute-start | bytes 786440 | tf_op jit(solution)/shard_map/ppermute | solution.py:387
  76.2 3.9 %collective-permute-start.22 = (bf16[128,4096]{1,0:T(8,128)(2,1)S(1)}, bf16[128,4096]{1,0:T(8,128)(2,1)S(1)}, u32[]{:S(2)}, u32[]{:S(2)}) collective-permute-start(bf16[128,4096]{1,0:T(8,128)(2,1)S(1)} %get-tuple-element.44.refs_2_), channel_id=1, source_target_pairs={{0,16},{16,0},{1,17},{17,1},{2,18},{18,2},{3,19},{19,3},{4,20},{20... | collective-permute-start | bytes 3145736 | tf_op jit(solution)/shard_map/ppermute | solution.py:387
  77.9 2.2 %collective-permute-start.21 = (bf16[128,2304]{1,0:T(8,128)(2,1)S(1)}, bf16[128,2304]{1,0:T(8,128)(2,1)S(1)}, u32[]{:S(2)}, u32[]{:S(2)}) collective-permute-start(bf16[128,2304]{1,0:T(8,128)(2,1)S(1)} %grads.1.refs_0_), channel_id=1, source_target_pairs={{0,16},{16,0},{1,17},{17,1},{2,18},{18,2},{3,19},{19,3},{4,20},{20... | collective-permute-start | bytes 1769480 | tf_op jit(solution)/shard_map/ppermute | solution.py:387
  (6 other events, 76.3 us)

commit v6 on v5

--- a/solution.py
+++ b/solution.py
@@ -160,11 +160,12 @@
         spread_ref, so_far_ref, refs = refs[0], refs[1], refs[2:]
         targets = spread_ref[...]
         sums = [so_far_ref[k] for k in range(3)]
-    q_ref, refs = refs[0], refs[1:]
+    q_ref, p_ref, refs = refs[0], refs[1], refs[2:]
     for j in range(0, rows, lane):
         e, d = soften(s_ref[:, j : j + lane])
         hit = hits(ids_ref[2] + (start + j), targets, e.shape)
         q = e * d
+        p_ref[:, j : j + lane] = q
         q_ref[:tokens, j : j + lane] = jnp.where(hit, 0.0, q).astype(bf16)
         q_ref[tokens:, j : j + lane] = jnp.where(hit, 1.0, 0.0).astype(bf16)
         sums[0] = sums[0] + e
@@ -185,7 +186,10 @@
 
 def numer_call(start, first, last, n, groups, ids, scores, operands):
     tokens, rows = sum(s.shape[0] for s in scores), scores[0].shape[1]
-    out_shape = [jax.ShapeDtypeStruct((2 * tokens, rows), bf16)]
+    out_shape = [
+        jax.ShapeDtypeStruct((2 * tokens, rows), bf16),
+        jax.ShapeDtypeStruct((tokens, rows), f32),
+    ]
     if last:
         out_shape.append(jax.ShapeDtypeStruct((1, tokens), f32))
         out_shape.append(jax.ShapeDtypeStruct((2, tokens), f32))
@@ -193,13 +197,12 @@
         out_shape.append(jax.ShapeDtypeStruct((3, tokens, 128), f32))
     if first:
         out_shape.append(jax.ShapeDtypeStruct((tokens, 128), jnp.int32))
-    if groups:
-        out_shape.append(jax.ShapeDtypeStruct((tokens, rows), f32))
     return pl.pallas_call(
         functools.partial(numer_kernel, start, first, last, n, groups),
         in_specs=[smem()] + [vmem()] * (len(scores) + len(operands)),
         out_specs=[vmem()] * len(out_shape),
         out_shape=out_shape,
+        scratch_shapes=[pltpu.VMEM((tokens, rows), f32)] if groups else [],
         compiler_params=params(0),
         cost_estimate=cost(40 * tokens * rows, 8 * tokens * rows),
         name="numer",
@@ -281,34 +284,33 @@
     )(ids, total, stats, loss_grad, *sums)
 
 
-def grads_kernel(count, ids_ref, t_ref, tot_ref, lg_ref, *refs):
-    g_ref = refs[count]
-    inv = column(1.0 / tot_ref[...])
-    lg = column(lg_ref[...])
+def grads_kernel(ids_ref, t_ref, tot_ref, stat_ref, lg_ref, *refs):
+    g_ref = refs[-1]
+    scale = column(lg_ref[...] / tot_ref[...])
+    peak = column(lg_ref[...] * stat_ref[1:2, :])
     targets = t_ref[...]
     step = 128
     at = 0
-    for s_ref in refs[:count]:
-        for j in range(0, s_ref.shape[1], step):
-            e, d = soften(s_ref[:, j : j + step])
-            hit = hits(ids_ref[2] + at, targets, e.shape)
-            p = jnp.where(hit, e * inv - 1.0, e * inv)
-            g_ref[:, at : at + step] = (lg * p * d).astype(bf16)
+    for p_ref in refs[:-1]:
+        for j in range(0, p_ref.shape[1], step):
+            p = scale * p_ref[:, j : j + step]
+            hit = hits(ids_ref[2] + at, targets, p.shape)
+            g_ref[:, at : at + step] = jnp.where(hit, p - peak, p).astype(bf16)
             at += step
 
 
-def grads_call(ids, scores, targets, total, loss_grad):
+def grads_call(ids, numers, targets, total, stats, loss_grad):
     tokens = total.shape[1]
-    rows = sum(s.shape[1] for s in scores)
-    return pl.pallas_call(
-        functools.partial(grads_kernel, len(scores)),
-        in_specs=[smem()] + [vmem()] * (3 + len(scores)),
+    rows = sum(p.shape[1] for p in numers)
+    return pl.pallas_call(
+        grads_kernel,
+        in_specs=[smem()] + [vmem()] * (4 + len(numers)),
         out_specs=vmem(),
         out_shape=jax.ShapeDtypeStruct((tokens, rows), bf16),
         compiler_params=params(0),
-        cost_estimate=cost(40 * tokens * rows, 6 * tokens * rows),
+        cost_estimate=cost(4 * tokens * rows, 6 * tokens * rows),
         name="grads",
-    )(ids, targets, total, loss_grad, *scores)
+    )(ids, targets, total, stats, loss_grad, *numers)
 
 
 def weight_kernel(first, start, block, ids_ref, *refs):
@@ -359,7 +361,7 @@
     out_shape = [jax.ShapeDtypeStruct((rows, width), f32)]
     if first:
         out_shape.append(jax.ShapeDtypeStruct((2 * tokens, width), bf16))
-    across = 4
+    across = 8
     steps = count // block * across
     return pl.pallas_call(
         functools.partial(weight_kernel, first, start, block),
@@ -397,7 +399,7 @@
 
 def portions(total, unit):
     tiles = total // unit
-    sizes = [tiles - tiles // 3 - 2, 1, tiles // 3, 1]
+    sizes = [tiles // 2, tiles - tiles // 2 - 1, 1]
     starts = [sum(sizes[:i]) for i in range(len(sizes))]
     return [(a * unit, c * unit) for a, c in zip(starts, sizes)]
 
@@ -450,16 +452,14 @@
             s = next_call(turned, unembed, *chunks[c])
         scores[c] = exchange(s)
     other_hidden = swap(all_hidden, "head", 1, 2)
-    qs, spread, so_far = [None] * 4, None, None
+    qs, ps, spread, so_far = [None] * 4, [None] * 4, None, None
     for c in (1, 2, 0, 3):
         first, last = c == 1, c == 3
         operands = [targets] if first else [spread, so_far]
         parts, groups = ([most, rest], (soon, late)) if c == 0 else ([scores[c]], None)
-        qs[c], *out = numer_call(
+        qs[c], ps[c], *out = numer_call(
             chunks[c][0], first, last, n, groups, ids, parts, operands
         )
-        if c == 0:
-            scores[0] = out.pop()
         if first:
             so_far, spread = out
         elif not last:
@@ -485,11 +485,12 @@
             got.append(both)
     row_grad = functools.reduce(lambda a, b: a + b, got)
 
-    g = grads_call(ids, scores, spread, total, loss_grad)
+    g = grads_call(ids, ps, spread, total, stats, loss_grad)
     g_other = swap(g, "head", 1, 2)
     d_unembed, hs = None, [all_hidden, other_hidden]
-    for p, (start, count) in enumerate(portions(block_rows, 256)):
-        out = weight_call(ids, g, g_other, hs, start, count, 256, d_unembed)
+    for p, (start, count) in enumerate(portions(block_rows, 128)):
+        block = 128 if count % 256 else 256
+        out = weight_call(ids, g, g_other, hs, start, count, block, d_unembed)
         d_unembed = out[0]
         if p == 0:
             hs = out[1:]

time: 98.8 us -> 97.5 us (0.987)
  Pallas kernels: 40 us -> 38.4 us
    pallas_call x4 -> x3, Pallas kernels: 18.4 us -> 17.1 us  [weight_call(): pl.pallas_call(functools.partial(weight_kernel, first, start, block), in_...]
  transfers between devices with their start and end apart: 23 -> 23, of which waited for: 12 -> 13; matrix products, arithmetic and copies ran while one was open for 1% -> 1% of each run, Pallas kernels for 18% -> 18%
where the time goes in v6:
time: 97.5 us; the launch traced here: 97.3 us
  Pallas kernels  38.4 us (39%)
  starting transfers between devices  32.5 us (33%)
  waiting for transfers between devices  22.5 us (23%)
  other arithmetic  2.85 us (3%)
  between operations  1.06 us (1%)
    ppermute x17, starting transfers between devices, swap(): return lax.ppermute(x, axis, [(i, i ^ mask) for i in range(size)])  19.4 us
    pallas_call x3, Pallas kernels, weight_call(): pl.pallas_call(functools.partial(weight_kernel, first, start, block), in_...  17.1 us
    ppermute x17, waiting for transfers between devices, swap(): return lax.ppermute(x, axis, [(i, i ^ mask) for i in range(size)])  14.6 us
    ppermute x6, starting transfers between devices, slide(): lax.ppermute(x, 'seq', [(i, (i // 2 + by) % half * 2 + i % 2) for i in ra...  13.1 us
    ppermute x6, waiting for transfers between devices, slide(): lax.ppermute(x, 'seq', [(i, (i // 2 + by) % half * 2 + i % 2) for i in ra...  7.95 us
    pallas_call x3, Pallas kernels, rows_call(): pl.pallas_call(functools.partial(rows_kernel, block, first, places), grid...  6.69 us
    pallas_call x2, Pallas kernels, part_call(): pl.pallas_call(functools.partial(part_kernel, start), in_specs=[vmem()] *...  3.66 us
    pallas_call x4, Pallas kernels, numer_call(): pl.pallas_call(functools.partial(numer_kernel, start, first, last, n, gro...  3.19 us
  transfers between devices with their start and end apart: 23, of which 13 were waited for; matrix products, arithmetic and copies ran while one was open for 1% of the time, Pallas kernels for 18%

profile of v6, /device:TPU:0, one launch (start us, length us, event | category | flops | bytes accessed | tf_op | source)
XLA Modules:
  0.0 97.3 jit_solution(18045067412385679238)
XLA Ops:
  1.6 3.1 %collective-permute-start.5 = (bf16[16,4096]{1,0:T(8,128)(2,1)S(1)}, bf16[16,4096]{1,0:T(8,128)(2,1)S(1)}, u32[]{:S(2)}, u32[]{:S(2)}) collective-permute-start(bf16[16,4096]{1,0:T(8,128)(2,1)S(1)} %fusion.refs_0_), channel_id=1, source_target_pairs={{0,4},{2,6},{4,8},{6,10},{8,12},{10,14},{12,0},{14,2},{1,5},{3,7},... | collective-permute-start | bytes 393224 | tf_op jit(solution)/shard_map/ppermute | solution.py:385
  4.7 2.6 %collective-permute-start.3 = (bf16[16,4096]{1,0:T(8,128)(2,1)S(1)}, bf16[16,4096]{1,0:T(8,128)(2,1)S(1)}, u32[]{:S(2)}, u32[]{:S(2)}) collective-permute-start(bf16[16,4096]{1,0:T(8,128)(2,1)S(1)} %fusion.refs_0_), channel_id=1, source_target_pairs={{0,8},{2,10},{4,12},{6,14},{8,0},{10,2},{12,4},{14,6},{1,9},{3,11}... | collective-permute-start | bytes 393224 | tf_op jit(solution)/shard_map/ppermute | solution.py:385
  11.2 1.7 %collective-permute-start.6 = (bf16[16,4096]{1,0:T(8,128)(2,1)S(1)}, bf16[16,4096]{1,0:T(8,128)(2,1)S(1)}, u32[]{:S(2)}, u32[]{:S(2)}) collective-permute-start(bf16[16,4096]{1,0:T(8,128)(2,1)S(1)} %collective-permute-done.5.refs_6_.refs_5_), channel_id=1, source_target_pairs={{0,2},{2,0},{4,6},{6,4},{8,10},{10,8},{12,14},{14,12},{1,3},{3,1},... | collective-permute-start | bytes 393224 | tf_op jit(solution)/shard_map/ppermute | solution.py:389
  13.0 3.0 %collective-permute-done.3.refs_4_ = bf16[16,4096]{1,0:T(8,128)(2,1)S(1)} collective-permute-done((bf16[16,4096]{1,0:T(8,128)(2,1)S(1)}, bf16[16,4096]{1,0:T(8,128)(2,1)S(1)}, u32[]{:S(2)}, u32[]{:S(2)}) %collective-permute-start.3) | collective-permute-done | bytes 131104 | tf_op jit(solution)/shard_map/ppermute | solution.py:385
  19.1 3.2 %collective-permute-done.4.refs_5_.refs_0_ = bf16[16,4096]{1,0:T(8,128)(2,1)S(1)} collective-permute-done((bf16[16,4096]{1,0:T(8,128)(2,1)S(1)}, bf16[16,4096]{1,0:T(8,128)(2,1)S(1)}, u32[]{:S(2)}, u32[]{:S(2)}) %collective-permute-start.4) | collective-permute-done | bytes 131104 | tf_op jit(solution)/shard_map/ppermute | solution.py:389
  22.4 1.8 %scores_part.3 = f32[16,768]{1,0:T(8,128)S(1)} custom-call(bf16[16,4096]{1,0:T(8,128)(2,1)S(1)} %collective-permute-done.4.refs_5_.refs_0_, bf16[2304,4096]{1,0:T(8,128)(2,1)S(1)} %bitcast.9), custom_call_target="tpu_custom_call" | custom-call | flops 100663296 | bytes 6291456 | tf_op jit(solution)/shard_map/scores_part/pallas_call | solution.py:71
  25.7 1.9 %scores_part.2 = f32[112,768]{1,0:T(8,128)S(1)} custom-call(bf16[16,4096]{1,0:T(8,128)(2,1)S(1)} %fusion.refs_0_, bf16[16,4096]{1,0:T(8,128)(2,1)S(1)} %collective-permute-done.refs_1_, bf16[16,4096]{1,0:T(8,128)(2,1)S(1)} %collective-permute-done.1.refs_2_, bf16[16,4096]{1,0:T(8,128)(2,1)S(1)} %collective-permute-done.2.refs_3_, ...), custom_call_target="tpu_custom_call" | custom-call | flops 704643072 | bytes 6291456 | tf_op jit(solution)/shard_map/scores_part/pallas_call | solution.py:71
  28.2 2.0 %scores_first.1 = (f32[128,512]{1,0:T(8,128)S(1)}, bf16[128,4096]{1,0:T(8,128)(2,1)S(1)}, bf16[4096,128]{1,0:T(8,128)(2,1)S(1)}) custom-call(s32[3]{0:T(128)S(1)} %tick.1.ids_ref, bf16[16,4096]{1,0:T(8,128)(2,1)S(1)} %fusion.refs_0_, bf16[16,4096]{1,0:T(8,128)(2,1)S(1)} %collective-permute-done.refs_1_, bf16[16,4096]{1,0:T(8,128)(2,1)S(1)} %collective-permute-done.1.refs_2_, ...), custom_call_target="tpu_custom_call" | custom-call | flops 536870912 | bytes 4194304 | tf_op jit(solution)/shard_map/scores_first/pallas_call | solution.py:102
  30.3 1.8 %scores_next.3 = f32[128,768]{1,0:T(8,128)S(1)} custom-call(bf16[4096,128]{1,0:T(8,128)(2,1)S(1)} %get-tuple-element.28.ht_ref, bf16[2304,4096]{1,0:T(8,128)(2,1)S(1)} %bitcast.9), custom_call_target="tpu_custom_call" | custom-call | flops 805306368 | bytes 6291456 | tf_op jit(solution)/shard_map/scores_next/pallas_call | solution.py:119
  32.9 1.6 %collective-permute-start.7 = (f16[128,256]{1,0:T(8,128)(2,1)S(1)}, f16[128,256]{1,0:T(8,128)(2,1)S(1)}, u32[]{:S(2)}, u32[]{:S(2)}) collective-permute-start(f16[128,256]{1,0:T(8,128)(2,1)S(1)} %convert_element_type.97), channel_id=1, source_target_pairs={{0,1},{1,0},{2,3},{3,2},{4,5},{5,4},{6,7},{7,6},{8,9},{9,8},{10,11... | collective-permute-start | bytes 196616 | tf_op jit(solution)/shard_map/ppermute | solution.py:389
  38.0 2.0 %collective-permute-done.8 = f16[128,512]{1,0:T(8,128)(2,1)S(1)} collective-permute-done((f16[128,512]{1,0:T(8,128)(2,1)S(1)}, f16[128,512]{1,0:T(8,128)(2,1)S(1)}, u32[]{:S(2)}, u32[]{:S(2)}) %collective-permute-start.8) | collective-permute-done | bytes 131104 | tf_op jit(solution)/shard_map/ppermute | solution.py:389
  44.6 1.6 %collective-permute-start.12 = (f32[1,128]{1,0:T(1,128)S(1)}, f32[1,128]{1,0:T(1,128)S(1)}, u32[]{:S(2)}, u32[]{:S(2)}) collective-permute-start(f32[1,128]{1,0:T(1,128)S(1)} %get-tuple-element.34), channel_id=1, source_target_pairs={{0,2},{2,0},{4,6},{6,4},{8,10},{10,8},{12,14},{14,12},{1,3},{3,1},... | collective-permute-start | bytes 1544 | tf_op jit(solution)/shard_map/ppermute | solution.py:389
  46.2 2.5 %rows.5.refs_2_ = f32[256,1536]{1,0:T(8,128)S(1)} custom-call(bf16[256,768]{1,0:T(8,128)(2,1)S(1)} %get-tuple-element.36.refs_0_, bf16[256,512]{1,0:T(8,128)(2,1)S(1)} %get-tuple-element.37.refs_1_, bf16[256,768]{1,0:T(8,128)(2,1)S(1)} %get-tuple-element.38.refs_2_, bf16[256,256]{1,0:T(8,128)(2,1)S(1)} %get-tuple-element.39.refs_3_, ...), custom_call_target="tpu_custom_call" | custom-call | flops 1811939328 | bytes 7077888 | tf_op jit(solution)/shard_map/rows/pallas_call | solution.py:227
  48.7 1.9 %collective-permute-start.13 = (f32[1,128]{1,0:T(1,128)S(1)}, f32[1,128]{1,0:T(1,128)S(1)}, u32[]{:S(2)}, u32[]{:S(2)}) collective-permute-start(f32[1,128]{1,0:T(1,128)S(1)} %add.57), channel_id=1, source_target_pairs={{0,4},{2,6},{4,0},{6,2},{8,12},{10,14},{12,8},{14,10},{1,5},{3,7},... | collective-permute-start | bytes 1544 | tf_op jit(solution)/shard_map/ppermute | solution.py:389
  50.7 2.5 %rows.3.refs_0_ = f32[256,1536]{1,0:T(8,128)S(1)} custom-call(bf16[256,768]{1,0:T(8,128)(2,1)S(1)} %get-tuple-element.36.refs_0_, bf16[256,512]{1,0:T(8,128)(2,1)S(1)} %get-tuple-element.37.refs_1_, bf16[256,768]{1,0:T(8,128)(2,1)S(1)} %get-tuple-element.38.refs_2_, bf16[256,256]{1,0:T(8,128)(2,1)S(1)} %get-tuple-element.39.refs_3_, ...), custom_call_target="tpu_custom_call" | custom-call | flops 1811939328 | bytes 7077888 | tf_op jit(solution)/shard_map/rows/pallas_call | solution.py:227
  53.2 2.0 %collective-permute-start.14 = (f32[1,128]{1,0:T(1,128)S(1)}, f32[1,128]{1,0:T(1,128)S(1)}, u32[]{:S(2)}, u32[]{:S(2)}) collective-permute-start(f32[1,128]{1,0:T(1,128)S(1)} %add.58), channel_id=1, source_target_pairs={{0,8},{2,10},{4,12},{6,14},{8,0},{10,2},{12,4},{14,6},{1,9},{3,11}... | collective-permute-start | bytes 1544 | tf_op jit(solution)/shard_map/ppermute | solution.py:389
  55.3 1.7 %rows.4.refs_1_ = f32[256,1024]{1,0:T(8,128)S(1)} custom-call(bf16[256,768]{1,0:T(8,128)(2,1)S(1)} %get-tuple-element.36.refs_0_, bf16[256,512]{1,0:T(8,128)(2,1)S(1)} %get-tuple-element.37.refs_1_, bf16[256,768]{1,0:T(8,128)(2,1)S(1)} %get-tuple-element.38.refs_2_, bf16[256,256]{1,0:T(8,128)(2,1)S(1)} %get-tuple-element.39.refs_3_, ...), custom_call_target="tpu_custom_call" | custom-call | flops 1207959552 | bytes 4718592 | tf_op jit(solution)/shard_map/rows/pallas_call | solution.py:227
  60.9 4.3 %collective-permute-done.15 = bf16[32,4096]{1,0:T(8,128)(2,1)S(1)} collective-permute-done((bf16[32,4096]{1,0:T(8,128)(2,1)S(1)}, bf16[32,4096]{1,0:T(8,128)(2,1)S(1)}, u32[]{:S(2)}, u32[]{:S(2)}) %collective-permute-start.15) | collective-permute-done | bytes 262176 | tf_op jit(solution)/shard_map/ppermute | solution.py:389
  65.3 2.0 %collective-permute-start.16 = (bf16[16,4096]{1,0:T(8,128)(2,1)S(1)}, bf16[16,4096]{1,0:T(8,128)(2,1)S(1)}, u32[]{:S(2)}, u32[]{:S(2)}) collective-permute-start(bf16[16,4096]{1,0:T(8,128)(2,1)S(1)} %get-tuple-element.55), channel_id=1, source_target_pairs={{0,8},{2,10},{4,12},{6,14},{8,0},{10,2},{12,4},{14,6},{1,9},{3,11}... | collective-permute-start | bytes 393224 | tf_op jit(solution)/shard_map/ppermute | solution.py:385
  68.4 3.1 %collective-permute-start.19 = (bf16[16,4096]{1,0:T(8,128)(2,1)S(1)}, bf16[16,4096]{1,0:T(8,128)(2,1)S(1)}, u32[]{:S(2)}, u32[]{:S(2)}) collective-permute-start(bf16[16,4096]{1,0:T(8,128)(2,1)S(1)} %add_convert_fusion.1), channel_id=1, source_target_pairs={{0,12},{2,14},{4,0},{6,2},{8,4},{10,6},{12,8},{14,10},{1,13},{3,15... | collective-permute-start | bytes 393224 | tf_op jit(solution)/shard_map/ppermute | solution.py:385
  78.5 1.7 %collective-permute-done.21.refs_1_ = bf16[128,2304]{1,0:T(8,128)(2,1)S(1)} collective-permute-done((bf16[128,2304]{1,0:T(8,128)(2,1)S(1)}, bf16[128,2304]{1,0:T(8,128)(2,1)S(1)}, u32[]{:S(2)}, u32[]{:S(2)}) %collective-permute-start.21) | collective-permute-done | bytes 589856 | tf_op jit(solution)/shard_map/ppermute | solution.py:389
  80.1 8.0 %weight.3 = (f32[2304,4096]{1,0:T(8,128)}, bf16[256,4096]{1,0:T(8,128)(2,1)S(1)}) custom-call(s32[3]{0:T(128)S(1)} %tick.1.ids_ref, bf16[128,2304]{1,0:T(8,128)(2,1)S(1)} %grads.1.refs_0_, bf16[128,2304]{1,0:T(8,128)(2,1)S(1)} %collective-permute-done.21.refs_1_, bf16[128,4096]{1,0:T(8,128)(2,1)S(1)} %get-tuple-element.50.refs_2_, ...), custom_call_target="tpu_custom_call" | custom-call | flops 2415919104 | bytes 18874368 | tf_op jit(solution)/shard_map/weight/pallas_call | solution.py:366
  88.1 6.9 %weight.4.refs_3_ = f32[2304,4096]{1,0:T(8,128)} custom-call(s32[3]{0:T(128)S(1)} %tick.1.ids_ref, bf16[128,2304]{1,0:T(8,128)(2,1)S(1)} %grads.1.refs_0_, bf16[128,2304]{1,0:T(8,128)(2,1)S(1)} %collective-permute-done.21.refs_1_, bf16[256,4096]{1,0:T(8,128)(2,1)S(1)} %get-tuple-element.51.refs_2_, ...), custom_call_target="tpu_custom_call", output_to_operand_aliasing={{}: (4, {})} | custom-call | flops 2147483648 | bytes 16777216 | tf_op jit(solution)/shard_map/weight/pallas_call | solution.py:366
  95.0 2.2 %weight.5 = f32[2304,4096]{1,0:T(8,128)} custom-call(s32[3]{0:T(128)S(1)} %tick.1.ids_ref, bf16[128,2304]{1,0:T(8,128)(2,1)S(1)} %grads.1.refs_0_, bf16[128,2304]{1,0:T(8,128)(2,1)S(1)} %collective-permute-done.21.refs_1_, bf16[256,4096]{1,0:T(8,128)(2,1)S(1)} %get-tuple-element.51.refs_2_, f32[2304,4096]{1,0:T(8,128)} %weight.4.refs_3_), custom_call_target="tpu_custom_call", output_to_operand_aliasing={{}: (4, {})} | custom-call | flops 268435456 | bytes 2097152 | tf_op jit(solution)/shard_map/weight/pallas_call | solution.py:366
  (74 shorter events, 31.1 us)
Async XLA Ops:
  1.6 9.6 %collective-permute-start.5 = (bf16[16,4096]{1,0:T(8,128)(2,1)S(1)}, bf16[16,4096]{1,0:T(8,128)(2,1)S(1)}, u32[]{:S(2)}, u32[]{:S(2)}) collective-permute-start(bf16[16,4096]{1,0:T(8,128)(2,1)S(1)} %fusion.refs_0_), channel_id=1, source_target_pairs={{0,4},{2,6},{4,8},{6,10},{8,12},{10,14},{12,0},{14,2},{1,5},{3,7},... | collective-permute-start | bytes 393224 | tf_op jit(solution)/shard_map/ppermute | solution.py:385
  4.7 11.2 %collective-permute-start.3 = (bf16[16,4096]{1,0:T(8,128)(2,1)S(1)}, bf16[16,4096]{1,0:T(8,128)(2,1)S(1)}, u32[]{:S(2)}, u32[]{:S(2)}) collective-permute-start(bf16[16,4096]{1,0:T(8,128)(2,1)S(1)} %fusion.refs_0_), channel_id=1, source_target_pairs={{0,8},{2,10},{4,12},{6,14},{8,0},{10,2},{12,4},{14,6},{1,9},{3,11}... | collective-permute-start | bytes 393224 | tf_op jit(solution)/shard_map/ppermute | solution.py:385
  7.3 10.2 %collective-permute-start.1 = (bf16[16,4096]{1,0:T(8,128)(2,1)S(1)}, bf16[16,4096]{1,0:T(8,128)(2,1)S(1)}, u32[]{:S(2)}, u32[]{:S(2)}) collective-permute-start(bf16[16,4096]{1,0:T(8,128)(2,1)S(1)} %fusion.refs_0_), channel_id=1, source_target_pairs={{0,12},{2,14},{4,0},{6,2},{8,4},{10,6},{12,8},{14,10},{1,13},{3,15... | collective-permute-start | bytes 393224 | tf_op jit(solution)/shard_map/ppermute | solution.py:385
  8.7 17.1 %collective-permute-start = (bf16[16,4096]{1,0:T(8,128)(2,1)S(1)}, bf16[16,4096]{1,0:T(8,128)(2,1)S(1)}, u32[]{:S(2)}, u32[]{:S(2)}) collective-permute-start(bf16[16,4096]{1,0:T(8,128)(2,1)S(1)} %fusion.refs_0_), channel_id=1, source_target_pairs={{0,2},{2,0},{4,6},{6,4},{8,10},{10,8},{12,14},{14,12},{1,3},{3,1},... | collective-permute-start | bytes 393224 | tf_op jit(solution)/shard_map/ppermute | solution.py:389
  10.2 12.1 %slice-start = ((s8[18874368]{0:T(1024)(128)(4,1)}), s8[4194304]{0:T(1024)(128)(4,1)S(1)}, s32[]{:S(2)}) async-start(s8[18874368]{0:T(1024)(128)(4,1)} %bitcast.8), calls=%async_computation | async-start | bytes 8388608
  11.2 14.5 %collective-permute-start.6 = (bf16[16,4096]{1,0:T(8,128)(2,1)S(1)}, bf16[16,4096]{1,0:T(8,128)(2,1)S(1)}, u32[]{:S(2)}, u32[]{:S(2)}) collective-permute-start(bf16[16,4096]{1,0:T(8,128)(2,1)S(1)} %collective-permute-done.5.refs_6_.refs_5_), channel_id=1, source_target_pairs={{0,2},{2,0},{4,6},{6,4},{8,10},{10,8},{12,14},{14,12},{1,3},{3,1},... | collective-permute-start | bytes 393224 | tf_op jit(solution)/shard_map/ppermute | solution.py:389
  16.0 6.4 %collective-permute-start.4 = (bf16[16,4096]{1,0:T(8,128)(2,1)S(1)}, bf16[16,4096]{1,0:T(8,128)(2,1)S(1)}, u32[]{:S(2)}, u32[]{:S(2)}) collective-permute-start(bf16[16,4096]{1,0:T(8,128)(2,1)S(1)} %collective-permute-done.3.refs_4_), channel_id=1, source_target_pairs={{0,2},{2,0},{4,6},{6,4},{8,10},{10,8},{12,14},{14,12},{1,3},{3,1},... | collective-permute-start | bytes 393224 | tf_op jit(solution)/shard_map/ppermute | solution.py:389
  17.5 8.2 %collective-permute-start.2 = (bf16[16,4096]{1,0:T(8,128)(2,1)S(1)}, bf16[16,4096]{1,0:T(8,128)(2,1)S(1)}, u32[]{:S(2)}, u32[]{:S(2)}) collective-permute-start(bf16[16,4096]{1,0:T(8,128)(2,1)S(1)} %collective-permute-done.1.refs_2_), channel_id=1, source_target_pairs={{0,2},{2,0},{4,6},{6,4},{8,10},{10,8},{12,14},{14,12},{1,3},{3,1},... | collective-permute-start | bytes 393224 | tf_op jit(solution)/shard_map/ppermute | solution.py:389
  24.2 12.5 %collective-permute-start.10 = (f16[16,768]{1,0:T(8,128)(2,1)S(1)}, f16[16,768]{1,0:T(8,128)(2,1)S(1)}, u32[]{:S(2)}, u32[]{:S(2)}) collective-permute-start(f16[16,768]{1,0:T(8,128)(2,1)S(1)} %convert_element_type.106), channel_id=1, source_target_pairs={{0,1},{1,0},{2,3},{3,2},{4,5},{5,4},{6,7},{7,6},{8,9},{9,8},{10,11... | collective-permute-start | bytes 73736 | tf_op jit(solution)/shard_map/ppermute | solution.py:389
  27.6 13.2 %collective-permute-start.9 = (f16[112,768]{1,0:T(8,128)(2,1)S(1)}, f16[112,768]{1,0:T(8,128)(2,1)S(1)}, u32[]{:S(2)}, u32[]{:S(2)}) collective-permute-start(f16[112,768]{1,0:T(8,128)(2,1)S(1)} %convert_element_type.103), channel_id=1, source_target_pairs={{0,1},{1,0},{2,3},{3,2},{4,5},{5,4},{6,7},{7,6},{8,9},{9,8},{10,11... | collective-permute-start | bytes 516104 | tf_op jit(solution)/shard_map/ppermute | solution.py:389
  32.9 5.0 %collective-permute-start.7 = (f16[128,256]{1,0:T(8,128)(2,1)S(1)}, f16[128,256]{1,0:T(8,128)(2,1)S(1)}, u32[]{:S(2)}, u32[]{:S(2)}) collective-permute-start(f16[128,256]{1,0:T(8,128)(2,1)S(1)} %convert_element_type.97), channel_id=1, source_target_pairs={{0,1},{1,0},{2,3},{3,2},{4,5},{5,4},{6,7},{7,6},{8,9},{9,8},{10,11... | collective-permute-start | bytes 196616 | tf_op jit(solution)/shard_map/ppermute | solution.py:389
  34.5 5.5 %collective-permute-start.8 = (f16[128,512]{1,0:T(8,128)(2,1)S(1)}, f16[128,512]{1,0:T(8,128)(2,1)S(1)}, u32[]{:S(2)}, u32[]{:S(2)}) collective-permute-start(f16[128,512]{1,0:T(8,128)(2,1)S(1)} %convert_element_type.100), channel_id=1, source_target_pairs={{0,1},{1,0},{2,3},{3,2},{4,5},{5,4},{6,7},{7,6},{8,9},{9,8},{10,11... | collective-permute-start | bytes 393224 | tf_op jit(solution)/shard_map/ppermute | solution.py:389
  35.1 7.0 %collective-permute-start.11 = (f16[128,768]{1,0:T(8,128)(2,1)S(1)}, f16[128,768]{1,0:T(8,128)(2,1)S(1)}, u32[]{:S(2)}, u32[]{:S(2)}) collective-permute-start(f16[128,768]{1,0:T(8,128)(2,1)S(1)} %convert_element_type.109), channel_id=1, source_target_pairs={{0,1},{1,0},{2,3},{3,2},{4,5},{5,4},{6,7},{7,6},{8,9},{9,8},{10,11... | collective-permute-start | bytes 589832 | tf_op jit(solution)/shard_map/ppermute | solution.py:389
  44.6 4.1 %collective-permute-start.12 = (f32[1,128]{1,0:T(1,128)S(1)}, f32[1,128]{1,0:T(1,128)S(1)}, u32[]{:S(2)}, u32[]{:S(2)}) collective-permute-start(f32[1,128]{1,0:T(1,128)S(1)} %get-tuple-element.34), channel_id=1, source_target_pairs={{0,2},{2,0},{4,6},{6,4},{8,10},{10,8},{12,14},{14,12},{1,3},{3,1},... | collective-permute-start | bytes 1544 | tf_op jit(solution)/shard_map/ppermute | solution.py:389
  48.7 4.5 %collective-permute-start.13 = (f32[1,128]{1,0:T(1,128)S(1)}, f32[1,128]{1,0:T(1,128)S(1)}, u32[]{:S(2)}, u32[]{:S(2)}) collective-permute-start(f32[1,128]{1,0:T(1,128)S(1)} %add.57), channel_id=1, source_target_pairs={{0,4},{2,6},{4,0},{6,2},{8,12},{10,14},{12,8},{14,10},{1,5},{3,7},... | collective-permute-start | bytes 1544 | tf_op jit(solution)/shard_map/ppermute | solution.py:389
  53.2 4.5 %collective-permute-start.14 = (f32[1,128]{1,0:T(1,128)S(1)}, f32[1,128]{1,0:T(1,128)S(1)}, u32[]{:S(2)}, u32[]{:S(2)}) collective-permute-start(f32[1,128]{1,0:T(1,128)S(1)} %add.58), channel_id=1, source_target_pairs={{0,8},{2,10},{4,12},{6,14},{8,0},{10,2},{12,4},{14,6},{1,9},{3,11}... | collective-permute-start | bytes 1544 | tf_op jit(solution)/shard_map/ppermute | solution.py:389
  58.8 6.4 %collective-permute-start.15 = (bf16[32,4096]{1,0:T(8,128)(2,1)S(1)}, bf16[32,4096]{1,0:T(8,128)(2,1)S(1)}, u32[]{:S(2)}, u32[]{:S(2)}) collective-permute-start(bf16[32,4096]{1,0:T(8,128)(2,1)S(1)} %get-tuple-element.41), channel_id=1, source_target_pairs={{0,2},{2,0},{4,6},{6,4},{8,10},{10,8},{12,14},{14,12},{1,3},{3,1},... | collective-permute-start | bytes 786440 | tf_op jit(solution)/shard_map/ppermute | solution.py:389
  59.9 8.5 %collective-permute-start.18 = (bf16[32,4096]{1,0:T(8,128)(2,1)S(1)}, bf16[32,4096]{1,0:T(8,128)(2,1)S(1)}, u32[]{:S(2)}, u32[]{:S(2)}) collective-permute-start(bf16[32,4096]{1,0:T(8,128)(2,1)S(1)} %get-tuple-element.44), channel_id=1, source_target_pairs={{0,2},{2,0},{4,6},{6,4},{8,10},{10,8},{12,14},{14,12},{1,3},{3,1},... | collective-permute-start | bytes 786440 | tf_op jit(solution)/shard_map/ppermute | solution.py:389
  65.3 7.4 %collective-permute-start.16 = (bf16[16,4096]{1,0:T(8,128)(2,1)S(1)}, bf16[16,4096]{1,0:T(8,128)(2,1)S(1)}, u32[]{:S(2)}, u32[]{:S(2)}) collective-permute-start(bf16[16,4096]{1,0:T(8,128)(2,1)S(1)} %get-tuple-element.55), channel_id=1, source_target_pairs={{0,8},{2,10},{4,12},{6,14},{8,0},{10,2},{12,4},{14,6},{1,9},{3,11}... | collective-permute-start | bytes 393224 | tf_op jit(solution)/shard_map/ppermute | solution.py:385
  67.4 6.9 %collective-permute-start.17 = (bf16[16,4096]{1,0:T(8,128)(2,1)S(1)}, bf16[16,4096]{1,0:T(8,128)(2,1)S(1)}, u32[]{:S(2)}, u32[]{:S(2)}) collective-permute-start(bf16[16,4096]{1,0:T(8,128)(2,1)S(1)} %get-tuple-element.56), channel_id=1, source_target_pairs={{0,4},{2,6},{4,8},{6,10},{8,12},{10,14},{12,0},{14,2},{1,5},{3,7},... | collective-permute-start | bytes 393224 | tf_op jit(solution)/shard_map/ppermute | solution.py:385
  68.4 7.1 %collective-permute-start.19 = (bf16[16,4096]{1,0:T(8,128)(2,1)S(1)}, bf16[16,4096]{1,0:T(8,128)(2,1)S(1)}, u32[]{:S(2)}, u32[]{:S(2)}) collective-permute-start(bf16[16,4096]{1,0:T(8,128)(2,1)S(1)} %add_convert_fusion.1), channel_id=1, source_target_pairs={{0,12},{2,14},{4,0},{6,2},{8,4},{10,6},{12,8},{14,10},{1,13},{3,15... | collective-permute-start | bytes 393224 | tf_op jit(solution)/shard_map/ppermute | solution.py:385
  76.2 1.5 %collective-permute-start.20 = (f32[16,4096]{1,0:T(8,128)S(1)}, f32[16,4096]{1,0:T(8,128)S(1)}, u32[]{:S(2)}, u32[]{:S(2)}) collective-permute-start(f32[16,4096]{1,0:T(8,128)S(1)} %get-tuple-element.54), channel_id=1, source_target_pairs={{0,16},{16,0},{1,17},{17,1},{2,18},{18,2},{3,19},{19,3},{4,20},{20... | collective-permute-start | bytes 786440 | tf_op jit(solution)/shard_map/ppermute | solution.py:389
  76.2 3.9 %collective-permute-start.22 = (bf16[128,4096]{1,0:T(8,128)(2,1)S(1)}, bf16[128,4096]{1,0:T(8,128)(2,1)S(1)}, u32[]{:S(2)}, u32[]{:S(2)}) collective-permute-start(bf16[128,4096]{1,0:T(8,128)(2,1)S(1)} %get-tuple-element.50.refs_2_), channel_id=1, source_target_pairs={{0,16},{16,0},{1,17},{17,1},{2,18},{18,2},{3,19},{19,3},{4,20},{20... | collective-permute-start | bytes 3145736 | tf_op jit(solution)/shard_map/ppermute | solution.py:389
  77.6 2.5 %collective-permute-start.21 = (bf16[128,2304]{1,0:T(8,128)(2,1)S(1)}, bf16[128,2304]{1,0:T(8,128)(2,1)S(1)}, u32[]{:S(2)}, u32[]{:S(2)}) collective-permute-start(bf16[128,2304]{1,0:T(8,128)(2,1)S(1)} %grads.1.refs_0_), channel_id=1, source_target_pairs={{0,16},{16,0},{1,17},{17,1},{2,18},{18,2},{3,19},{19,3},{4,20},{20... | collective-permute-start | bytes 1769480 | tf_op jit(solution)/shard_map/ppermute | solution.py:389
  (6 other events, 67.1 us)

commit v7 on v6

--- a/solution.py
+++ b/solution.py
@@ -313,18 +313,30 @@
     )(ids, targets, total, stats, loss_grad, *numers)
 
 
-def weight_kernel(first, start, block, ids_ref, *refs):
+def join_kernel(ids_ref, h0_ref, h1_ref, o_ref):
+    tokens = h0_ref.shape[0]
+    o_ref[pl.ds(pl.multiple_of(ids_ref[1] * tokens, tokens), tokens), :] = h0_ref[...]
+    o_ref[pl.ds(pl.multiple_of((1 - ids_ref[1]) * tokens, tokens), tokens), :] = h1_ref[...]
+
+
+def join_call(ids, h0, h1):
+    return pl.pallas_call(
+        join_kernel,
+        in_specs=[smem()] + [vmem()] * 2,
+        out_specs=vmem(),
+        out_shape=jax.ShapeDtypeStruct((2 * h0.shape[0], h0.shape[1]), h0.dtype),
+        compiler_params=params(0),
+        cost_estimate=cost(h0.size, 8 * h0.size),
+        name="join",
+    )(ids, h0, h1)
+
+
+def weight_kernel(start, block, ids_ref, *refs):
     g0_ref, g1_ref, refs = refs[0], refs[1], refs[2:]
-    if first:
-        h0_ref, h1_ref, o_ref, h_ref, g_ref, r_ref, sem = refs
-    else:
-        h_ref, _, o_ref, g_ref, r_ref, sem = refs
+    h_ref, (o_ref, g_ref, r_ref, sem) = refs[0], refs[-4:]
     tokens, count = g0_ref.shape[0], g_ref.shape[1]
     mine = pl.multiple_of(ids_ref[1] * tokens, tokens)
     other = pl.multiple_of((1 - ids_ref[1]) * tokens, tokens)
-    if first:
-        h_ref[pl.ds(mine, tokens), :] = h0_ref[...]
-        h_ref[pl.ds(other, tokens), :] = h1_ref[...]
     g_ref[pl.ds(mine, tokens), :] = g0_ref[:, start : start + count]
     g_ref[pl.ds(other, tokens), :] = g1_ref[:, start : start + count]
     turned = g_ref[...].T
@@ -357,17 +369,13 @@
     first = into is None
     operands = [ids, g0, g1, *hs] + ([] if first else [into])
     specs = [smem()] + [vmem()] * (2 + len(hs)) + ([] if first else [hbm])
-    out_specs = [hbm] + ([vmem()] if first else [])
-    out_shape = [jax.ShapeDtypeStruct((rows, width), f32)]
-    if first:
-        out_shape.append(jax.ShapeDtypeStruct((2 * tokens, width), bf16))
     across = 8
     steps = count // block * across
     return pl.pallas_call(
-        functools.partial(weight_kernel, first, start, block),
+        functools.partial(weight_kernel, start, block),
         in_specs=specs,
-        out_specs=out_specs,
-        out_shape=out_shape,
+        out_specs=hbm,
+        out_shape=jax.ShapeDtypeStruct((rows, width), f32),
         scratch_shapes=[
             pltpu.VMEM((2 * tokens, count), bf16),
             pltpu.VMEM((steps, block, width // across), f32),
@@ -399,7 +407,7 @@
 
 def portions(total, unit):
     tiles = total // unit
-    sizes = [tiles // 2, tiles - tiles // 2 - 1, 1]
+    sizes = [tiles - tiles // 3 - 4, 3, tiles // 3, 1]
     starts = [sum(sizes[:i]) for i in range(len(sizes))]
     return [(a * unit, c * unit) for a, c in zip(starts, sizes)]
 
@@ -487,13 +495,11 @@
 
     g = grads_call(ids, ps, spread, total, stats, loss_grad)
     g_other = swap(g, "head", 1, 2)
-    d_unembed, hs = None, [all_hidden, other_hidden]
-    for p, (start, count) in enumerate(portions(block_rows, 128)):
+    hs = [join_call(ids, all_hidden, other_hidden)]
+    d_unembed = None
+    for start, count in portions(block_rows, 128):
         block = 128 if count % 256 else 256
-        out = weight_call(ids, g, g_other, hs, start, count, block, d_unembed)
-        d_unembed = out[0]
-        if p == 0:
-            hs = out[1:]
+        d_unembed = weight_call(ids, g, g_other, hs, start, count, block, d_unembed)
 
     d_trunk = row_grad + swap(row_grad, "head", 1, 2)
     return (row_grad.astype(bf16)[None], d_trunk.astype(bf16), d_unembed)

time: 97.5 us -> 98.7 us (1.012)
  Pallas kernels: 38.4 us -> 40.3 us
    pallas_call x3 -> x5, Pallas kernels: 17.1 us -> 19 us  [the longest x4 18.3 us: weight_call(): pl.pallas_call(functools.partial(weight_kernel, start, block), in_specs=s...]
  transfers between devices with their start and end apart: 23 -> 23, of which waited for: 13 -> 14; matrix products, arithmetic and copies ran while one was open for 1% -> 1% of each run, Pallas kernels for 18% -> 19%
where the time goes in v7:
time: 98.7 us; the launch traced here: 98.6 us
  Pallas kernels  40.3 us (41%)
  starting transfers between devices  32.6 us (33%)
  waiting for transfers between devices  21.8 us (22%)
  other arithmetic  2.85 us (3%)
  between operations  1.07 us (1%)
    ppermute x17, starting transfers between devices, swap(): return lax.ppermute(x, axis, [(i, i ^ mask) for i in range(size)])  19.4 us
    pallas_call x4, Pallas kernels, weight_call(): pl.pallas_call(functools.partial(weight_kernel, start, block), in_specs=s...  18.3 us
    ppermute x17, waiting for transfers between devices, swap(): return lax.ppermute(x, axis, [(i, i ^ mask) for i in range(size)])  13.9 us
    ppermute x6, starting transfers between devices, slide(): lax.ppermute(x, 'seq', [(i, (i // 2 + by) % half * 2 + i % 2) for i in ra...  13.1 us
    ppermute x6, waiting for transfers between devices, slide(): lax.ppermute(x, 'seq', [(i, (i // 2 + by) % half * 2 + i % 2) for i in ra...  7.95 us
    pallas_call x3, Pallas kernels, rows_call(): pl.pallas_call(functools.partial(rows_kernel, block, first, places), grid...  6.68 us
    pallas_call x2, Pallas kernels, part_call(): pl.pallas_call(functools.partial(part_kernel, start), in_specs=[vmem()] *...  3.66 us
    pallas_call x4, Pallas kernels, numer_call(): pl.pallas_call(functools.partial(numer_kernel, start, first, last, n, gro...  3.19 us
  transfers between devices with their start and end apart: 23, of which 14 were waited for; matrix products, arithmetic and copies ran while one was open for 1% of the time, Pallas kernels for 19%

profile of v7, /device:TPU:0, one launch (start us, length us, event | category | flops | bytes accessed | tf_op | source)
XLA Modules:
  0.0 98.6 jit_solution(14331347868593229430)
XLA Ops:
  1.6 3.1 %collective-permute-start.5 = (bf16[16,4096]{1,0:T(8,128)(2,1)S(1)}, bf16[16,4096]{1,0:T(8,128)(2,1)S(1)}, u32[]{:S(2)}, u32[]{:S(2)}) collective-permute-start(bf16[16,4096]{1,0:T(8,128)(2,1)S(1)} %fusion.refs_0_), channel_id=1, source_target_pairs={{0,4},{2,6},{4,8},{6,10},{8,12},{10,14},{12,0},{14,2},{1,5},{3,7},... | collective-permute-start | bytes 393224 | tf_op jit(solution)/shard_map/ppermute | solution.py:393
  4.7 2.6 %collective-permute-start.3 = (bf16[16,4096]{1,0:T(8,128)(2,1)S(1)}, bf16[16,4096]{1,0:T(8,128)(2,1)S(1)}, u32[]{:S(2)}, u32[]{:S(2)}) collective-permute-start(bf16[16,4096]{1,0:T(8,128)(2,1)S(1)} %fusion.refs_0_), channel_id=1, source_target_pairs={{0,8},{2,10},{4,12},{6,14},{8,0},{10,2},{12,4},{14,6},{1,9},{3,11}... | collective-permute-start | bytes 393224 | tf_op jit(solution)/shard_map/ppermute | solution.py:393
  11.2 1.7 %collective-permute-start.6 = (bf16[16,4096]{1,0:T(8,128)(2,1)S(1)}, bf16[16,4096]{1,0:T(8,128)(2,1)S(1)}, u32[]{:S(2)}, u32[]{:S(2)}) collective-permute-start(bf16[16,4096]{1,0:T(8,128)(2,1)S(1)} %collective-permute-done.5.refs_6_.refs_5_), channel_id=1, source_target_pairs={{0,2},{2,0},{4,6},{6,4},{8,10},{10,8},{12,14},{14,12},{1,3},{3,1},... | collective-permute-start | bytes 393224 | tf_op jit(solution)/shard_map/ppermute | solution.py:397
  13.0 3.0 %collective-permute-done.3.refs_4_ = bf16[16,4096]{1,0:T(8,128)(2,1)S(1)} collective-permute-done((bf16[16,4096]{1,0:T(8,128)(2,1)S(1)}, bf16[16,4096]{1,0:T(8,128)(2,1)S(1)}, u32[]{:S(2)}, u32[]{:S(2)}) %collective-permute-start.3) | collective-permute-done | bytes 131104 | tf_op jit(solution)/shard_map/ppermute | solution.py:393
  19.1 3.2 %collective-permute-done.4.refs_5_.refs_0_ = bf16[16,4096]{1,0:T(8,128)(2,1)S(1)} collective-permute-done((bf16[16,4096]{1,0:T(8,128)(2,1)S(1)}, bf16[16,4096]{1,0:T(8,128)(2,1)S(1)}, u32[]{:S(2)}, u32[]{:S(2)}) %collective-permute-start.4) | collective-permute-done | bytes 131104 | tf_op jit(solution)/shard_map/ppermute | solution.py:397
  22.4 1.8 %scores_part.3 = f32[16,768]{1,0:T(8,128)S(1)} custom-call(bf16[16,4096]{1,0:T(8,128)(2,1)S(1)} %collective-permute-done.4.refs_5_.refs_0_, bf16[2304,4096]{1,0:T(8,128)(2,1)S(1)} %bitcast.9), custom_call_target="tpu_custom_call" | custom-call | flops 100663296 | bytes 6291456 | tf_op jit(solution)/shard_map/scores_part/pallas_call | solution.py:71
  24.2 1.6 %collective-permute-start.10 = (f16[16,768]{1,0:T(8,128)(2,1)S(1)}, f16[16,768]{1,0:T(8,128)(2,1)S(1)}, u32[]{:S(2)}, u32[]{:S(2)}) collective-permute-start(f16[16,768]{1,0:T(8,128)(2,1)S(1)} %convert_element_type.106), channel_id=1, source_target_pairs={{0,1},{1,0},{2,3},{3,2},{4,5},{5,4},{6,7},{7,6},{8,9},{9,8},{10,11... | collective-permute-start | bytes 73736 | tf_op jit(solution)/shard_map/ppermute | solution.py:397
  25.8 1.9 %scores_part.2 = f32[112,768]{1,0:T(8,128)S(1)} custom-call(bf16[16,4096]{1,0:T(8,128)(2,1)S(1)} %fusion.refs_0_, bf16[16,4096]{1,0:T(8,128)(2,1)S(1)} %collective-permute-done.refs_1_, bf16[16,4096]{1,0:T(8,128)(2,1)S(1)} %collective-permute-done.1.refs_2_, bf16[16,4096]{1,0:T(8,128)(2,1)S(1)} %collective-permute-done.2.refs_3_, ...), custom_call_target="tpu_custom_call" | custom-call | flops 704643072 | bytes 6291456 | tf_op jit(solution)/shard_map/scores_part/pallas_call | solution.py:71
  28.3 2.0 %scores_first.1 = (f32[128,512]{1,0:T(8,128)S(1)}, bf16[128,4096]{1,0:T(8,128)(2,1)S(1)}, bf16[4096,128]{1,0:T(8,128)(2,1)S(1)}) custom-call(s32[3]{0:T(128)S(1)} %tick.1.ids_ref, bf16[16,4096]{1,0:T(8,128)(2,1)S(1)} %fusion.refs_0_, bf16[16,4096]{1,0:T(8,128)(2,1)S(1)} %collective-permute-done.refs_1_, bf16[16,4096]{1,0:T(8,128)(2,1)S(1)} %collective-permute-done.1.refs_2_, ...), custom_call_target="tpu_custom_call" | custom-call | flops 536870912 | bytes 4194304 | tf_op jit(solution)/shard_map/scores_first/pallas_call | solution.py:102
  30.3 1.9 %scores_next.3 = f32[128,768]{1,0:T(8,128)S(1)} custom-call(bf16[4096,128]{1,0:T(8,128)(2,1)S(1)} %get-tuple-element.26.ht_ref, bf16[2304,4096]{1,0:T(8,128)(2,1)S(1)} %bitcast.9), custom_call_target="tpu_custom_call" | custom-call | flops 805306368 | bytes 6291456 | tf_op jit(solution)/shard_map/scores_next/pallas_call | solution.py:119
  38.0 2.0 %collective-permute-done.8 = f16[128,512]{1,0:T(8,128)(2,1)S(1)} collective-permute-done((f16[128,512]{1,0:T(8,128)(2,1)S(1)}, f16[128,512]{1,0:T(8,128)(2,1)S(1)}, u32[]{:S(2)}, u32[]{:S(2)}) %collective-permute-start.8) | collective-permute-done | bytes 131104 | tf_op jit(solution)/shard_map/ppermute | solution.py:397
  44.6 1.6 %collective-permute-start.12 = (f32[1,128]{1,0:T(1,128)S(1)}, f32[1,128]{1,0:T(1,128)S(1)}, u32[]{:S(2)}, u32[]{:S(2)}) collective-permute-start(f32[1,128]{1,0:T(1,128)S(1)} %get-tuple-element.32), channel_id=1, source_target_pairs={{0,2},{2,0},{4,6},{6,4},{8,10},{10,8},{12,14},{14,12},{1,3},{3,1},... | collective-permute-start | bytes 1544 | tf_op jit(solution)/shard_map/ppermute | solution.py:397
  46.2 2.5 %rows.5.refs_2_ = f32[256,1536]{1,0:T(8,128)S(1)} custom-call(bf16[256,768]{1,0:T(8,128)(2,1)S(1)} %get-tuple-element.34.refs_0_, bf16[256,512]{1,0:T(8,128)(2,1)S(1)} %get-tuple-element.35.refs_1_, bf16[256,768]{1,0:T(8,128)(2,1)S(1)} %get-tuple-element.36.refs_2_, bf16[256,256]{1,0:T(8,128)(2,1)S(1)} %get-tuple-element.37.refs_3_, ...), custom_call_target="tpu_custom_call" | custom-call | flops 1811939328 | bytes 7077888 | tf_op jit(solution)/shard_map/rows/pallas_call | solution.py:227
  48.7 2.0 %collective-permute-start.13 = (f32[1,128]{1,0:T(1,128)S(1)}, f32[1,128]{1,0:T(1,128)S(1)}, u32[]{:S(2)}, u32[]{:S(2)}) collective-permute-start(f32[1,128]{1,0:T(1,128)S(1)} %add.57), channel_id=1, source_target_pairs={{0,4},{2,6},{4,0},{6,2},{8,12},{10,14},{12,8},{14,10},{1,5},{3,7},... | collective-permute-start | bytes 1544 | tf_op jit(solution)/shard_map/ppermute | solution.py:397
  50.7 2.5 %rows.3.refs_0_ = f32[256,1536]{1,0:T(8,128)S(1)} custom-call(bf16[256,768]{1,0:T(8,128)(2,1)S(1)} %get-tuple-element.34.refs_0_, bf16[256,512]{1,0:T(8,128)(2,1)S(1)} %get-tuple-element.35.refs_1_, bf16[256,768]{1,0:T(8,128)(2,1)S(1)} %get-tuple-element.36.refs_2_, bf16[256,256]{1,0:T(8,128)(2,1)S(1)} %get-tuple-element.37.refs_3_, ...), custom_call_target="tpu_custom_call" | custom-call | flops 1811939328 | bytes 7077888 | tf_op jit(solution)/shard_map/rows/pallas_call | solution.py:227
  53.2 2.0 %collective-permute-start.14 = (f32[1,128]{1,0:T(1,128)S(1)}, f32[1,128]{1,0:T(1,128)S(1)}, u32[]{:S(2)}, u32[]{:S(2)}) collective-permute-start(f32[1,128]{1,0:T(1,128)S(1)} %add.58), channel_id=1, source_target_pairs={{0,8},{2,10},{4,12},{6,14},{8,0},{10,2},{12,4},{14,6},{1,9},{3,11}... | collective-permute-start | bytes 1544 | tf_op jit(solution)/shard_map/ppermute | solution.py:397
  55.3 1.7 %rows.4.refs_1_ = f32[256,1024]{1,0:T(8,128)S(1)} custom-call(bf16[256,768]{1,0:T(8,128)(2,1)S(1)} %get-tuple-element.34.refs_0_, bf16[256,512]{1,0:T(8,128)(2,1)S(1)} %get-tuple-element.35.refs_1_, bf16[256,768]{1,0:T(8,128)(2,1)S(1)} %get-tuple-element.36.refs_2_, bf16[256,256]{1,0:T(8,128)(2,1)S(1)} %get-tuple-element.37.refs_3_, ...), custom_call_target="tpu_custom_call" | custom-call | flops 1207959552 | bytes 4718592 | tf_op jit(solution)/shard_map/rows/pallas_call | solution.py:227
  60.9 4.3 %collective-permute-done.15 = bf16[32,4096]{1,0:T(8,128)(2,1)S(1)} collective-permute-done((bf16[32,4096]{1,0:T(8,128)(2,1)S(1)}, bf16[32,4096]{1,0:T(8,128)(2,1)S(1)}, u32[]{:S(2)}, u32[]{:S(2)}) %collective-permute-start.15) | collective-permute-done | bytes 262176 | tf_op jit(solution)/shard_map/ppermute | solution.py:397
  65.4 2.0 %collective-permute-start.16 = (bf16[16,4096]{1,0:T(8,128)(2,1)S(1)}, bf16[16,4096]{1,0:T(8,128)(2,1)S(1)}, u32[]{:S(2)}, u32[]{:S(2)}) collective-permute-start(bf16[16,4096]{1,0:T(8,128)(2,1)S(1)} %get-tuple-element.51), channel_id=1, source_target_pairs={{0,8},{2,10},{4,12},{6,14},{8,0},{10,2},{12,4},{14,6},{1,9},{3,11}... | collective-permute-start | bytes 393224 | tf_op jit(solution)/shard_map/ppermute | solution.py:393
  68.4 3.1 %collective-permute-start.19 = (bf16[16,4096]{1,0:T(8,128)(2,1)S(1)}, bf16[16,4096]{1,0:T(8,128)(2,1)S(1)}, u32[]{:S(2)}, u32[]{:S(2)}) collective-permute-start(bf16[16,4096]{1,0:T(8,128)(2,1)S(1)} %add_convert_fusion.1), channel_id=1, source_target_pairs={{0,12},{2,14},{4,0},{6,2},{8,4},{10,6},{12,8},{14,10},{1,13},{3,15... | collective-permute-start | bytes 393224 | tf_op jit(solution)/shard_map/ppermute | solution.py:393
  80.1 6.9 %weight.4.refs_3_ = f32[2304,4096]{1,0:T(8,128)} custom-call(s32[3]{0:T(128)S(1)} %tick.1.ids_ref, bf16[128,2304]{1,0:T(8,128)(2,1)S(1)} %grads.1.refs_0_, bf16[128,2304]{1,0:T(8,128)(2,1)S(1)} %collective-permute-done.21.refs_1_, bf16[256,4096]{1,0:T(8,128)(2,1)S(1)} %join.1.refs_2_), custom_call_target="tpu_custom_call" | custom-call | flops 2147483648 | bytes 16777216 | tf_op jit(solution)/shard_map/weight/pallas_call | solution.py:374
  87.0 3.6 %weight.5.refs_3_ = f32[2304,4096]{1,0:T(8,128)} custom-call(s32[3]{0:T(128)S(1)} %tick.1.ids_ref, bf16[128,2304]{1,0:T(8,128)(2,1)S(1)} %grads.1.refs_0_, bf16[128,2304]{1,0:T(8,128)(2,1)S(1)} %collective-permute-done.21.refs_1_, bf16[256,4096]{1,0:T(8,128)(2,1)S(1)} %join.1.refs_2_, f32[2304,4096]{1,0:T(8,128)} %weight.4.refs_3_), custom_call_target="tpu_custom_call", output_to_operand_aliasing={{}: (4, {})} | custom-call | flops 805306368 | bytes 6291456 | tf_op jit(solution)/shard_map/weight/pallas_call | solution.py:374
  90.7 5.6 %weight.6.refs_3_ = f32[2304,4096]{1,0:T(8,128)} custom-call(s32[3]{0:T(128)S(1)} %tick.1.ids_ref, bf16[128,2304]{1,0:T(8,128)(2,1)S(1)} %grads.1.refs_0_, bf16[128,2304]{1,0:T(8,128)(2,1)S(1)} %collective-permute-done.21.refs_1_, bf16[256,4096]{1,0:T(8,128)(2,1)S(1)} %join.1.refs_2_, f32[2304,4096]{1,0:T(8,128)} %weight.5.refs_3_), custom_call_target="tpu_custom_call", output_to_operand_aliasing={{}: (4, {})} | custom-call | flops 1610612736 | bytes 12582912 | tf_op jit(solution)/shard_map/weight/pallas_call | solution.py:374
  96.3 2.2 %weight.7 = f32[2304,4096]{1,0:T(8,128)} custom-call(s32[3]{0:T(128)S(1)} %tick.1.ids_ref, bf16[128,2304]{1,0:T(8,128)(2,1)S(1)} %grads.1.refs_0_, bf16[128,2304]{1,0:T(8,128)(2,1)S(1)} %collective-permute-done.21.refs_1_, bf16[256,4096]{1,0:T(8,128)(2,1)S(1)} %join.1.refs_2_, f32[2304,4096]{1,0:T(8,128)} %weight.6.refs_3_), custom_call_target="tpu_custom_call", output_to_operand_aliasing={{}: (4, {})} | custom-call | flops 268435456 | bytes 2097152 | tf_op jit(solution)/shard_map/weight/pallas_call | solution.py:374
  (76 shorter events, 32.7 us)
Async XLA Ops:
  1.6 9.6 %collective-permute-start.5 = (bf16[16,4096]{1,0:T(8,128)(2,1)S(1)}, bf16[16,4096]{1,0:T(8,128)(2,1)S(1)}, u32[]{:S(2)}, u32[]{:S(2)}) collective-permute-start(bf16[16,4096]{1,0:T(8,128)(2,1)S(1)} %fusion.refs_0_), channel_id=1, source_target_pairs={{0,4},{2,6},{4,8},{6,10},{8,12},{10,14},{12,0},{14,2},{1,5},{3,7},... | collective-permute-start | bytes 393224 | tf_op jit(solution)/shard_map/ppermute | solution.py:393
  4.7 11.2 %collective-permute-start.3 = (bf16[16,4096]{1,0:T(8,128)(2,1)S(1)}, bf16[16,4096]{1,0:T(8,128)(2,1)S(1)}, u32[]{:S(2)}, u32[]{:S(2)}) collective-permute-start(bf16[16,4096]{1,0:T(8,128)(2,1)S(1)} %fusion.refs_0_), channel_id=1, source_target_pairs={{0,8},{2,10},{4,12},{6,14},{8,0},{10,2},{12,4},{14,6},{1,9},{3,11}... | collective-permute-start | bytes 393224 | tf_op jit(solution)/shard_map/ppermute | solution.py:393
  7.3 10.2 %collective-permute-start.1 = (bf16[16,4096]{1,0:T(8,128)(2,1)S(1)}, bf16[16,4096]{1,0:T(8,128)(2,1)S(1)}, u32[]{:S(2)}, u32[]{:S(2)}) collective-permute-start(bf16[16,4096]{1,0:T(8,128)(2,1)S(1)} %fusion.refs_0_), channel_id=1, source_target_pairs={{0,12},{2,14},{4,0},{6,2},{8,4},{10,6},{12,8},{14,10},{1,13},{3,15... | collective-permute-start | bytes 393224 | tf_op jit(solution)/shard_map/ppermute | solution.py:393
  8.7 17.1 %collective-permute-start = (bf16[16,4096]{1,0:T(8,128)(2,1)S(1)}, bf16[16,4096]{1,0:T(8,128)(2,1)S(1)}, u32[]{:S(2)}, u32[]{:S(2)}) collective-permute-start(bf16[16,4096]{1,0:T(8,128)(2,1)S(1)} %fusion.refs_0_), channel_id=1, source_target_pairs={{0,2},{2,0},{4,6},{6,4},{8,10},{10,8},{12,14},{14,12},{1,3},{3,1},... | collective-permute-start | bytes 393224 | tf_op jit(solution)/shard_map/ppermute | solution.py:397
  11.2 14.5 %collective-permute-start.6 = (bf16[16,4096]{1,0:T(8,128)(2,1)S(1)}, bf16[16,4096]{1,0:T(8,128)(2,1)S(1)}, u32[]{:S(2)}, u32[]{:S(2)}) collective-permute-start(bf16[16,4096]{1,0:T(8,128)(2,1)S(1)} %collective-permute-done.5.refs_6_.refs_5_), channel_id=1, source_target_pairs={{0,2},{2,0},{4,6},{6,4},{8,10},{10,8},{12,14},{14,12},{1,3},{3,1},... | collective-permute-start | bytes 393224 | tf_op jit(solution)/shard_map/ppermute | solution.py:397
  16.0 6.4 %collective-permute-start.4 = (bf16[16,4096]{1,0:T(8,128)(2,1)S(1)}, bf16[16,4096]{1,0:T(8,128)(2,1)S(1)}, u32[]{:S(2)}, u32[]{:S(2)}) collective-permute-start(bf16[16,4096]{1,0:T(8,128)(2,1)S(1)} %collective-permute-done.3.refs_4_), channel_id=1, source_target_pairs={{0,2},{2,0},{4,6},{6,4},{8,10},{10,8},{12,14},{14,12},{1,3},{3,1},... | collective-permute-start | bytes 393224 | tf_op jit(solution)/shard_map/ppermute | solution.py:397
  17.5 8.3 %collective-permute-start.2 = (bf16[16,4096]{1,0:T(8,128)(2,1)S(1)}, bf16[16,4096]{1,0:T(8,128)(2,1)S(1)}, u32[]{:S(2)}, u32[]{:S(2)}) collective-permute-start(bf16[16,4096]{1,0:T(8,128)(2,1)S(1)} %collective-permute-done.1.refs_2_), channel_id=1, source_target_pairs={{0,2},{2,0},{4,6},{6,4},{8,10},{10,8},{12,14},{14,12},{1,3},{3,1},... | collective-permute-start | bytes 393224 | tf_op jit(solution)/shard_map/ppermute | solution.py:397
  24.2 12.5 %collective-permute-start.10 = (f16[16,768]{1,0:T(8,128)(2,1)S(1)}, f16[16,768]{1,0:T(8,128)(2,1)S(1)}, u32[]{:S(2)}, u32[]{:S(2)}) collective-permute-start(f16[16,768]{1,0:T(8,128)(2,1)S(1)} %convert_element_type.106), channel_id=1, source_target_pairs={{0,1},{1,0},{2,3},{3,2},{4,5},{5,4},{6,7},{7,6},{8,9},{9,8},{10,11... | collective-permute-start | bytes 73736 | tf_op jit(solution)/shard_map/ppermute | solution.py:397
  27.7 13.2 %collective-permute-start.9 = (f16[112,768]{1,0:T(8,128)(2,1)S(1)}, f16[112,768]{1,0:T(8,128)(2,1)S(1)}, u32[]{:S(2)}, u32[]{:S(2)}) collective-permute-start(f16[112,768]{1,0:T(8,128)(2,1)S(1)} %convert_element_type.103), channel_id=1, source_target_pairs={{0,1},{1,0},{2,3},{3,2},{4,5},{5,4},{6,7},{7,6},{8,9},{9,8},{10,11... | collective-permute-start | bytes 516104 | tf_op jit(solution)/shard_map/ppermute | solution.py:397
  32.9 24.8 %copy-start = (f32[1,128]{1,0:T(1,128)S(1)}, f32[1,128]{1,0:T(1,128)}, u32[]{:S(2)}) copy-start(f32[1,128]{1,0:T(1,128)} %lg_ref.3) | copy-start | bytes 1540
  33.0 5.0 %collective-permute-start.7 = (f16[128,256]{1,0:T(8,128)(2,1)S(1)}, f16[128,256]{1,0:T(8,128)(2,1)S(1)}, u32[]{:S(2)}, u32[]{:S(2)}) collective-permute-start(f16[128,256]{1,0:T(8,128)(2,1)S(1)} %convert_element_type.97), channel_id=1, source_target_pairs={{0,1},{1,0},{2,3},{3,2},{4,5},{5,4},{6,7},{7,6},{8,9},{9,8},{10,11... | collective-permute-start | bytes 196616 | tf_op jit(solution)/shard_map/ppermute | solution.py:397
  34.5 5.5 %collective-permute-start.8 = (f16[128,512]{1,0:T(8,128)(2,1)S(1)}, f16[128,512]{1,0:T(8,128)(2,1)S(1)}, u32[]{:S(2)}, u32[]{:S(2)}) collective-permute-start(f16[128,512]{1,0:T(8,128)(2,1)S(1)} %convert_element_type.100), channel_id=1, source_target_pairs={{0,1},{1,0},{2,3},{3,2},{4,5},{5,4},{6,7},{7,6},{8,9},{9,8},{10,11... | collective-permute-start | bytes 393224 | tf_op jit(solution)/shard_map/ppermute | solution.py:397
  35.2 7.0 %collective-permute-start.11 = (f16[128,768]{1,0:T(8,128)(2,1)S(1)}, f16[128,768]{1,0:T(8,128)(2,1)S(1)}, u32[]{:S(2)}, u32[]{:S(2)}) collective-permute-start(f16[128,768]{1,0:T(8,128)(2,1)S(1)} %convert_element_type.109), channel_id=1, source_target_pairs={{0,1},{1,0},{2,3},{3,2},{4,5},{5,4},{6,7},{7,6},{8,9},{9,8},{10,11... | collective-permute-start | bytes 589832 | tf_op jit(solution)/shard_map/ppermute | solution.py:397
  44.6 4.1 %collective-permute-start.12 = (f32[1,128]{1,0:T(1,128)S(1)}, f32[1,128]{1,0:T(1,128)S(1)}, u32[]{:S(2)}, u32[]{:S(2)}) collective-permute-start(f32[1,128]{1,0:T(1,128)S(1)} %get-tuple-element.32), channel_id=1, source_target_pairs={{0,2},{2,0},{4,6},{6,4},{8,10},{10,8},{12,14},{14,12},{1,3},{3,1},... | collective-permute-start | bytes 1544 | tf_op jit(solution)/shard_map/ppermute | solution.py:397
  48.7 4.5 %collective-permute-start.13 = (f32[1,128]{1,0:T(1,128)S(1)}, f32[1,128]{1,0:T(1,128)S(1)}, u32[]{:S(2)}, u32[]{:S(2)}) collective-permute-start(f32[1,128]{1,0:T(1,128)S(1)} %add.57), channel_id=1, source_target_pairs={{0,4},{2,6},{4,0},{6,2},{8,12},{10,14},{12,8},{14,10},{1,5},{3,7},... | collective-permute-start | bytes 1544 | tf_op jit(solution)/shard_map/ppermute | solution.py:397
  53.2 4.5 %collective-permute-start.14 = (f32[1,128]{1,0:T(1,128)S(1)}, f32[1,128]{1,0:T(1,128)S(1)}, u32[]{:S(2)}, u32[]{:S(2)}) collective-permute-start(f32[1,128]{1,0:T(1,128)S(1)} %add.58), channel_id=1, source_target_pairs={{0,8},{2,10},{4,12},{6,14},{8,0},{10,2},{12,4},{14,6},{1,9},{3,11}... | collective-permute-start | bytes 1544 | tf_op jit(solution)/shard_map/ppermute | solution.py:397
  58.9 6.4 %collective-permute-start.15 = (bf16[32,4096]{1,0:T(8,128)(2,1)S(1)}, bf16[32,4096]{1,0:T(8,128)(2,1)S(1)}, u32[]{:S(2)}, u32[]{:S(2)}) collective-permute-start(bf16[32,4096]{1,0:T(8,128)(2,1)S(1)} %get-tuple-element.39), channel_id=1, source_target_pairs={{0,2},{2,0},{4,6},{6,4},{8,10},{10,8},{12,14},{14,12},{1,3},{3,1},... | collective-permute-start | bytes 786440 | tf_op jit(solution)/shard_map/ppermute | solution.py:397
  59.9 8.5 %collective-permute-start.18 = (bf16[32,4096]{1,0:T(8,128)(2,1)S(1)}, bf16[32,4096]{1,0:T(8,128)(2,1)S(1)}, u32[]{:S(2)}, u32[]{:S(2)}) collective-permute-start(bf16[32,4096]{1,0:T(8,128)(2,1)S(1)} %get-tuple-element.42), channel_id=1, source_target_pairs={{0,2},{2,0},{4,6},{6,4},{8,10},{10,8},{12,14},{14,12},{1,3},{3,1},... | collective-permute-start | bytes 786440 | tf_op jit(solution)/shard_map/ppermute | solution.py:397
  65.4 7.4 %collective-permute-start.16 = (bf16[16,4096]{1,0:T(8,128)(2,1)S(1)}, bf16[16,4096]{1,0:T(8,128)(2,1)S(1)}, u32[]{:S(2)}, u32[]{:S(2)}) collective-permute-start(bf16[16,4096]{1,0:T(8,128)(2,1)S(1)} %get-tuple-element.51), channel_id=1, source_target_pairs={{0,8},{2,10},{4,12},{6,14},{8,0},{10,2},{12,4},{14,6},{1,9},{3,11}... | collective-permute-start | bytes 393224 | tf_op jit(solution)/shard_map/ppermute | solution.py:393
  67.4 6.9 %collective-permute-start.17 = (bf16[16,4096]{1,0:T(8,128)(2,1)S(1)}, bf16[16,4096]{1,0:T(8,128)(2,1)S(1)}, u32[]{:S(2)}, u32[]{:S(2)}) collective-permute-start(bf16[16,4096]{1,0:T(8,128)(2,1)S(1)} %get-tuple-element.52), channel_id=1, source_target_pairs={{0,4},{2,6},{4,8},{6,10},{8,12},{10,14},{12,0},{14,2},{1,5},{3,7},... | collective-permute-start | bytes 393224 | tf_op jit(solution)/shard_map/ppermute | solution.py:393
  68.4 7.1 %collective-permute-start.19 = (bf16[16,4096]{1,0:T(8,128)(2,1)S(1)}, bf16[16,4096]{1,0:T(8,128)(2,1)S(1)}, u32[]{:S(2)}, u32[]{:S(2)}) collective-permute-start(bf16[16,4096]{1,0:T(8,128)(2,1)S(1)} %add_convert_fusion.1), channel_id=1, source_target_pairs={{0,12},{2,14},{4,0},{6,2},{8,4},{10,6},{12,8},{14,10},{1,13},{3,15... | collective-permute-start | bytes 393224 | tf_op jit(solution)/shard_map/ppermute | solution.py:393
  76.2 1.5 %collective-permute-start.20 = (f32[16,4096]{1,0:T(8,128)S(1)}, f32[16,4096]{1,0:T(8,128)S(1)}, u32[]{:S(2)}, u32[]{:S(2)}) collective-permute-start(f32[16,4096]{1,0:T(8,128)S(1)} %get-tuple-element.50), channel_id=1, source_target_pairs={{0,16},{16,0},{1,17},{17,1},{2,18},{18,2},{3,19},{19,3},{4,20},{20... | collective-permute-start | bytes 786440 | tf_op jit(solution)/shard_map/ppermute | solution.py:397
  76.2 3.0 %collective-permute-start.22 = (bf16[128,4096]{1,0:T(8,128)(2,1)S(1)}, bf16[128,4096]{1,0:T(8,128)(2,1)S(1)}, u32[]{:S(2)}, u32[]{:S(2)}) collective-permute-start(bf16[128,4096]{1,0:T(8,128)(2,1)S(1)} %get-tuple-element.48.h0_ref), channel_id=1, source_target_pairs={{0,16},{16,0},{1,17},{17,1},{2,18},{18,2},{3,19},{19,3},{4,20},{20... | collective-permute-start | bytes 3145736 | tf_op jit(solution)/shard_map/ppermute | solution.py:397
  77.6 2.5 %collective-permute-start.21 = (bf16[128,2304]{1,0:T(8,128)(2,1)S(1)}, bf16[128,2304]{1,0:T(8,128)(2,1)S(1)}, u32[]{:S(2)}, u32[]{:S(2)}) collective-permute-start(bf16[128,2304]{1,0:T(8,128)(2,1)S(1)} %grads.1.refs_0_), channel_id=1, source_target_pairs={{0,16},{16,0},{1,17},{17,1},{2,18},{18,2},{3,19},{19,3},{4,20},{20... | collective-permute-start | bytes 1769480 | tf_op jit(solution)/shard_map/ppermute | solution.py:397
  (6 other events, 76.3 us)
